TPU v7x, 512 devices: a whole 4x8x8 slice. The times are simulated.
512 devices in a mesh: panel: 32 (over y_lo, z, core), rhs: 16 (over x, y_hi).
Axes of the slice: x: 4, y: 8 (y_hi: 4, y_lo: 2; y = y_hi * 2 + y_lo), z: 8, core: 2. Of those that a mesh axis runs over, the one named last changes fastest.
Arguments:
- pivot_rhs: float32 [2, 2048, 2048], P(None, 'panel', 'rhs'), may hold values from -6 to 6
- update_rhs: float32 [4096, 2048], P('panel', 'rhs'), may hold values from -6 to 6
- parent_rhs: float32 [4096, 2048], P('panel', 'rhs'), may hold values from -6 to 6
- lower_pivot: bfloat16 [2, 2048, 2048], P(None, 'panel', 'rhs'), may hold values from -1 to 1.4, as said below
- lower_update: bfloat16 [4096, 2048], P('panel', 'rhs'), may hold values from -0.125 to 0.125
- parent_lower: bfloat16 [4096, 4096], P('panel', 'rhs'), may hold values from -1 to 1.4, as said below
- parent_upper: bfloat16 [4096, 4096], P('panel', 'rhs'), may hold values from -1 to 1.4, as said below
- upper_pivot: bfloat16 [2, 2048, 2048], P(None, 'panel', 'rhs'), may hold values from -1 to 1.4, as said below
- upper_update: bfloat16 [2, 2048, 2048], P(None, 'panel', 'rhs'), may hold values from -0.125 to 0.125
- maps: int32 [4096], replicated, may hold values from 0 to 4095, as said below
Outputs:
- parent_solution: float32 [4096, 2048], P('panel', 'rhs')
- child_solution: float32 [2, 2048, 2048], P(None, 'panel', 'rhs')
Inputs may be any that keep to these rules, and one draw needn't show every extreme that they name: `maps`: for each child k, entry k * 2048 + i is 2 * i + b with b equal to 0 or 1; both values of b occur for each child in every draw. `lower_pivot`: each block is lower triangular, diagonal 0.6 to 1.4. `upper_pivot`: each block is upper triangular, diagonal 0.6 to 1.4. `parent_lower`: lower triangular, diagonal 0.6 to 1.4. `parent_upper`: upper triangular, diagonal 0.6 to 1.4.
All inputs are finite; a program needn't handle non-finite values.
Results may differ from a plain program's by a relative error of at most 0.0054.
Values may be sent and summed in bfloat16 or wider, within the bound.
No kernel may reach another device: no remote copies, remote signals or barrier semaphores. Data moves between devices by JAX's collectives and lax.ppermute only.
A program may use at most 64 MiB of HBM per device.

v0:
```python
import jax
import jax.numpy as jnp
from jax import lax
from jax.sharding import PartitionSpec as P

FU = 2048


def copy_for_each(shard, axis):
    peers = lax.axis_size(axis)
    return lax.all_to_all(
        jnp.broadcast_to(shard[None], (peers, *shard.shape)), axis, 0, 0, tiled=True
    )


def laid_out(blocks, dim):
    blocks = jnp.moveaxis(blocks, 0, dim)
    lengths = blocks.shape
    return blocks.reshape(*lengths[:dim], lengths[dim] * lengths[dim + 1], *lengths[dim + 2 :])


def collect(shard, axis, dim):
    blocks = copy_for_each(shard, axis)
    return laid_out(blocks, dim)


def sent_together(arrays, axis, dim, along):
    ends, at = ([], 0)
    for a in arrays[:-1]:
        at += a.shape[along]
        ends.append(at)
    both = jnp.concatenate(arrays, axis=along)
    return tuple(jnp.split(lax.all_gather(both, axis, axis=dim, tiled=True), ends, axis=along))


def product(left, right):
    return jnp.dot(left, right, preferred_element_type=jnp.float32)


def paired(left, right):
    return jnp.einsum("kqw,kwr->kqr", left, right, preferred_element_type=jnp.float32)


def through(factor, vector):
    return product(collect(factor, "rhs", 1), vector)


def shards(
    pivot_rhs,
    update_rhs,
    parent_rhs,
    lower_pivot,
    lower_update,
    parent_lower,
    parent_upper,
    upper_pivot,
    upper_update,
    maps,
):
    panel_index = lax.axis_index("panel")
    row_count = update_rhs.shape[0]
    rhs_width = update_rhs.shape[1]
    pivot_local = pivot_rhs.shape[1]
    first_row = panel_index * row_count
    child_index = first_row // FU
    pivot_all = collect(pivot_rhs.astype(jnp.bfloat16), "panel", 1)
    own_rhs = lax.dynamic_index_in_dim(pivot_all, child_index, 0, keepdims=False)
    lower_flat = lower_pivot.reshape(2 * pivot_local, lower_pivot.shape[2])
    pieces = sent_together((lower_flat, lower_update), "rhs", 1, 0)
    width = pieces[0].shape[1]
    blocks = pieces[0].reshape(2, pivot_local, width)
    pivot_mid = paired(blocks, pivot_all)
    update_sum = product(pieces[1], own_rhs)
    update_half = (update_rhs + update_sum).astype(jnp.bfloat16)
    pivot_half = pivot_mid.astype(jnp.bfloat16)
    pivot_known = collect(pivot_half, "panel", 1)
    own_rows = first_row + lax.broadcasted_iota(jnp.int32, (row_count, 1), 0)
    select = (own_rows == maps[None, :]).astype(jnp.bfloat16)
    parent_sum = parent_rhs + product(select, collect(update_half, "panel", 0))
    parent_all = collect(parent_sum.astype(jnp.bfloat16), "panel", 0)
    parent_mid = through(parent_lower, parent_all)
    middle_all = collect(parent_mid.astype(jnp.bfloat16), "panel", 0)
    parent_solution = through(parent_upper, middle_all)
    solution_half = parent_solution.astype(jnp.bfloat16)
    solution_all = collect(solution_half, "panel", 0)
    remote_rows = jnp.take(solution_all, maps, axis=0).reshape(2, FU, rhs_width)
    pieces = sent_together((upper_pivot, upper_update), "rhs", 2, 0)
    child_solution = paired(pieces[0], pivot_known) + paired(pieces[1], remote_rows)
    return (parent_solution, child_solution)


def solution(mesh):
    placed = (
        P(None, "panel", "rhs"),
        P("panel", "rhs"),
        P("panel", "rhs"),
        P(None, "panel", "rhs"),
        P("panel", "rhs"),
        P("panel", "rhs"),
        P("panel", "rhs"),
        P(None, "panel", "rhs"),
        P(None, "panel", "rhs"),
        P(),
    )
    return jax.shard_map(
        shards,
        mesh=mesh,
        in_specs=placed,
        out_specs=(P("panel", "rhs"), P(None, "panel", "rhs")),
        check_vma=False,
    )
```

profile of v0, /device:TPU:1, one launch (start us, length us, event | category | flops | bytes accessed | tf_op | source)
XLA Modules:
  0.0 352.0 jit_solution(16716216847756293906)
XLA Ops:
  7.2 0.8 convert_element_type.22
  8.0 1.2 broadcast_in_dim.27
  9.2 0.0 copy-start.6
  9.2 0.0 copy-start.7
  9.2 13.1 %all-to-all-start = ((bf16[32,2,64,128]{3,2,1,0:T(8,128)(2,1)}), bf16[32,2,64,128]{3,2,1,0:T(8,128)(2,1)S(1)}, u32[]{:S(2)}, u32[]{:S(2)}) async-start(bf16[32,2,64,128]{3,2,1,0:T(8,128)(2,1)} %broadcast_in_dim.27), calls=%async_computation | async-start | bytes 2097152 | tf_op jit(solution)/shard_map/all_to_all | solution.py:11
  22.3 0.0 all-gather.3.cloned.1.call-start
  22.4 0.0 copy-done.6
  22.4 0.0 copy-done.7
  22.4 0.6 pad_maximum_fusion
  23.1 0.0 all-gather.3.cloned.1.call-update
  23.1 26.2 %all-to-all-done = bf16[32,2,64,128]{3,2,1,0:T(8,128)(2,1)S(1)} async-done(((bf16[32,2,64,128]{3,2,1,0:T(8,128)(2,1)}), bf16[32,2,64,128]{3,2,1,0:T(8,128)(2,1)S(1)}, u32[]{:S(2)}, u32[]{:S(2)}) %all-to-all-start) | async-done | bytes 1048608 | tf_op jit(solution)/shard_map/all_to_all | solution.py:11
  49.3 0.0 copy-start.2
  49.3 0.1 copy.20
  49.4 34.8 %all-gather.3.cloned.1.call-done = bf16[256,2048]{1,0:T(8,128)(2,1)} async-done(((bf16[256,128]{1,0:T(8,128)(2,1)}), bf16[256,2048]{1,0:T(8,128)(2,1)}) %all-gather.3.cloned.1.call-update) | async-done | bytes 1048592 | tf_op jit(solution)/shard_map/all_gather | solution.py:33
  84.2 0.0 copy-done.2
  84.2 1.3 fusion.5
  85.5 1.2 broadcast_in_dim.28
  86.7 10.5 %all-to-all-start.1 = ((bf16[32,128,128]{2,1,0:T(8,128)(2,1)}), bf16[32,128,128]{2,1,0:T(8,128)(2,1)S(1)}, u32[]{:S(2)}, u32[]{:S(2)}) async-start(bf16[32,128,128]{2,1,0:T(8,128)(2,1)} %broadcast_in_dim.28), calls=%async_computation.1 | async-start | bytes 2097152 | tf_op jit(solution)/shard_map/all_to_all | solution.py:11
  97.2 0.0 copy-done.4
  97.2 0.1 copy.21
  97.3 26.8 %all-to-all-done.1 = bf16[32,128,128]{2,1,0:T(8,128)(2,1)S(1)} async-done(((bf16[32,128,128]{2,1,0:T(8,128)(2,1)}), bf16[32,128,128]{2,1,0:T(8,128)(2,1)S(1)}, u32[]{:S(2)}, u32[]{:S(2)}) %all-to-all-start.1) | async-done | bytes 1048608 | tf_op jit(solution)/shard_map/all_to_all | solution.py:11
  124.1 1.2 broadcast_in_dim.30
  125.3 6.0 %all-to-all-start.3 = ((bf16[16,128,256]{1,2,0:T(8,128)(2,1)}), bf16[16,128,256]{1,2,0:T(8,128)(2,1)S(1)}, u32[]{:S(2)}, u32[]{:S(2)}) async-start(bf16[16,128,256]{1,2,0:T(8,128)(2,1)} %broadcast_in_dim.30), calls=%async_computation.3 | async-start | bytes 2097152 | tf_op jit(solution)/shard_map/all_to_all | solution.py:11
  131.3 0.0 copy-done.3
  131.3 0.0 copy-done.10
  131.4 0.5 fusion.6
  131.9 24.4 %all-to-all-done.3 = bf16[16,128,256]{1,2,0:T(8,128)(2,1)S(1)} async-done(((bf16[16,128,256]{1,2,0:T(8,128)(2,1)}), bf16[16,128,256]{1,2,0:T(8,128)(2,1)S(1)}, u32[]{:S(2)}, u32[]{:S(2)}) %all-to-all-start.3) | async-done | bytes 1048608 | tf_op jit(solution)/shard_map/all_to_all | solution.py:11
  156.3 1.2 broadcast_in_dim.29
  157.5 10.8 %all-to-all-start.2 = ((bf16[32,128,128]{2,1,0:T(8,128)(2,1)}), bf16[32,128,128]{2,1,0:T(8,128)(2,1)S(1)}, u32[]{:S(2)}, u32[]{:S(2)}) async-start(bf16[32,128,128]{2,1,0:T(8,128)(2,1)} %broadcast_in_dim.29), calls=%async_computation.2 | async-start | bytes 2097152 | tf_op jit(solution)/shard_map/all_to_all | solution.py:11
  168.4 0.0 copy-done.5
  168.4 0.1 copy.23
  168.5 26.8 %all-to-all-done.2 = bf16[32,128,128]{2,1,0:T(8,128)(2,1)S(1)} async-done(((bf16[32,128,128]{2,1,0:T(8,128)(2,1)}), bf16[32,128,128]{2,1,0:T(8,128)(2,1)S(1)}, u32[]{:S(2)}, u32[]{:S(2)}) %all-to-all-start.2) | async-done | bytes 1048608 | tf_op jit(solution)/shard_map/all_to_all | solution.py:11
  195.3 1.3 broadcast_in_dim.32
  196.6 0.0 copy-done
  196.6 3.7 %all-to-all-start.5 = ((bf16[16,128,256]{1,2,0:T(8,128)(2,1)}), bf16[16,128,256]{1,2,0:T(8,128)(2,1)S(1)}, u32[]{:S(2)}, u32[]{:S(2)}) async-start(bf16[16,128,256]{1,2,0:T(8,128)(2,1)} %broadcast_in_dim.32), calls=%async_computation.5 | async-start | bytes 2097152 | tf_op jit(solution)/shard_map/all_to_all | solution.py:11
  200.3 1.7 fusion.9
  202.0 0.1 copy.22
  202.1 23.1 %all-to-all-done.5 = bf16[16,128,256]{1,2,0:T(8,128)(2,1)S(1)} async-done(((bf16[16,128,256]{1,2,0:T(8,128)(2,1)}), bf16[16,128,256]{1,2,0:T(8,128)(2,1)S(1)}, u32[]{:S(2)}, u32[]{:S(2)}) %all-to-all-start.5) | async-done | bytes 1048608 | tf_op jit(solution)/shard_map/all_to_all | solution.py:11
  225.2 1.2 broadcast_in_dim.31
  226.4 10.9 %all-to-all-start.4 = ((bf16[32,128,128]{2,1,0:T(8,128)(2,1)}), bf16[32,128,128]{2,1,0:T(8,128)(2,1)S(1)}, u32[]{:S(2)}, u32[]{:S(2)}) async-start(bf16[32,128,128]{2,1,0:T(8,128)(2,1)} %broadcast_in_dim.31), calls=%async_computation.4 | async-start | bytes 2097152 | tf_op jit(solution)/shard_map/all_to_all | solution.py:11
  237.3 0.0 slice-start
  237.3 1.0 slice-done
  238.3 0.3 convolution_convert_fusion
  238.7 25.5 %all-to-all-done.4 = bf16[32,128,128]{2,1,0:T(8,128)(2,1)S(1)} async-done(((bf16[32,128,128]{2,1,0:T(8,128)(2,1)}), bf16[32,128,128]{2,1,0:T(8,128)(2,1)S(1)}, u32[]{:S(2)}, u32[]{:S(2)}) %all-to-all-start.4) | async-done | bytes 1048608 | tf_op jit(solution)/shard_map/all_to_all | solution.py:11
  264.2 1.2 broadcast_in_dim.33
  265.4 5.6 %all-to-all-start.6 = ((bf16[32,2,64,128]{3,2,1,0:T(8,128)(2,1)}), bf16[32,2,64,128]{3,2,1,0:T(8,128)(2,1)S(1)}, u32[]{:S(2)}, u32[]{:S(2)}) async-start(bf16[32,2,64,128]{3,2,1,0:T(8,128)(2,1)} %broadcast_in_dim.33), calls=%async_computation.6 | async-start | bytes 2097152 | tf_op jit(solution)/shard_map/all_to_all | solution.py:11
  271.0 0.0 all-gather.5.cloned.1.call-start
  271.1 0.0 copy-done.8
  271.1 0.0 copy-done.9
  271.1 0.6 pad_maximum_fusion.1
  271.7 0.0 all-gather.5.cloned.1.call-update
  271.8 0.5 fusion.21
  272.2 0.1 copy.25
  272.4 25.6 %all-to-all-done.6 = bf16[32,2,64,128]{3,2,1,0:T(8,128)(2,1)S(1)} async-done(((bf16[32,2,64,128]{3,2,1,0:T(8,128)(2,1)}), bf16[32,2,64,128]{3,2,1,0:T(8,128)(2,1)S(1)}, u32[]{:S(2)}, u32[]{:S(2)}) %all-to-all-start.6) | async-done | bytes 1048608 | tf_op jit(solution)/shard_map/all_to_all | solution.py:11
  297.9 1.2 broadcast_in_dim.72
  299.1 5.4 %all-to-all-start.7 = ((bf16[32,128,128]{2,1,0:T(8,128)(2,1)}), bf16[32,128,128]{2,1,0:T(8,128)(2,1)S(1)}, u32[]{:S(2)}, u32[]{:S(2)}) async-start(bf16[32,128,128]{2,1,0:T(8,128)(2,1)} %broadcast_in_dim.72), calls=%async_computation.7 | async-start | bytes 2097152 | tf_op jit(solution)/shard_map/all_to_all | solution.py:11
  304.6 0.1 copy.24
  304.7 24.2 %all-gather.5.cloned.1.call-done = bf16[4,64,2048]{2,1,0:T(8,128)(2,1)} async-done(((bf16[4,64,128]{2,1,0:T(8,128)(2,1)}), bf16[4,64,2048]{2,1,0:T(8,128)(2,1)}) %all-gather.5.cloned.1.call-update) | async-done | bytes 1048592 | tf_op jit(solution)/shard_map/all_gather | solution.py:33
  329.0 1.3 fusion.22
  330.3 0.7 copy.26
  331.0 0.6 all-to-all-done.7
  331.7 12.1 %gather_fusion = bf16[4096,128]{1,0:T(8,128)(2,1)S(1)} fusion(bf16[4096,128]{1,0:T(8,128)(2,1)S(1)} %bitcast.34, s32[4096]{0:T(1024)S(1)} %fusion.18), kind=kCustom, calls=%fused_computation | custom fusion | bytes 2113536 | tf_op jit(solution)/shard_map/jit(_take)/gather | solution.py:86
  343.8 0.0 copy-done.1
  343.8 1.4 convolution_add_fusion
  (12 shorter events, 0.0 us)
Async XLA Ops:
  9.2 13.2 %copy-start.6 = (bf16[128,128]{1,0:T(8,128)(2,1)S(1)}, bf16[128,128]{1,0:T(8,128)(2,1)}, u32[]{:S(2)}) copy-start(bf16[128,128]{1,0:T(8,128)(2,1)} %param.14) | copy-start | bytes 98308
  9.2 13.2 %copy-start.7 = (bf16[2,64,128]{2,1,0:T(8,128)(2,1)S(1)}, bf16[2,64,128]{2,1,0:T(8,128)(2,1)}, u32[]{:S(2)}) copy-start(bf16[2,64,128]{2,1,0:T(8,128)(2,1)} %param.13) | copy-start | bytes 98308
  9.2 40.0 %all-to-all-start = ((bf16[32,2,64,128]{3,2,1,0:T(8,128)(2,1)}), bf16[32,2,64,128]{3,2,1,0:T(8,128)(2,1)S(1)}, u32[]{:S(2)}, u32[]{:S(2)}) async-start(bf16[32,2,64,128]{3,2,1,0:T(8,128)(2,1)} %broadcast_in_dim.27), calls=%async_computation | async-start | bytes 2097152 | tf_op jit(solution)/shard_map/all_to_all | solution.py:11
  22.3 61.8 %all-gather.3.cloned.1.call-start = ((), (), s32[]{:S(2)}) async-start(), calls=%async_computation.8 | async-start | bytes 1114112 | tf_op jit(solution)/shard_map/all_gather | solution.py:33
  49.3 34.9 %copy-start.2 = (f32[128,128]{1,0:T(8,128)S(1)}, f32[128,128]{1,0:T(8,128)}, u32[]{:S(2)}) copy-start(f32[128,128]{1,0:T(8,128)} %param.11) | copy-start | bytes 196612
  86.7 10.5 %copy-start.4 = (bf16[128,256]{1,0:T(8,128)(2,1)S(1)}, bf16[128,256]{1,0:T(8,128)(2,1)}, u32[]{:S(2)}) copy-start(bf16[128,256]{1,0:T(8,128)(2,1)} %param.15) | copy-start | bytes 196612
  86.7 37.4 %all-to-all-start.1 = ((bf16[32,128,128]{2,1,0:T(8,128)(2,1)}), bf16[32,128,128]{2,1,0:T(8,128)(2,1)S(1)}, u32[]{:S(2)}, u32[]{:S(2)}) async-start(bf16[32,128,128]{2,1,0:T(8,128)(2,1)} %broadcast_in_dim.28), calls=%async_computation.1 | async-start | bytes 2097152 | tf_op jit(solution)/shard_map/all_to_all | solution.py:11
  125.3 6.1 %copy-start.3 = (s32[4096]{0:T(1024)S(1)}, s32[4096]{0:T(1024)}, u32[]{:S(2)}) copy-start(s32[4096]{0:T(1024)} %param.19) | copy-start | bytes 49156
  125.3 6.1 %copy-start.10 = (f32[128,128]{1,0:T(8,128)S(1)}, f32[128,128]{1,0:T(8,128)}, u32[]{:S(2)}) copy-start(f32[128,128]{1,0:T(8,128)} %param.12) | copy-start | bytes 196612
  125.3 31.1 %all-to-all-start.3 = ((bf16[16,128,256]{1,2,0:T(8,128)(2,1)}), bf16[16,128,256]{1,2,0:T(8,128)(2,1)S(1)}, u32[]{:S(2)}, u32[]{:S(2)}) async-start(bf16[16,128,256]{1,2,0:T(8,128)(2,1)} %broadcast_in_dim.30), calls=%async_computation.3 | async-start | bytes 2097152 | tf_op jit(solution)/shard_map/all_to_all | solution.py:11
  157.5 10.9 %copy-start.5 = (bf16[128,256]{1,0:T(8,128)(2,1)S(1)}, bf16[128,256]{1,0:T(8,128)(2,1)}, u32[]{:S(2)}) copy-start(bf16[128,256]{1,0:T(8,128)(2,1)} %param.16) | copy-start | bytes 196612
  157.5 37.8 %all-to-all-start.2 = ((bf16[32,128,128]{2,1,0:T(8,128)(2,1)}), bf16[32,128,128]{2,1,0:T(8,128)(2,1)S(1)}, u32[]{:S(2)}, u32[]{:S(2)}) async-start(bf16[32,128,128]{2,1,0:T(8,128)(2,1)} %broadcast_in_dim.29), calls=%async_computation.2 | async-start | bytes 2097152 | tf_op jit(solution)/shard_map/all_to_all | solution.py:11
  195.3 1.3 copy-start
  196.6 28.6 %all-to-all-start.5 = ((bf16[16,128,256]{1,2,0:T(8,128)(2,1)}), bf16[16,128,256]{1,2,0:T(8,128)(2,1)S(1)}, u32[]{:S(2)}, u32[]{:S(2)}) async-start(bf16[16,128,256]{1,2,0:T(8,128)(2,1)} %broadcast_in_dim.32), calls=%async_computation.5 | async-start | bytes 2097152 | tf_op jit(solution)/shard_map/all_to_all | solution.py:11
  226.4 37.8 %all-to-all-start.4 = ((bf16[32,128,128]{2,1,0:T(8,128)(2,1)}), bf16[32,128,128]{2,1,0:T(8,128)(2,1)S(1)}, u32[]{:S(2)}, u32[]{:S(2)}) async-start(bf16[32,128,128]{2,1,0:T(8,128)(2,1)} %broadcast_in_dim.31), calls=%async_computation.4 | async-start | bytes 2097152 | tf_op jit(solution)/shard_map/all_to_all | solution.py:11
  237.3 1.0 slice-start
  265.4 5.6 %copy-start.8 = (bf16[2,64,128]{2,1,0:T(8,128)(2,1)S(1)}, bf16[2,64,128]{2,1,0:T(8,128)(2,1)}, u32[]{:S(2)}) copy-start(bf16[2,64,128]{2,1,0:T(8,128)(2,1)} %param.18) | copy-start | bytes 98308
  265.4 5.6 %copy-start.9 = (bf16[2,64,128]{2,1,0:T(8,128)(2,1)S(1)}, bf16[2,64,128]{2,1,0:T(8,128)(2,1)}, u32[]{:S(2)}) copy-start(bf16[2,64,128]{2,1,0:T(8,128)(2,1)} %param.17) | copy-start | bytes 98308
  265.4 32.5 %all-to-all-start.6 = ((bf16[32,2,64,128]{3,2,1,0:T(8,128)(2,1)}), bf16[32,2,64,128]{3,2,1,0:T(8,128)(2,1)S(1)}, u32[]{:S(2)}, u32[]{:S(2)}) async-start(bf16[32,2,64,128]{3,2,1,0:T(8,128)(2,1)} %broadcast_in_dim.33), calls=%async_computation.6 | async-start | bytes 2097152 | tf_op jit(solution)/shard_map/all_to_all | solution.py:11
  271.0 57.9 %all-gather.5.cloned.1.call-start = ((), (), s32[]{:S(2)}) async-start(), calls=%async_computation.9 | async-start | bytes 1114112 | tf_op jit(solution)/shard_map/all_gather | solution.py:33
  299.1 32.5 %all-to-all-start.7 = ((bf16[32,128,128]{2,1,0:T(8,128)(2,1)}), bf16[32,128,128]{2,1,0:T(8,128)(2,1)S(1)}, u32[]{:S(2)}, u32[]{:S(2)}) async-start(bf16[32,128,128]{2,1,0:T(8,128)(2,1)} %broadcast_in_dim.72), calls=%async_computation.7 | async-start | bytes 2097152 | tf_op jit(solution)/shard_map/all_to_all | solution.py:11
  331.7 12.1 %copy-start.1 = (bf16[4,64,2048]{2,1,0:T(8,128)(2,1)S(1)}, bf16[4,64,2048]{2,1,0:T(8,128)(2,1)}, u32[]{:S(2)}) copy-start(bf16[4,64,2048]{2,1,0:T(8,128)(2,1)} %all-gather.5.cloned.1.call-done) | copy-start | bytes 3145732
Sparse Core Ops, SparseCore 0:
  26.7 57.4 all-gather.2
  275.4 53.5 all-gather.4
where the time goes:
time: 353 us; the launch traced here: 352 us
  waiting for transfers between devices  238 us (67%)
  starting transfers between devices  66.1 us (19%)
  local copies, waits for them, and re-layouts  24.2 us (7%)
  between operations  14.3 us (4%)
  matrix products  7.12 us (2%)
    all_to_all x8, waiting for transfers between devices, copy_for_each(): lax.all_to_all(jnp.broadcast_to(shard[None], (peers, *shard.shape)), axis...  179 us
    all_to_all x8, starting transfers between devices, copy_for_each(): lax.all_to_all(jnp.broadcast_to(shard[None], (peers, *shard.shape)), axis...  66 us
    all_gather x2, waiting for transfers between devices, sent_together(): lax.all_gather(both, axis, axis=dim, tiled=True)  59 us
    gather x1, local copies, waits for them, and re-layouts, shards(): remote_rows = jnp.take(solution_all, maps, axis=0).reshape(2, FU, rhs_width)  12.1 us
    broadcast_in_dim x8, local copies, waits for them, and re-layouts, copy_for_each(): jnp.broadcast_to(shard[None], (peers, *shard.shape))  9.72 us
  transfers between devices with their start and end apart: 10, of which 10 were waited for; matrix products, arithmetic and copies ran while one was open for 2% of the time, Pallas kernels for 0%

commit v1 on v0

v1 whole, which is shorter than its diff:
```python
import functools

import jax
import jax.numpy as jnp
from jax import lax
from jax.experimental import pallas as pl
from jax.experimental.pallas import tpu as pltpu
from jax.sharding import Mesh, PartitionSpec as P

BF = jnp.bfloat16
F32 = jnp.float32
CHIPS = ("yl", "z")
RHS = ("x", "yh")
PANEL = ("yl", "z", "c")
NP = 16
W = 64
ROWS = 256
HALF = 128


def nt(a, b):
    return lax.dot_general(a, b, (((1,), (1,)), ((), ())), preferred_element_type=F32)


def nn(a, b):
    return lax.dot_general(a, b, (((1,), (0,)), ((), ())), preferred_element_type=F32)


def vmem():
    return pl.BlockSpec(memory_space=pltpu.VMEM)


def smem():
    return pl.BlockSpec(memory_space=pltpu.SMEM)


def call(kernel, outs, *args):
    return pl.pallas_call(
        kernel,
        out_shape=outs,
        in_specs=[smem()] + [vmem()] * (len(args) - 1),
        out_specs=jax.tree.map(lambda _: vmem(), outs),
    )(*args)


def ordered(both, core):
    half = both.shape[1] // 2
    swapped = jnp.concatenate([both[:, half:], both[:, :half]], axis=1)
    return jnp.where(core == 0, both, swapped)


def row_ids(core, n):
    at = lax.broadcasted_iota(jnp.int32, (n, n), 0)
    half = n // 2
    return jnp.where(core == 0, at, jnp.where(at < half, at + half, at - half))


def keep(x, cond):
    return jnp.where(cond, x, jnp.zeros_like(x))


def forward_children(pos, xg, fm, fo, ur, pr, e, send, ps_out, piv_out):
    chip, core = pos[0], pos[1]
    acc_m = jnp.zeros((W, HALF), F32)
    acc_o = jnp.zeros((W, HALF), F32)
    piv = [jnp.zeros((W, HALF), F32), jnp.zeros((W, HALF), F32)]
    for r in range(NP):
        x = xg[r]
        xs = (x[:, :HALF], x[:, HALF:])
        xc = jnp.where(core == 0, xs[0], xs[1])
        xo = jnp.where(core == 0, xs[1], xs[0])
        acc_m += nt(xc, fm[r, 0:HALF, :])
        acc_o += nt(xo, fo[r, 0:HALF, :])
        for k in range(2):
            lo = HALF + 64 * k
            block = jnp.concatenate([fm[r, lo : lo + 64, :], fo[r, lo : lo + 64, :]], axis=0)
            piv[k] += nt(keep(xs[k], r < chip), block)
    u0 = jnp.where(core == 0, acc_m, acc_o) + ur[0]
    u1 = jnp.where(core == 0, acc_o, acc_m) + ur[1]
    u = jnp.concatenate([u0.astype(BF), u1.astype(BF)], axis=1)
    ps = (pr[...] + nn(u, e[...])).astype(BF)
    rows = row_ids(core, HALF)
    cols = lax.broadcasted_iota(jnp.int32, (HALF, HALF), 1)
    own = xg[chip]
    outs = []
    for k in range(2):
        lo = HALF + 64 * k
        block = jnp.concatenate([fm[chip, lo : lo + 64, :], fo[chip, lo : lo + 64, :]], axis=0)
        x = own[:, k * HALF : (k + 1) * HALF]
        total = ordered(piv[k] + nt(x, keep(block, cols < rows)), core)
        diag = fm[chip, 256:272, :].astype(F32)[k : k + 1] + fo[chip, 256:272, :].astype(F32)[k : k + 1]
        outs.append((total + x.astype(F32) * diag).astype(BF))
    pivot = jnp.concatenate(outs, axis=1)
    ps_out[...] = ps
    piv_out[...] = pivot
    for q in range(NP):
        send[q] = jnp.where(chip <= q, ps, pivot)


def parent_forward(pos, g, ps_ref, mm, mo, send):
    chip, core = pos[0], pos[1]
    acc_m = jnp.zeros((W, HALF), F32)
    acc_o = jnp.zeros((W, HALF), F32)
    for r in range(NP):
        x = keep(g[r], r < chip)
        acc_m += nt(x, mm[r, 0:HALF, :])
        acc_o += nt(x, mo[r, 0:HALF, :])
    rows = row_ids(core, ROWS)
    cols = lax.broadcasted_iota(jnp.int32, (ROWS, ROWS), 1)
    block = jnp.concatenate([mm[chip, 0:HALF, :], mo[chip, 0:HALF, :]], axis=0)
    ps = ps_ref[...]
    total = ordered(jnp.concatenate([acc_m, acc_o], axis=1) + nt(ps, keep(block, cols < rows)), core)
    diag = mm[chip, 128:144, :].astype(F32)[0:1] + mo[chip, 128:144, :].astype(F32)[0:1]
    mid = (total + ps.astype(F32) * diag).astype(BF)
    for q in range(NP):
        send[q] = mid


def parent_backward(pos, g, mm, mo, e, send, sol_out):
    chip, core = pos[0], pos[1]
    acc_m = jnp.zeros((W, HALF), F32)
    acc_o = jnp.zeros((W, HALF), F32)
    for r in range(NP):
        x = keep(g[r], r > chip)
        acc_m += nt(x, mm[r, 0:HALF, :])
        acc_o += nt(x, mo[r, 0:HALF, :])
    rows = row_ids(core, ROWS)
    cols = lax.broadcasted_iota(jnp.int32, (ROWS, ROWS), 1)
    block = jnp.concatenate([mm[chip, 0:HALF, :], mo[chip, 0:HALF, :]], axis=0)
    sol = ordered(jnp.concatenate([acc_m, acc_o], axis=1) + nt(g[chip], keep(block, cols >= rows)), core)
    sol_out[...] = sol
    picked = nt(sol.astype(BF), e[...]).astype(BF)
    for q in range(NP):
        send[q] = picked


def pivot_backward(pos, g, piv_ref, fm, fo, out):
    chip, core = pos[0], pos[1]
    rows = row_ids(core, HALF)
    cols = lax.broadcasted_iota(jnp.int32, (HALF, HALF), 1)
    for k in range(2):
        lo = HALF + 64 * k
        acc = jnp.zeros((HALF, W), F32)
        for r in range(NP):
            block = jnp.concatenate([fm[r, lo : lo + 64, :], fo[r, lo : lo + 64, :]], axis=0)
            acc += nt(block, keep(g[r, :, k * HALF : (k + 1) * HALF], r > chip))
        block = jnp.concatenate([fm[chip, lo : lo + 64, :], fo[chip, lo : lo + 64, :]], axis=0)
        acc += nt(keep(block, cols >= rows), piv_ref[:, k * HALF : (k + 1) * HALF])
        out[k] = acc


def children_backward(pos, g, mm, mo, part, mine, other):
    for k in range(2):
        acc = part[k]
        for r in range(NP):
            cut = slice(k * HALF, (k + 1) * HALF)
            block = jnp.concatenate([mm[r, 144:208, cut], mo[r, 144:208, cut]], axis=0)
            acc += nt(block, g[r, :, cut])
        mine[k] = acc[:64]
        other[k] = acc[64:]


def to_all(block, axes, n):
    return lax.all_to_all(jnp.broadcast_to(block[None], (n, *block.shape)), axes, 0, 0, tiled=True)


def over_rhs(shard):
    by_y = to_all(shard, "yh", 4)
    by_x = to_all(by_y, "x", 4)
    return by_x.reshape(16, *shard.shape)


def partner(x):
    return lax.ppermute(x, "c", [(0, 1), (1, 0)])


def exchange(send):
    return lax.all_to_all(send, CHIPS, 0, 0, tiled=True)


def halves(x, core, axis):
    a, b = jnp.split(x, 2, axis=axis)
    return jnp.where(core == 0, a, b), jnp.where(core == 0, b, a)


def two_terms(x):
    high = lax.reduce_precision(x, 8, 7)
    return high.astype(BF), (x - high).astype(BF)


def shards(pivot_rhs, update_rhs, parent_rhs, lower_pivot, lower_update, parent_lower, parent_upper, upper_pivot, upper_update, maps):
    core = lax.axis_index("c")
    chip = lax.axis_index("yl") * 8 + lax.axis_index("z")
    group = lax.axis_index("x") * 4 + lax.axis_index("yh")
    pos = jnp.stack([chip, core]).astype(jnp.int32)

    to_parent = []
    for p in range(32):
        k, j = divmod(p, 16)
        to_parent.append((p, 2 * j + k))
    uh, ul = two_terms(update_rhs.T)
    moved = lax.ppermute(jnp.concatenate([lower_update, uh, ul], axis=0), PANEL, to_parent)

    xt = pivot_rhs.astype(BF).transpose(2, 0, 1).reshape(128, 128)
    ph, plo = two_terms(parent_rhs.T)
    x_mine, x_give = halves(xt, core, 0)
    ph_mine, ph_give = halves(ph, core, 0)
    pl_mine, pl_give = halves(plo, core, 0)
    got = partner(jnp.concatenate([x_give, ph_give, pl_give], axis=0))

    def sides(mine, other):
        return jnp.where(core == 0, mine, other), jnp.where(core == 0, other, mine)

    x0, x1 = sides(x_mine, got[:64])
    x_block = jnp.concatenate([x0[:, :64], x1[:, :64], x0[:, 64:], x1[:, 64:]], axis=1)
    pr_own = ph_mine.astype(F32) + pl_mine.astype(F32)
    pr_got = got[64:128].astype(F32) + got[128:].astype(F32)
    pr = jnp.concatenate(sides(pr_own, pr_got), axis=1)

    r_at = lax.broadcasted_iota(jnp.int32, (1, 64, 128), 1) + core * 64
    c_at = lax.broadcasted_iota(jnp.int32, (1, 64, 128), 2)
    full_l, on_block = group < chip, group == chip
    pick_low = jnp.logical_or(full_l, jnp.logical_and(on_block, c_at < r_at))
    pivots = jnp.where(pick_low, lower_pivot, upper_pivot).reshape(128, 128)
    diag = jnp.sum(jnp.where(jnp.logical_and(on_block, c_at == r_at), lower_pivot, jnp.zeros_like(lower_pivot)), axis=1)
    diag = jnp.pad(diag, ((0, 14), (0, 0)))
    first = over_rhs(jnp.concatenate([moved[:128], pivots, diag], axis=0))
    first_other = partner(first)

    xg = to_all(x_block, CHIPS, NP)

    r_at = lax.broadcasted_iota(jnp.int32, (128, 256), 0) + core * 128
    c_at = lax.broadcasted_iota(jnp.int32, (128, 256), 1)
    pick_low = jnp.logical_or(full_l, jnp.logical_and(on_block, c_at < r_at))
    parents = jnp.where(pick_low, parent_lower, parent_upper)
    pdiag = jnp.sum(jnp.where(jnp.logical_and(on_block, c_at == r_at), parent_lower, jnp.zeros_like(parent_lower)), axis=0)
    pdiag = jnp.pad(pdiag[None], ((0, 15), (0, 0)))
    uu = jnp.concatenate([upper_update[0], upper_update[1]], axis=1)
    second = over_rhs(jnp.concatenate([parents, pdiag, uu], axis=0))
    second_other = partner(second)

    uh_mine, uh_give = halves(moved[128:256], core, 0)
    ul_mine, ul_give = halves(moved[256:384], core, 0)
    got = partner(jnp.concatenate([uh_give, ul_give], axis=0))
    ur_own = uh_mine.astype(F32) + ul_mine.astype(F32)
    ur_got = got[:64].astype(F32) + got[64:].astype(F32)
    ur = jnp.stack(sides(ur_own, ur_got), axis=0)

    own_maps = lax.dynamic_slice(maps.reshape(2, 2048), (0, chip * 128), (2, 128)).reshape(256, 1)
    spots = lax.broadcasted_iota(jnp.int32, (256, 256), 1) + chip * 256
    e = (own_maps == spots).astype(BF)

    block = jax.ShapeDtypeStruct((W, ROWS), BF)
    sent = jax.ShapeDtypeStruct((NP, W, ROWS), BF)
    send2, ps, piv = call(forward_children, [sent, block, block], pos, xg, first, first_other, ur, pr, e)
    g2 = exchange(send2)
    send3 = call(parent_forward, sent, pos, g2, ps, second, second_other)
    g3 = exchange(send3)
    part = call(pivot_backward, jax.ShapeDtypeStruct((2, HALF, W), F32), pos, g2, piv, first, first_other)
    send4, sol_t = call(parent_backward, [sent, jax.ShapeDtypeStruct((W, ROWS), F32)], pos, g3, second, second_other, e)
    g4 = exchange(send4)

    s0, s1 = halves(sol_t, core, 1)
    s_got = partner(s1)
    parent_solution = jnp.concatenate(sides(s0, s_got), axis=0).T

    out_half = jax.ShapeDtypeStruct((2, 64, W), F32)
    mine, other = call(children_backward, [out_half, out_half], pos, g4, second, second_other, part)
    got = partner(other)
    child_solution = jnp.concatenate(sides(mine, got), axis=2)
    return (parent_solution, child_solution)


def solution(mesh):
    fine = Mesh(mesh.devices.reshape(2, 8, 2, 4, 4), ("yl", "z", "c", "x", "yh"))
    three = P(None, PANEL, RHS)
    two = P(PANEL, RHS)
    return jax.shard_map(
        shards,
        mesh=fine,
        in_specs=(three, two, two, three, two, two, two, three, three, P()),
        out_specs=(two, three),
        check_vma=False,
    )
```

time: 353 us -> 207 us (0.59)
  waiting for transfers between devices: 238 us -> 51.9 us
  blocking collectives: 0 us -> 55.8 us
  Pallas kernels: 0 us -> 18.2 us
  local copies, waits for them, and re-layouts: 24.2 us -> 8.31 us
  between operations: 14.3 us -> 1.03 us
  matrix products: 7.12 us -> 0 us
  other arithmetic: 2.14 us -> 7.2 us
    all_to_all x8 -> x5, waiting for transfers between devices: 179 us -> 49.2 us  [the longest x4 43.5 us: to_all(): lax.all_to_all(jnp.broadcast_to(block[None], (n, *block.shape)), axes, 0,...]
    all_gather x2 -> x0, waiting for transfers between devices: 59 us -> none  [sent_together(): lax.all_gather(both, axis, axis=dim, tiled=True)]
    all_to_all x0 -> x3, blocking collectives: none -> 55.8 us  [the longest x2 41.2 us: exchange(): return lax.all_to_all(send, CHIPS, 0, 0, tiled=True)]
    all_to_all x8 -> x5, starting transfers between devices: 66 us -> 39.3 us  [the longest x4 30.7 us: to_all(): lax.all_to_all(jnp.broadcast_to(block[None], (n, *block.shape)), axes, 0,...]
    ppermute x0 -> x7, starting transfers between devices: none -> 24 us  [the longest x6 18.6 us: partner(): return lax.ppermute(x, 'c', [(0, 1), (1, 0)])]
    pallas_call x0 -> x5, Pallas kernels: none -> 18.2 us  [call(): pl.pallas_call(kernel, out_shape=outs, in_specs=[smem()] + [vmem()] * (le...]
    gather x1 -> x0, local copies, waits for them, and re-layouts: 12.1 us -> none  [shards(): remote_rows = jnp.take(solution_all, maps, axis=0).reshape(2, FU, rhs_width)]
    dot_general x7 -> x0, matrix products: 7.12 us -> none  [the longest x4 4.04 us: product(): return jnp.dot(left, right, preferred_element_type=jnp.float32)]
  transfers between devices with their start and end apart: 10 -> 12, of which waited for: 10 -> 8; matrix products, arithmetic and copies ran while one was open for 2% -> 4% of each run, Pallas kernels for 0% -> 3%
where the time goes in v1:
time: 207 us; the launch traced here: 206 us
  starting transfers between devices  63.2 us (31%)
  blocking collectives  55.8 us (27%)
  waiting for transfers between devices  51.9 us (25%)
  Pallas kernels  18.2 us (9%)
  local copies, waits for them, and re-layouts  8.31 us (4%)
  other arithmetic  7.2 us (3%)
    all_to_all x4, waiting for transfers between devices, to_all(): lax.all_to_all(jnp.broadcast_to(block[None], (n, *block.shape)), axes, 0,...  43.5 us
    all_to_all x2, blocking collectives, exchange(): return lax.all_to_all(send, CHIPS, 0, 0, tiled=True)  41.2 us
    all_to_all x4, starting transfers between devices, to_all(): lax.all_to_all(jnp.broadcast_to(block[None], (n, *block.shape)), axes, 0,...  30.7 us
    ppermute x6, starting transfers between devices, partner(): return lax.ppermute(x, 'c', [(0, 1), (1, 0)])  18.6 us
    pallas_call x5, Pallas kernels, call(): pl.pallas_call(kernel, out_shape=outs, in_specs=[smem()] + [vmem()] * (le...  18.2 us
    all_to_all x1, blocking collectives, to_all(): lax.all_to_all(jnp.broadcast_to(block[None], (n, *block.shape)), axes, 0,...  14.6 us
    all_to_all x1, starting transfers between devices, exchange(): return lax.all_to_all(send, CHIPS, 0, 0, tiled=True)  8.56 us
    all_to_all x1, waiting for transfers between devices, exchange(): return lax.all_to_all(send, CHIPS, 0, 0, tiled=True)  5.65 us
  transfers between devices with their start and end apart: 12, of which 8 were waited for; matrix products, arithmetic and copies ran while one was open for 4% of the time, Pallas kernels for 3%

profile of v1, /device:TPU:1, one launch (start us, length us, event | category | flops | bytes accessed | tf_op | source)
XLA Modules:
  0.0 205.7 jit_solution(13173042112366032091)
XLA Ops:
  0.6 0.0 copy-start.5
  0.6 0.0 copy-start.4
  0.7 0.0 copy-start.8
  0.7 1.0 copy.15
  1.7 0.8 pad_maximum_fusion
  2.4 5.4 %collective-permute-start.1 = (bf16[384,128]{1,0:T(8,128)(2,1)S(1)}, bf16[384,128]{1,0:T(8,128)(2,1)S(1)}, u32[]{:S(2)}, u32[]{:S(2)}) collective-permute-start(bf16[384,128]{1,0:T(8,128)(2,1)S(1)} %pad_maximum_fusion), channel_id=1, source_target_pairs={{0,0},{16,32},{32,64},{48,96},{64,128},{80,160},{96,192},{112,224}... | collective-permute-start | bytes 294920 | tf_op jit(solution)/shard_map/ppermute | solution.py:202
  7.8 0.1 fusion.15
  7.9 0.8 broadcast_select_fusion.2
  8.7 1.7 collective-permute-done.1
  10.4 0.7 broadcast_in_dim.56
  11.2 6.8 %all-to-all-start.1 = ((bf16[4,272,128]{2,1,0:T(8,128)(2,1)}), bf16[4,272,128]{2,1,0:T(8,128)(2,1)S(1)}, u32[]{:S(2)}, u32[]{:S(2)}) async-start(bf16[4,272,128]{2,1,0:T(8,128)(2,1)} %broadcast_in_dim.56), calls=%async_computation.1 | async-start | bytes 557056 | tf_op jit(solution)/shard_map/all_to_all | solution.py:164
  18.0 0.0 copy-done.5
  18.0 0.0 copy-done.4
  18.0 0.1 fusion.5
  18.2 7.8 %all-to-all-done.1 = bf16[4,272,128]{2,1,0:T(8,128)(2,1)S(1)} async-done(((bf16[4,272,128]{2,1,0:T(8,128)(2,1)}), bf16[4,272,128]{2,1,0:T(8,128)(2,1)S(1)}, u32[]{:S(2)}, u32[]{:S(2)}) %all-to-all-start.1) | async-done | bytes 278560 | tf_op jit(solution)/shard_map/all_to_all | solution.py:164
  26.0 14.6 %all_to_all.40 = bf16[4,208,256]{2,1,0:T(8,128)(2,1)S(1)} all-to-all(bf16[4,208,256]{2,1,0:T(8,128)(2,1)S(1)} %broadcast_in_dim.60), channel_id=1, replica_groups=mesh['yl'=2,'z'=8,'c'=2,'x'=4,'yh'=4] {'yh'}, dimensions={0} | all-to-all | bytes 851968 | tf_op jit(solution)/shard_map/all_to_all | solution.py:164
  40.6 1.1 broadcast_in_dim.57
  41.7 4.2 %all-to-all-start.2 = ((bf16[4,4,272,128]{3,2,1,0:T(8,128)(2,1)}), bf16[4,4,272,128]{3,2,1,0:T(8,128)(2,1)}, u32[]{:S(2)}, u32[]{:S(2)}) async-start(bf16[4,4,272,128]{3,2,1,0:T(8,128)(2,1)} %broadcast_in_dim.57), calls=%async_computation.2 | async-start | bytes 2228224 | tf_op jit(solution)/shard_map/all_to_all | solution.py:164
  46.0 0.1 broadcast_select_fusion.3
  46.1 0.1 copy.18
  46.2 0.1 copy.14
  46.4 1.9 collective-permute-start
  48.3 13.9 %all-to-all-done.2 = bf16[4,4,272,128]{3,2,1,0:T(8,128)(2,1)} async-done(((bf16[4,4,272,128]{3,2,1,0:T(8,128)(2,1)}), bf16[4,4,272,128]{3,2,1,0:T(8,128)(2,1)}, u32[]{:S(2)}, u32[]{:S(2)}) %all-to-all-start.2) | async-done | bytes 1114144 | tf_op jit(solution)/shard_map/all_to_all | solution.py:164
  62.1 1.3 broadcast_in_dim.61
  63.5 3.7 %all-to-all-start.5 = ((bf16[4,4,208,256]{3,2,1,0:T(8,128)(2,1)}), bf16[4,4,208,256]{3,2,1,0:T(8,128)(2,1)S(1)}, u32[]{:S(2)}, u32[]{:S(2)}) async-start(bf16[4,4,208,256]{3,2,1,0:T(8,128)(2,1)} %broadcast_in_dim.61), calls=%async_computation.5 | async-start | bytes 3407872 | tf_op jit(solution)/shard_map/all_to_all | solution.py:164
  67.2 0.8 compare_convert_fusion.e
  68.0 0.6 pad_add_fusion.pos
  68.6 0.1 copy.17
  68.7 0.0 collective-permute-done
  68.8 0.1 fusion.19
  68.8 0.1 fusion.20
  68.9 2.3 %collective-permute-start.2 = (bf16[16,272,128]{2,1,0:T(8,128)(2,1)}, bf16[16,272,128]{2,1,0:T(8,128)(2,1)}, u32[]{:S(2)}, u32[]{:S(2)}) collective-permute-start(bf16[16,272,128]{2,1,0:T(8,128)(2,1)} %bitcast.8.fm), channel_id=1, source_target_pairs={{0,16},{16,0},{1,17},{17,1},{2,18},{18,2},{3,19},{19,3},{4,20},{20... | collective-permute-start | bytes 3342344 | tf_op jit(solution)/shard_map/ppermute | solution.py:174
  71.2 0.1 pad_maximum_fusion.5
  71.3 17.7 %all-to-all-done.5 = bf16[4,4,208,256]{3,2,1,0:T(8,128)(2,1)S(1)} async-done(((bf16[4,4,208,256]{3,2,1,0:T(8,128)(2,1)}), bf16[4,4,208,256]{3,2,1,0:T(8,128)(2,1)S(1)}, u32[]{:S(2)}, u32[]{:S(2)}) %all-to-all-start.5) | async-done | bytes 1703968 | tf_op jit(solution)/shard_map/all_to_all | solution.py:164
  89.0 0.9 broadcast_in_dim.52
  89.9 16.0 %all-to-all-start = ((bf16[16,64,256]{2,1,0:T(8,128)(2,1)}), bf16[16,64,256]{2,1,0:T(8,128)(2,1)}, u32[]{:S(2)}, u32[]{:S(2)}) async-start(bf16[16,64,256]{2,1,0:T(8,128)(2,1)} %broadcast_in_dim.52), calls=%async_computation | async-start | bytes 1048576 | tf_op jit(solution)/shard_map/all_to_all | solution.py:164
  105.9 4.1 %collective-permute-start.4 = (bf16[16,208,256]{2,1,0:T(8,128)(2,1)S(1)}, bf16[16,208,256]{2,1,0:T(8,128)(2,1)S(1)}, u32[]{:S(2)}, u32[]{:S(2)}) collective-permute-start(bf16[16,208,256]{2,1,0:T(8,128)(2,1)S(1)} %bitcast.27), channel_id=1, source_target_pairs={{0,16},{16,0},{1,17},{17,1},{2,18},{18,2},{3,19},{19,3},{4,20},{20... | collective-permute-start | bytes 5111816 | tf_op jit(solution)/shard_map/ppermute | solution.py:174
  110.0 1.9 collective-permute-start.3
  112.0 0.6 pad_maximum_fusion.2.pr
  112.6 0.7 collective-permute-done.3
  113.3 0.6 pad_maximum_fusion.1.ur
  113.9 4.2 %all-to-all-done.xg = bf16[16,64,256]{2,1,0:T(8,128)(2,1)} async-done(((bf16[16,64,256]{2,1,0:T(8,128)(2,1)}), bf16[16,64,256]{2,1,0:T(8,128)(2,1)}, u32[]{:S(2)}, u32[]{:S(2)}) %all-to-all-start) | async-done | bytes 524320 | tf_op jit(solution)/shard_map/all_to_all | solution.py:164
  118.1 0.0 collective-permute-done.2.fo
  118.1 4.3 %shard_map.113 = (bf16[16,64,256]{2,1,0:T(8,128)(2,1)}, bf16[64,256]{1,0:T(8,128)(2,1)}, bf16[64,256]{1,0:T(8,128)(2,1)}) custom-call(s32[2]{0:T(128)} %pad_add_fusion.pos, bf16[16,64,256]{2,1,0:T(8,128)(2,1)} %all-to-all-done.xg, bf16[16,272,128]{2,1,0:T(8,128)(2,1)} %bitcast.8.fm, bf16[16,272,128]{2,1,0:T(8,128)(2,1)} %collective-permute-done.2.fo, ...), custom_call_target="tpu_custom_call" | custom-call | tf_op jit(solution)/shard_map/pallas_call | solution.py:38
  122.4 20.5 %all_to_all.41.g = bf16[16,64,256]{2,1,0:T(8,128)(2,1)} all-to-all(bf16[16,64,256]{2,1,0:T(8,128)(2,1)} %get-tuple-element.9), channel_id=1, replica_groups=mesh['yl'=2,'z'=8,'c'=2,'x'=4,'yh'=4] {'yl','z'}, dimensions={0} | all-to-all | bytes 1048576 | tf_op jit(solution)/shard_map/all_to_all | solution.py:178
  142.9 0.0 collective-permute-done.4.mo
  142.9 1.2 copy-done.1
  144.1 3.9 %shard_map.114 = bf16[16,64,256]{2,1,0:T(8,128)(2,1)} custom-call(s32[2]{0:T(128)} %pad_add_fusion.pos, bf16[16,64,256]{2,1,0:T(8,128)(2,1)} %all_to_all.41.g, bf16[64,256]{1,0:T(8,128)(2,1)} %get-tuple-element.10.ps_ref, bf16[16,208,256]{2,1,0:T(8,128)(2,1)} %bitcast.28, bf16[16,208,256]{2,1,0:T(8,128)(2,1)} %copy-done.1), custom_call_target="tpu_custom_call" | custom-call | tf_op jit(solution)/shard_map/pallas_call | solution.py:38
  148.0 20.7 %all_to_all.42.g = bf16[16,64,256]{2,1,0:T(8,128)(2,1)} all-to-all(bf16[16,64,256]{2,1,0:T(8,128)(2,1)} %shard_map.114), channel_id=1, replica_groups=mesh['yl'=2,'z'=8,'c'=2,'x'=4,'yh'=4] {'yl','z'}, dimensions={0} | all-to-all | bytes 1048576 | tf_op jit(solution)/shard_map/all_to_all | solution.py:178
  168.7 4.0 %shard_map.115 = (bf16[16,64,256]{2,1,0:T(8,128)(2,1)}, f32[64,256]{1,0:T(8,128)}) custom-call(s32[2]{0:T(128)} %pad_add_fusion.pos, bf16[16,64,256]{2,1,0:T(8,128)(2,1)} %all_to_all.42.g, bf16[16,208,256]{2,1,0:T(8,128)(2,1)} %bitcast.29, bf16[16,208,256]{2,1,0:T(8,128)(2,1)} %copy-done.1, bf16[256,256]{1,0:T(8,128)(2,1)} %compare_convert_fusion.e), custom_call_target="tpu_custom_call" | custom-call | tf_op jit(solution)/shard_map/pallas_call | solution.py:38
  172.7 8.6 %all-to-all-start.7 = ((bf16[16,64,256]{2,1,0:T(8,128)(2,1)}), bf16[16,64,256]{2,1,0:T(8,128)(2,1)S(1)}, u32[]{:S(2)}, u32[]{:S(2)}) async-start(bf16[16,64,256]{2,1,0:T(8,128)(2,1)} %get-tuple-element.12), calls=%async_computation.7 | async-start | bytes 1048576 | tf_op jit(solution)/shard_map/all_to_all | solution.py:178
  181.3 0.0 copy-start.3
  181.3 0.8 slice_select_fusion
  182.1 2.7 %collective-permute-start.5 = (f32[64,128]{1,0:T(8,128)S(1)}, f32[64,128]{1,0:T(8,128)S(1)}, u32[]{:S(2)}, u32[]{:S(2)}) collective-permute-start(f32[64,128]{1,0:T(8,128)S(1)} %slice_select_fusion), channel_id=1, source_target_pairs={{0,16},{16,0},{1,17},{17,1},{2,18},{18,2},{3,19},{19,3},{4,20},{20... | collective-permute-start | bytes 98312 | tf_op jit(solution)/shard_map/ppermute | solution.py:174
  184.9 2.9 %shard_map.116.part = f32[2,128,64]{2,1,0:T(8,128)} custom-call(s32[2]{0:T(128)} %pad_add_fusion.pos, bf16[16,64,256]{2,1,0:T(8,128)(2,1)} %all_to_all.41.g, bf16[64,256]{1,0:T(8,128)(2,1)} %get-tuple-element.13.piv_ref, bf16[16,272,128]{2,1,0:T(8,128)(2,1)} %bitcast.8.fm, bf16[16,272,128]{2,1,0:T(8,128)(2,1)} %collective-permute-done.2.fo), custom_call_target="tpu_custom_call" | custom-call | tf_op jit(solution)/shard_map/pallas_call | solution.py:38
  187.8 0.0 collective-permute-done.5
  187.8 5.6 %all-to-all-done.7.g = bf16[16,64,256]{2,1,0:T(8,128)(2,1)S(1)} async-done(((bf16[16,64,256]{2,1,0:T(8,128)(2,1)}), bf16[16,64,256]{2,1,0:T(8,128)(2,1)S(1)}, u32[]{:S(2)}, u32[]{:S(2)}) %all-to-all-start.7) | async-done | bytes 524320 | tf_op jit(solution)/shard_map/all_to_all | solution.py:178
  193.4 0.8 copy-done.2
  194.2 3.2 %shard_map.117 = (f32[2,64,64]{2,1,0:T(8,128)}, f32[2,64,64]{2,1,0:T(8,128)}) custom-call(s32[2]{0:T(128)} %pad_add_fusion.pos, bf16[16,64,256]{2,1,0:T(8,128)(2,1)} %copy-done.2, bf16[16,208,256]{2,1,0:T(8,128)(2,1)} %bitcast.30, bf16[16,208,256]{2,1,0:T(8,128)(2,1)} %copy-done.1, f32[2,128,64]{2,1,0:T(8,128)} %shard_map.116.part), custom_call_target="tpu_custom_call" | custom-call | tf_op jit(solution)/shard_map/pallas_call | solution.py:38
  197.4 5.6 %collective-permute-start.6 = (f32[2,64,64]{2,1,0:T(8,128)}, f32[2,64,64]{2,1,0:T(8,128)S(1)}, u32[]{:S(2)}, u32[]{:S(2)}) collective-permute-start(f32[2,64,64]{2,1,0:T(8,128)} %get-tuple-element.15), channel_id=1, source_target_pairs={{0,16},{16,0},{1,17},{17,1},{2,18},{18,2},{3,19},{19,3},{4,20},{20... | collective-permute-start | bytes 98312 | tf_op jit(solution)/shard_map/ppermute | solution.py:174
  203.0 0.7 copy.16
  203.7 0.3 collective-permute-done.6
  204.1 0.8 broadcast_select_fusion.1
  204.9 0.7 pad_maximum_fusion.3
  (35 shorter events, 0.2 us)
Async XLA Ops:
  0.6 17.3 %copy-start.5 = (bf16[128,256]{1,0:T(8,128)(2,1)S(1)}, bf16[128,256]{1,0:T(8,128)(2,1)}, u32[]{:S(2)}) copy-start(bf16[128,256]{1,0:T(8,128)(2,1)} %param.16) | copy-start | bytes 196612
  0.6 17.3 %copy-start.4 = (bf16[128,256]{1,0:T(8,128)(2,1)S(1)}, bf16[128,256]{1,0:T(8,128)(2,1)}, u32[]{:S(2)}) copy-start(bf16[128,256]{1,0:T(8,128)(2,1)} %param.15) | copy-start | bytes 196612
  0.7 17.5 %copy-start.8 = (bf16[2,64,128]{2,1,0:T(8,128)(2,1)S(1)}, bf16[2,64,128]{2,1,0:T(8,128)(2,1)}, u32[]{:S(2)}) copy-start(bf16[2,64,128]{2,1,0:T(8,128)(2,1)} %param.18) | copy-start | bytes 98308
  2.4 8.0 %collective-permute-start.1 = (bf16[384,128]{1,0:T(8,128)(2,1)S(1)}, bf16[384,128]{1,0:T(8,128)(2,1)S(1)}, u32[]{:S(2)}, u32[]{:S(2)}) collective-permute-start(bf16[384,128]{1,0:T(8,128)(2,1)S(1)} %pad_maximum_fusion), channel_id=1, source_target_pairs={{0,0},{16,32},{32,64},{48,96},{64,128},{80,160},{96,192},{112,224}... | collective-permute-start | bytes 294920 | tf_op jit(solution)/shard_map/ppermute | solution.py:202
  11.2 14.8 %all-to-all-start.1 = ((bf16[4,272,128]{2,1,0:T(8,128)(2,1)}), bf16[4,272,128]{2,1,0:T(8,128)(2,1)S(1)}, u32[]{:S(2)}, u32[]{:S(2)}) async-start(bf16[4,272,128]{2,1,0:T(8,128)(2,1)} %broadcast_in_dim.56), calls=%async_computation.1 | async-start | bytes 557056 | tf_op jit(solution)/shard_map/all_to_all | solution.py:164
  40.6 5.4 %copy-start.6 = (f32[2,64,128]{2,1,0:T(8,128)S(1)}, f32[2,64,128]{2,1,0:T(8,128)}, u32[]{:S(2)}) copy-start(f32[2,64,128]{2,1,0:T(8,128)} %param.10) | copy-start | bytes 196612
  40.6 5.6 %copy-start.7 = (f32[128,128]{1,0:T(8,128)S(1)}, f32[128,128]{1,0:T(8,128)}, u32[]{:S(2)}) copy-start(f32[128,128]{1,0:T(8,128)} %param.12) | copy-start | bytes 196612
  41.7 20.4 %all-to-all-start.2 = ((bf16[4,4,272,128]{3,2,1,0:T(8,128)(2,1)}), bf16[4,4,272,128]{3,2,1,0:T(8,128)(2,1)}, u32[]{:S(2)}, u32[]{:S(2)}) async-start(bf16[4,4,272,128]{3,2,1,0:T(8,128)(2,1)} %broadcast_in_dim.57), calls=%async_computation.2 | async-start | bytes 2228224 | tf_op jit(solution)/shard_map/all_to_all | solution.py:164
  46.4 22.4 %collective-permute-start = (bf16[192,128]{1,0:T(8,128)(2,1)S(1)}, bf16[192,128]{1,0:T(8,128)(2,1)S(1)}, u32[]{:S(2)}, u32[]{:S(2)}) collective-permute-start(bf16[192,128]{1,0:T(8,128)(2,1)S(1)} %pad_maximum_fusion.4), channel_id=1, source_target_pairs={{0,16},{16,0},{1,17},{17,1},{2,18},{18,2},{3,19},{19,3},{4,20},{20... | collective-permute-start | bytes 147464 | tf_op jit(solution)/shard_map/ppermute | solution.py:174
  63.5 3.7 %copy-start.9 = (s32[4096]{0:T(1024)S(1)}, s32[4096]{0:T(1024)}, u32[]{:S(2)}) copy-start(s32[4096]{0:T(1024)} %param.19) | copy-start | bytes 49156
  63.5 25.5 %all-to-all-start.5 = ((bf16[4,4,208,256]{3,2,1,0:T(8,128)(2,1)}), bf16[4,4,208,256]{3,2,1,0:T(8,128)(2,1)S(1)}, u32[]{:S(2)}, u32[]{:S(2)}) async-start(bf16[4,4,208,256]{3,2,1,0:T(8,128)(2,1)} %broadcast_in_dim.61), calls=%async_computation.5 | async-start | bytes 3407872 | tf_op jit(solution)/shard_map/all_to_all | solution.py:164
  68.9 49.2 %collective-permute-start.2 = (bf16[16,272,128]{2,1,0:T(8,128)(2,1)}, bf16[16,272,128]{2,1,0:T(8,128)(2,1)}, u32[]{:S(2)}, u32[]{:S(2)}) collective-permute-start(bf16[16,272,128]{2,1,0:T(8,128)(2,1)} %bitcast.8.fm), channel_id=1, source_target_pairs={{0,16},{16,0},{1,17},{17,1},{2,18},{18,2},{3,19},{19,3},{4,20},{20... | collective-permute-start | bytes 3342344 | tf_op jit(solution)/shard_map/ppermute | solution.py:174
  89.0 33.5 %copy-start = (bf16[4,4,208,256]{3,2,1,0:T(8,128)(2,1)}, bf16[4,4,208,256]{3,2,1,0:T(8,128)(2,1)S(1)}, u32[]{:S(2)}) copy-start(bf16[4,4,208,256]{3,2,1,0:T(8,128)(2,1)S(1)} %all-to-all-done.5) | copy-start | bytes 5111812
  89.9 28.3 %all-to-all-start = ((bf16[16,64,256]{2,1,0:T(8,128)(2,1)}), bf16[16,64,256]{2,1,0:T(8,128)(2,1)}, u32[]{:S(2)}, u32[]{:S(2)}) async-start(bf16[16,64,256]{2,1,0:T(8,128)(2,1)} %broadcast_in_dim.52), calls=%async_computation | async-start | bytes 1048576 | tf_op jit(solution)/shard_map/all_to_all | solution.py:164
  105.9 37.0 %collective-permute-start.4 = (bf16[16,208,256]{2,1,0:T(8,128)(2,1)S(1)}, bf16[16,208,256]{2,1,0:T(8,128)(2,1)S(1)}, u32[]{:S(2)}, u32[]{:S(2)}) collective-permute-start(bf16[16,208,256]{2,1,0:T(8,128)(2,1)S(1)} %bitcast.27), channel_id=1, source_target_pairs={{0,16},{16,0},{1,17},{17,1},{2,18},{18,2},{3,19},{19,3},{4,20},{20... | collective-permute-start | bytes 5111816 | tf_op jit(solution)/shard_map/ppermute | solution.py:174
  110.0 3.2 %collective-permute-start.3 = (bf16[128,128]{1,0:T(8,128)(2,1)S(1)}, bf16[128,128]{1,0:T(8,128)(2,1)S(1)}, u32[]{:S(2)}, u32[]{:S(2)}) collective-permute-start(bf16[128,128]{1,0:T(8,128)(2,1)S(1)} %pad_maximum_fusion.6), channel_id=1, source_target_pairs={{0,16},{16,0},{1,17},{17,1},{2,18},{18,2},{3,19},{19,3},{4,20},{20... | collective-permute-start | bytes 98312 | tf_op jit(solution)/shard_map/ppermute | solution.py:174
  142.9 1.2 copy-start.1
  172.7 20.7 %all-to-all-start.7 = ((bf16[16,64,256]{2,1,0:T(8,128)(2,1)}), bf16[16,64,256]{2,1,0:T(8,128)(2,1)S(1)}, u32[]{:S(2)}, u32[]{:S(2)}) async-start(bf16[16,64,256]{2,1,0:T(8,128)(2,1)} %get-tuple-element.12), calls=%async_computation.7 | async-start | bytes 1048576 | tf_op jit(solution)/shard_map/all_to_all | solution.py:178
  181.3 6.5 %copy-start.3 = (f32[64,256]{1,0:T(8,128)S(1)}, f32[64,256]{1,0:T(8,128)}, u32[]{:S(2)}) copy-start(f32[64,256]{1,0:T(8,128)} %get-tuple-element.11) | copy-start | bytes 196612
  182.1 5.6 %collective-permute-start.5 = (f32[64,128]{1,0:T(8,128)S(1)}, f32[64,128]{1,0:T(8,128)S(1)}, u32[]{:S(2)}, u32[]{:S(2)}) collective-permute-start(f32[64,128]{1,0:T(8,128)S(1)} %slice_select_fusion), channel_id=1, source_target_pairs={{0,16},{16,0},{1,17},{17,1},{2,18},{18,2},{3,19},{19,3},{4,20},{20... | collective-permute-start | bytes 98312 | tf_op jit(solution)/shard_map/ppermute | solution.py:174
  193.4 0.8 copy-start.2
  197.4 6.7 %collective-permute-start.6 = (f32[2,64,64]{2,1,0:T(8,128)}, f32[2,64,64]{2,1,0:T(8,128)S(1)}, u32[]{:S(2)}, u32[]{:S(2)}) collective-permute-start(f32[2,64,64]{2,1,0:T(8,128)} %get-tuple-element.15), channel_id=1, source_target_pairs={{0,16},{16,0},{1,17},{17,1},{2,18},{18,2},{3,19},{19,3},{4,20},{20... | collective-permute-start | bytes 98312 | tf_op jit(solution)/shard_map/ppermute | solution.py:174

commit v2 on v1

v2 whole, which is shorter than its diff:
```python
import jax
import jax.numpy as jnp
from jax import lax
from jax.experimental import pallas as pl
from jax.experimental.pallas import tpu as pltpu
from jax.sharding import Mesh, PartitionSpec as P


BF = jnp.bfloat16
F32 = jnp.float32
CHIPS = ("yl", "z")
RHS = ("x", "yh")
PANEL = ("yl", "z", "c")
NP = 16
W = 64
ROWS = 256
HALF = 128


def nt(a, b):
    return lax.dot_general(a, b, (((1,), (1,)), ((), ())), preferred_element_type=F32)


def nn(a, b):
    return lax.dot_general(a, b, (((1,), (0,)), ((), ())), preferred_element_type=F32)


def vmem():
    return pl.BlockSpec(memory_space=pltpu.VMEM)


def smem():
    return pl.BlockSpec(memory_space=pltpu.SMEM)


def near(x):
    return pltpu.with_memory_space_constraint(x, pltpu.VMEM)


def call(kernel, outs, pos, *args):
    args = [pos] + [near(a) if a.ndim > 2 else a for a in args]
    return pl.pallas_call(
        kernel,
        out_shape=outs,
        in_specs=[smem()] + [vmem()] * (len(args) - 1),
        out_specs=jax.tree.map(lambda _: vmem(), outs),
        compiler_params=pltpu.CompilerParams(vmem_limit_bytes=16 * 2**20),
    )(*args)


def ordered(both, core):
    half = both.shape[1] // 2
    swapped = jnp.concatenate([both[:, half:], both[:, :half]], axis=1)
    return jnp.where(core == 0, both, swapped)


def row_ids(core, n):
    at = lax.broadcasted_iota(jnp.int32, (n, n), 0)
    half = n // 2
    return jnp.where(core == 0, at, jnp.where(at < half, at + half, at - half))


def keep(x, cond):
    return jnp.where(cond, x, jnp.zeros_like(x))


def pivot_rows(mine, other, at, k):
    cut = slice(k * HALF, (k + 1) * HALF)
    return jnp.concatenate([mine[at, 64:128, cut], other[at, 64:128, cut]], axis=0)


def update_rows(f, at):
    return jnp.concatenate([f[at, 0:64, :HALF], f[at, 0:64, HALF:]], axis=0)


def forward_children(pos, xg, fm, fo, ur, pr, e, send, ps_out, piv_out):
    chip, core, mid_at = pos[0], pos[1], pos[2]
    acc_m = jnp.zeros((W, HALF), F32)
    acc_o = jnp.zeros((W, HALF), F32)
    piv = [jnp.zeros((W, HALF), F32), jnp.zeros((W, HALF), F32)]
    for r in range(NP):
        src = pos[4 + r]
        x = xg[src]
        xs = (x[:, :HALF], x[:, HALF:])
        xc = jnp.where(core == 0, xs[0], xs[1])
        xo = jnp.where(core == 0, xs[1], xs[0])
        acc_m += nt(xc, update_rows(fm, r))
        acc_o += nt(xo, update_rows(fo, r))
        for k in range(2):
            piv[k] += nt(keep(xs[k], src < chip), pivot_rows(fm, fo, r, k))
    u0 = jnp.where(core == 0, acc_m, acc_o) + ur[0]
    u1 = jnp.where(core == 0, acc_o, acc_m) + ur[1]
    u = jnp.concatenate([u0.astype(BF), u1.astype(BF)], axis=1)
    ps = (pr[...] + nn(u, e[...])).astype(BF)
    rows = row_ids(core, HALF)
    cols = lax.broadcasted_iota(jnp.int32, (HALF, HALF), 1)
    own = xg[chip]
    diag = fm[mid_at, 128:144, :].astype(F32)[0:1] + fo[mid_at, 128:144, :].astype(F32)[0:1]
    outs = []
    for k in range(2):
        cut = slice(k * HALF, (k + 1) * HALF)
        x = own[:, cut]
        total = ordered(piv[k] + nt(x, keep(pivot_rows(fm, fo, mid_at, k), cols < rows)), core)
        outs.append((total + x.astype(F32) * diag[:, cut]).astype(BF))
    pivot = jnp.concatenate(outs, axis=1)
    ps_out[...] = ps
    piv_out[...] = pivot
    for q in range(NP):
        send[q] = jnp.where(chip <= q, ps, pivot)


def parent_forward(pos, g, ps_ref, mm, mo, send):
    chip, core, mid_at = pos[0], pos[1], pos[3]
    acc_m = jnp.zeros((W, HALF), F32)
    acc_o = jnp.zeros((W, HALF), F32)
    for r in range(NP):
        src = pos[20 + r]
        x = keep(g[src], src < chip)
        acc_m += nt(x, mm[r, 0:HALF, :])
        acc_o += nt(x, mo[r, 0:HALF, :])
    rows = row_ids(core, ROWS)
    cols = lax.broadcasted_iota(jnp.int32, (ROWS, ROWS), 1)
    block = jnp.concatenate([mm[mid_at, 0:HALF, :], mo[mid_at, 0:HALF, :]], axis=0)
    ps = ps_ref[...]
    total = ordered(jnp.concatenate([acc_m, acc_o], axis=1) + nt(ps, keep(block, cols < rows)), core)
    diag = mm[mid_at, 128:144, :].astype(F32)[0:1] + mo[mid_at, 128:144, :].astype(F32)[0:1]
    mid = (total + ps.astype(F32) * diag).astype(BF)
    for q in range(NP):
        send[q] = mid


def parent_backward(pos, g, mm, mo, e, send, sol_out):
    chip, core, mid_at = pos[0], pos[1], pos[3]
    acc_m = jnp.zeros((W, HALF), F32)
    acc_o = jnp.zeros((W, HALF), F32)
    for r in range(NP):
        src = pos[20 + r]
        x = keep(g[src], src > chip)
        acc_m += nt(x, mm[r, 0:HALF, :])
        acc_o += nt(x, mo[r, 0:HALF, :])
    rows = row_ids(core, ROWS)
    cols = lax.broadcasted_iota(jnp.int32, (ROWS, ROWS), 1)
    block = jnp.concatenate([mm[mid_at, 0:HALF, :], mo[mid_at, 0:HALF, :]], axis=0)
    sol = ordered(jnp.concatenate([acc_m, acc_o], axis=1) + nt(g[chip], keep(block, cols >= rows)), core)
    sol_out[...] = sol
    picked = nt(sol.astype(BF), e[...]).astype(BF)
    for q in range(NP):
        send[q] = picked


def pivot_backward(pos, g, piv_ref, fm, fo, out):
    chip, core, mid_at = pos[0], pos[1], pos[2]
    rows = row_ids(core, HALF)
    cols = lax.broadcasted_iota(jnp.int32, (HALF, HALF), 1)
    for k in range(2):
        cut = slice(k * HALF, (k + 1) * HALF)
        acc = jnp.zeros((HALF, W), F32)
        for r in range(NP):
            src = pos[4 + r]
            acc += nt(pivot_rows(fm, fo, r, k), keep(g[src, :, cut], src > chip))
        acc += nt(keep(pivot_rows(fm, fo, mid_at, k), cols >= rows), piv_ref[:, cut])
        out[k] = acc


def children_backward(pos, g, um, uo, part, mine, other):
    for k in range(2):
        acc = part[k]
        for r in range(NP):
            cut = slice(k * HALF, (k + 1) * HALF)
            block = jnp.concatenate([um[r, :, cut], uo[r, :, cut]], axis=0)
            acc += nt(block, g[pos[20 + r], :, cut])
        mine[k] = acc[:64]
        other[k] = acc[64:]


def to_all(block, axes, n):
    return lax.all_to_all(jnp.broadcast_to(block[None], (n, *block.shape)), axes, 0, 0, tiled=True)


def shifts(x, axis):
    return [x] + [lax.ppermute(x, axis, [(i, (i + k) % 4) for i in range(4)]) for k in (1, 2, 3)]


def partner(x):
    return lax.ppermute(x, "c", [(0, 1), (1, 0)])


def after(x, *done):
    return lax.optimization_barrier((x, done))[0]


def exchange(send):
    return lax.all_to_all(send, CHIPS, 0, 0, tiled=True)


def halves(x, core, axis):
    a, b = jnp.split(x, 2, axis=axis)
    return jnp.where(core == 0, a, b), jnp.where(core == 0, b, a)


def two_terms(x):
    high = lax.reduce_precision(x, 8, 7)
    return high.astype(BF), (x - high).astype(BF)


def shards(pivot_rhs, update_rhs, parent_rhs, lower_pivot, lower_update, parent_lower, parent_upper, upper_pivot, upper_update, maps):
    core = lax.axis_index("c")
    chip = lax.axis_index("yl") * 8 + lax.axis_index("z")
    group = lax.axis_index("x") * 4 + lax.axis_index("yh")
    place = jnp.arange(4)
    gx, gy = lax.axis_index("x"), lax.axis_index("yh")
    y_from = (gy - place) % 4
    x_from = (gx - place) % 4
    y_at = (gy - chip % 4) % 4
    sources_ax = (place[:, None] * 4 + y_from[None, :]).reshape(16)
    sources_rx = (x_from[:, None] * 4 + y_from[None, :]).reshape(16)
    mid_ax = chip // 4 * 4 + y_at
    mid_rx = (gx - chip // 4) % 4 * 4 + y_at
    pos = jnp.concatenate([jnp.stack([chip, core, mid_ax, mid_rx]), sources_ax, sources_rx]).astype(jnp.int32)

    to_parent = []
    for p in range(32):
        k, j = divmod(p, 16)
        to_parent.append((p, 2 * j + k))
    uh, ul = two_terms(update_rhs.T)
    moved = lax.ppermute(jnp.concatenate([lower_update, uh, ul], axis=0), PANEL, to_parent)

    xt = pivot_rhs.astype(BF).transpose(2, 0, 1).reshape(128, 128)
    ph, plo = two_terms(parent_rhs.T)
    x_mine, x_give = halves(xt, core, 0)
    ph_mine, ph_give = halves(ph, core, 0)
    pl_mine, pl_give = halves(plo, core, 0)
    got = partner(jnp.concatenate([x_give, ph_give, pl_give], axis=0))

    def sides(mine, other):
        return jnp.where(core == 0, mine, other), jnp.where(core == 0, other, mine)

    x0, x1 = sides(x_mine, got[:64])
    x_block = jnp.concatenate([x0[:, :64], x1[:, :64], x0[:, 64:], x1[:, 64:]], axis=1)
    pr_own = ph_mine.astype(F32) + pl_mine.astype(F32)
    pr_got = got[64:128].astype(F32) + got[128:].astype(F32)
    pr = jnp.concatenate(sides(pr_own, pr_got), axis=1)

    xg = to_all(x_block, CHIPS, NP)

    full_l, on_block = group < chip, group == chip
    r_at = lax.broadcasted_iota(jnp.int32, (1, 64, 128), 1) + core * 64
    c_at = lax.broadcasted_iota(jnp.int32, (1, 64, 128), 2)
    pick_low = jnp.logical_or(full_l, jnp.logical_and(on_block, c_at < r_at))
    pivots = jnp.where(pick_low, lower_pivot, upper_pivot)
    diag = jnp.sum(jnp.where(jnp.logical_and(on_block, c_at == r_at), lower_pivot, jnp.zeros_like(lower_pivot)), axis=1)
    r_at = lax.broadcasted_iota(jnp.int32, (128, 256), 0) + core * 128
    c_at = lax.broadcasted_iota(jnp.int32, (128, 256), 1)
    pick_low = jnp.logical_or(full_l, jnp.logical_and(on_block, c_at < r_at))
    parents = jnp.where(pick_low, parent_lower, parent_upper)
    pdiag = jnp.sum(jnp.where(jnp.logical_and(on_block, c_at == r_at), parent_lower, jnp.zeros_like(parent_lower)), axis=0)
    diags = jnp.stack([jnp.concatenate([diag[0], diag[1]]), pdiag])
    diags = jnp.broadcast_to(diags[:, None], (2, 16, 256))

    def side_by_side(two):
        return jnp.concatenate([two[0], two[1]], axis=1)

    own = jnp.concatenate(
        [side_by_side((moved[0:64], moved[64:128])), side_by_side(pivots), diags[0], parents, diags[1]], axis=0
    )
    by_y = shifts(own, "yh")
    first_y, xg = lax.optimization_barrier((jnp.stack([a[:144] for a in by_y]), xg))
    first = to_all(first_y, "x", 4).reshape(16, 144, 256)
    first_other = partner(first)
    second_y = jnp.stack([a[144:] for a in by_y])
    second_x = shifts(second_y, "x")

    uh_mine, uh_give = halves(moved[128:256], core, 0)
    ul_mine, ul_give = halves(moved[256:384], core, 0)
    got = partner(jnp.concatenate([uh_give, ul_give], axis=0))
    ur_own = uh_mine.astype(F32) + ul_mine.astype(F32)
    ur_got = got[:64].astype(F32) + got[64:].astype(F32)
    ur = jnp.stack(sides(ur_own, ur_got), axis=0)

    own_maps = lax.dynamic_slice(maps.reshape(2, 2048), (0, chip * 128), (2, 128)).reshape(256, 1)
    spots = lax.broadcasted_iota(jnp.int32, (256, 256), 1) + chip * 256
    e = (own_maps == spots).astype(BF)

    block = jax.ShapeDtypeStruct((W, ROWS), BF)
    sent = jax.ShapeDtypeStruct((NP, W, ROWS), BF)
    send2, ps, piv = call(forward_children, [sent, block, block], pos, xg, first, first_other, ur, pr, e)
    g2 = exchange(send2)
    second = jnp.concatenate(after(second_x, ps), axis=0)
    second_other = partner(second)
    last_y = jnp.stack(shifts(after(side_by_side(upper_update), ps), "yh"))
    send3 = call(parent_forward, sent, pos, g2, ps, second, second_other)
    g3 = exchange(send3)
    last_x = shifts(after(last_y, send3), "x")
    part = call(pivot_backward, jax.ShapeDtypeStruct((2, HALF, W), F32), pos, g2, piv, first, first_other)
    send4, sol_t = call(parent_backward, [sent, jax.ShapeDtypeStruct((W, ROWS), F32)], pos, g3, second, second_other, e)
    g4 = exchange(send4)
    last = jnp.concatenate(after(last_x, sol_t), axis=0)
    last_other = partner(last)

    s0, s1 = halves(sol_t, core, 1)
    s_got = partner(s1)
    parent_solution = jnp.concatenate(sides(s0, s_got), axis=0).T

    out_half = jax.ShapeDtypeStruct((2, 64, W), F32)
    mine, other = call(children_backward, [out_half, out_half], pos, g4, last, last_other, part)
    got = partner(other)
    child_solution = jnp.concatenate(sides(mine, got), axis=2)
    return (parent_solution, child_solution)


def solution(mesh):
    fine = Mesh(mesh.devices.reshape(2, 8, 2, 4, 4), ("yl", "z", "c", "x", "yh"))
    three = P(None, PANEL, RHS)
    two = P(PANEL, RHS)

    return jax.shard_map(
        shards,
        mesh=fine,
        in_specs=(three, two, two, three, two, two, two, three, three, P()),
        out_specs=(two, three),
        check_vma=False,
    )
```

time: 207 us -> 196 us (0.947)
  starting transfers between devices: 63.2 us -> 106 us
  blocking collectives: 55.8 us -> 18.7 us
  waiting for transfers between devices: 51.9 us -> 35.4 us
  local copies, waits for them, and re-layouts: 8.31 us -> 20.2 us
  Pallas kernels: 18.2 us -> 7.72 us
  other arithmetic: 7.2 us -> 3.95 us
    ppermute x0 -> x12, starting transfers between devices: none -> 46.9 us  [shifts(): lax.ppermute(x, axis, [(i, (i + k) % 4) for i in range(4)])]
    all_to_all x4 -> x2, waiting for transfers between devices: 43.5 us -> 15.5 us  [to_all(): lax.all_to_all(jnp.broadcast_to(block[None], (n, *block.shape)), axes, 0,...]
    all_to_all x2 -> x1, blocking collectives: 41.2 us -> 18.7 us  [exchange(): return lax.all_to_all(send, CHIPS, 0, 0, tiled=True)]
    ppermute x0 -> x12, waiting for transfers between devices: none -> 19.7 us  [shifts(): lax.ppermute(x, axis, [(i, (i + k) % 4) for i in range(4)])]
    all_to_all x4 -> x2, starting transfers between devices: 30.7 us -> 12.8 us  [to_all(): lax.all_to_all(jnp.broadcast_to(block[None], (n, *block.shape)), axes, 0,...]
    all_to_all x1 -> x0, blocking collectives: 14.6 us -> none  [to_all(): lax.all_to_all(jnp.broadcast_to(block[None], (n, *block.shape)), axes, 0,...]
    unnamed x23 -> x54, local copies, waits for them, and re-layouts: 3.8 us -> 15.9 us
    pallas_call x5, Pallas kernels: 18.2 us -> 7.72 us  [call(): pl.pallas_call(kernel, out_shape=outs, in_specs=[smem()] + [vmem()] * (le...]
  transfers between devices with their start and end apart: 12 -> 24, of which waited for: 8 -> 8; matrix products, arithmetic and copies ran while one was open for 4% -> 5% of each run, Pallas kernels for 3% -> 3%
where the time goes in v2:
time: 196 us; the launch traced here: 193 us
  starting transfers between devices  106 us (54%)
  waiting for transfers between devices  35.4 us (18%)
  local copies, waits for them, and re-layouts  20.2 us (10%)
  blocking collectives  18.7 us (10%)
  Pallas kernels  7.72 us (4%)
  other arithmetic  3.95 us (2%)
    ppermute x12, starting transfers between devices, shifts(): lax.ppermute(x, axis, [(i, (i + k) % 4) for i in range(4)])  46.9 us
    ppermute x7, starting transfers between devices, partner(): return lax.ppermute(x, 'c', [(0, 1), (1, 0)])  28.7 us
    ppermute x12, waiting for transfers between devices, shifts(): lax.ppermute(x, axis, [(i, (i + k) % 4) for i in range(4)])  19.7 us
    all_to_all x1, blocking collectives, exchange(): return lax.all_to_all(send, CHIPS, 0, 0, tiled=True)  18.7 us
    unnamed x54, local copies, waits for them, and re-layouts  15.9 us
    all_to_all x2, waiting for transfers between devices, to_all(): lax.all_to_all(jnp.broadcast_to(block[None], (n, *block.shape)), axes, 0,...  15.5 us
    all_to_all x2, starting transfers between devices, exchange(): return lax.all_to_all(send, CHIPS, 0, 0, tiled=True)  15.1 us
    all_to_all x2, starting transfers between devices, to_all(): lax.all_to_all(jnp.broadcast_to(block[None], (n, *block.shape)), axes, 0,...  12.8 us
  transfers between devices with their start and end apart: 24, of which 8 were waited for; matrix products, arithmetic and copies ran while one was open for 5% of the time, Pallas kernels for 3%

profile of v2, /device:TPU:1, one launch (start us, length us, event | category | flops | bytes accessed | tf_op | source)
XLA Modules:
  0.0 193.0 jit_solution(11568497893246067995)
XLA Ops:
  0.7 0.9 copy.15
  1.6 0.8 convert_bitcast_fusion
  2.7 8.7 %collective-permute-start.4 = (bf16[192,128]{1,0:T(8,128)(2,1)S(1)}, bf16[192,128]{1,0:T(8,128)(2,1)S(1)}, u32[]{:S(2)}, u32[]{:S(2)}) collective-permute-start(bf16[192,128]{1,0:T(8,128)(2,1)S(1)} %pad_maximum_fusion.7), channel_id=1, source_target_pairs={{0,16},{16,0},{1,17},{17,1},{2,18},{18,2},{3,19},{19,3},{4,20},{20... | collective-permute-start | bytes 147464 | tf_op jit(solution)/shard_map/ppermute | solution.py:185
  11.4 0.9 copy.12
  12.4 0.8 pad_maximum_fusion.3
  13.2 1.9 collective-permute-start
  15.7 0.9 broadcast_in_dim.49
  16.6 8.7 %all-to-all-start = ((bf16[16,64,256]{2,1,0:T(8,128)(2,1)}), bf16[16,64,256]{2,1,0:T(8,128)(2,1)S(1)}, u32[]{:S(2)}, u32[]{:S(2)}) async-start(bf16[16,64,256]{2,1,0:T(8,128)(2,1)} %broadcast_in_dim.49), calls=%async_computation | async-start | bytes 1048576 | tf_op jit(solution)/shard_map/all_to_all | solution.py:177
  25.3 0.1 constant_dynamic-update-slice_fusion.1
  25.5 4.2 %collective-permute-start.1 = (bf16[288,256]{1,0:T(8,128)(2,1)S(1)}, bf16[288,256]{1,0:T(8,128)(2,1)S(1)}, u32[]{:S(2)}, u32[]{:S(2)}) collective-permute-start(bf16[288,256]{1,0:T(8,128)(2,1)S(1)} %constant_dynamic-update-slice_fusion), channel_id=1, source_target_pairs={{0,1},{1,2},{2,3},{3,0},{4,5},{5,6},{6,7},{7,4},{8,9},{9,10},{10,1... | collective-permute-start | bytes 442376 | tf_op jit(solution)/shard_map/ppermute | solution.py:181
  29.7 5.7 %collective-permute-start.2 = (bf16[288,256]{1,0:T(8,128)(2,1)S(1)}, bf16[288,256]{1,0:T(8,128)(2,1)S(1)}, u32[]{:S(2)}, u32[]{:S(2)}) collective-permute-start(bf16[288,256]{1,0:T(8,128)(2,1)S(1)} %constant_dynamic-update-slice_fusion), channel_id=1, source_target_pairs={{0,2},{1,3},{2,0},{3,1},{4,6},{5,7},{6,4},{7,5},{8,10},{9,11},{10,... | collective-permute-start | bytes 442376 | tf_op jit(solution)/shard_map/ppermute | solution.py:181
  35.4 5.0 %collective-permute-start.3 = (bf16[288,256]{1,0:T(8,128)(2,1)S(1)}, bf16[288,256]{1,0:T(8,128)(2,1)S(1)}, u32[]{:S(2)}, u32[]{:S(2)}) collective-permute-start(bf16[288,256]{1,0:T(8,128)(2,1)S(1)} %constant_dynamic-update-slice_fusion), channel_id=1, source_target_pairs={{0,3},{1,0},{2,1},{3,2},{4,7},{5,4},{6,5},{7,6},{8,11},{9,8},{10,9... | collective-permute-start | bytes 442376 | tf_op jit(solution)/shard_map/ppermute | solution.py:181
  40.4 2.3 %collective-permute-done.1 = bf16[288,256]{1,0:T(8,128)(2,1)S(1)} collective-permute-done((bf16[288,256]{1,0:T(8,128)(2,1)S(1)}, bf16[288,256]{1,0:T(8,128)(2,1)S(1)}, u32[]{:S(2)}, u32[]{:S(2)}) %collective-permute-start.1) | collective-permute-done | bytes 147488 | tf_op jit(solution)/shard_map/ppermute | solution.py:181
  42.7 8.0 %collective-permute-done.2 = bf16[288,256]{1,0:T(8,128)(2,1)S(1)} collective-permute-done((bf16[288,256]{1,0:T(8,128)(2,1)S(1)}, bf16[288,256]{1,0:T(8,128)(2,1)S(1)}, u32[]{:S(2)}, u32[]{:S(2)}) %collective-permute-start.2) | collective-permute-done | bytes 147488 | tf_op jit(solution)/shard_map/ppermute | solution.py:181
  50.8 1.1 broadcast_in_dim.50
  51.9 4.1 %all-to-all-start.1 = ((bf16[4,4,144,256]{3,2,1,0:T(8,128)(2,1)}), bf16[4,4,144,256]{3,2,1,0:T(8,128)(2,1)S(1)}, u32[]{:S(2)}, u32[]{:S(2)}) async-start(bf16[4,4,144,256]{3,2,1,0:T(8,128)(2,1)} %broadcast_in_dim.50), calls=%async_computation.1 | async-start | bytes 2359296 | tf_op jit(solution)/shard_map/all_to_all | solution.py:177
  56.4 15.5 %all-to-all-done.1 = bf16[4,4,144,256]{3,2,1,0:T(8,128)(2,1)S(1)} async-done(((bf16[4,4,144,256]{3,2,1,0:T(8,128)(2,1)}), bf16[4,4,144,256]{3,2,1,0:T(8,128)(2,1)S(1)}, u32[]{:S(2)}, u32[]{:S(2)}) %all-to-all-start.1) | async-done | bytes 1179680 | tf_op jit(solution)/shard_map/all_to_all | solution.py:177
  71.9 3.5 %collective-permute-start.5 = (bf16[16,144,256]{2,1,0:T(8,128)(2,1)S(1)}, bf16[16,144,256]{2,1,0:T(8,128)(2,1)S(1)}, u32[]{:S(2)}, u32[]{:S(2)}) collective-permute-start(bf16[16,144,256]{2,1,0:T(8,128)(2,1)S(1)} %bitcast.55), channel_id=1, source_target_pairs={{0,16},{16,0},{1,17},{17,1},{2,18},{18,2},{3,19},{19,3},{4,20},{20... | collective-permute-start | bytes 3538952 | tf_op jit(solution)/shard_map/ppermute | solution.py:185
  75.6 1.9 collective-permute-start.6
  77.6 2.2 %collective-permute-start.7 = (bf16[4,144,256]{2,1,0:T(8,128)(2,1)S(1)}, bf16[4,144,256]{2,1,0:T(8,128)(2,1)S(1)}, u32[]{:S(2)}, u32[]{:S(2)}) collective-permute-start(bf16[4,144,256]{2,1,0:T(8,128)(2,1)S(1)} %pad_maximum_fusion.1), channel_id=1, source_target_pairs={{0,4},{4,8},{8,12},{12,0},{1,5},{5,9},{9,13},{13,1},{2,6},{6,10},{... | collective-permute-start | bytes 884744 | tf_op jit(solution)/shard_map/ppermute | solution.py:181
  79.8 3.7 %collective-permute-start.8 = (bf16[4,144,256]{2,1,0:T(8,128)(2,1)S(1)}, bf16[4,144,256]{2,1,0:T(8,128)(2,1)S(1)}, u32[]{:S(2)}, u32[]{:S(2)}) collective-permute-start(bf16[4,144,256]{2,1,0:T(8,128)(2,1)S(1)} %pad_maximum_fusion.1), channel_id=1, source_target_pairs={{0,8},{4,12},{8,0},{12,4},{1,9},{5,13},{9,1},{13,5},{2,10},{6,14},... | collective-permute-start | bytes 884744 | tf_op jit(solution)/shard_map/ppermute | solution.py:181
  83.5 2.5 %collective-permute-start.9 = (bf16[4,144,256]{2,1,0:T(8,128)(2,1)S(1)}, bf16[4,144,256]{2,1,0:T(8,128)(2,1)S(1)}, u32[]{:S(2)}, u32[]{:S(2)}) collective-permute-start(bf16[4,144,256]{2,1,0:T(8,128)(2,1)S(1)} %pad_maximum_fusion.1), channel_id=1, source_target_pairs={{0,12},{4,0},{8,4},{12,8},{1,13},{5,1},{9,5},{13,9},{2,14},{6,2},{... | collective-permute-start | bytes 884744 | tf_op jit(solution)/shard_map/ppermute | solution.py:181
  86.1 2.2 %shard_map.113 = (bf16[16,64,256]{2,1,0:T(8,128)(2,1)S(1)}, bf16[64,256]{1,0:T(8,128)(2,1)S(1)}, bf16[64,256]{1,0:T(8,128)(2,1)S(1)}) custom-call(s32[36]{0:T(128)S(1)} %concatenate.51.pos, bf16[16,64,256]{2,1,0:T(8,128)(2,1)S(1)} %all-to-all-done.xg, bf16[16,144,256]{2,1,0:T(8,128)(2,1)S(1)} %bitcast.56, ...), custom_call_target="tpu_custom_call" | custom-call | tf_op jit(solution)/shard_map/pallas_call | solution.py:42
  88.4 0.6 copy-done.15
  89.0 0.4 collective-permute-done.7
  89.4 5.2 %collective-permute-done.8 = bf16[4,144,256]{2,1,0:T(8,128)(2,1)S(1)} collective-permute-done((bf16[4,144,256]{2,1,0:T(8,128)(2,1)S(1)}, bf16[4,144,256]{2,1,0:T(8,128)(2,1)S(1)}, u32[]{:S(2)}, u32[]{:S(2)}) %collective-permute-start.8) | collective-permute-done | bytes 294944 | tf_op jit(solution)/shard_map/ppermute | solution.py:181
  94.5 2.9 %collective-permute-done.9 = bf16[4,144,256]{2,1,0:T(8,128)(2,1)S(1)} collective-permute-done((bf16[4,144,256]{2,1,0:T(8,128)(2,1)S(1)}, bf16[4,144,256]{2,1,0:T(8,128)(2,1)S(1)}, u32[]{:S(2)}, u32[]{:S(2)}) %collective-permute-start.9) | collective-permute-done | bytes 294944 | tf_op jit(solution)/shard_map/ppermute | solution.py:181
  97.5 3.5 %collective-permute-start.10 = (bf16[16,144,256]{2,1,0:T(8,128)(2,1)S(1)}, bf16[16,144,256]{2,1,0:T(8,128)(2,1)S(1)}, u32[]{:S(2)}, u32[]{:S(2)}) collective-permute-start(bf16[16,144,256]{2,1,0:T(8,128)(2,1)S(1)} %constant_dynamic-update-slice_fusion.3.mm), channel_id=1, source_target_pairs={{0,16},{16,0},{1,17},{17,1},{2,18},{18,2},{3,19},{19,3},{4,20},{20... | collective-permute-start | bytes 3538952 | tf_op jit(solution)/shard_map/ppermute | solution.py:185
  101.0 18.7 %all_to_all.25.g = bf16[16,64,256]{2,1,0:T(8,128)(2,1)S(1)} all-to-all(bf16[16,64,256]{2,1,0:T(8,128)(2,1)S(1)} %get-tuple-element.23), channel_id=1, replica_groups=mesh['yl'=2,'z'=8,'c'=2,'x'=4,'yh'=4] {'yl','z'}, dimensions={0} | all-to-all | bytes 1048576 | tf_op jit(solution)/shard_map/all_to_all | solution.py:193
  119.7 1.4 shard_map.114
  121.1 1.0 copy-done
  122.2 0.8 copy-done.2
  123.0 0.8 copy-done.4
  123.8 7.6 %all-to-all-start.3 = ((bf16[16,64,256]{2,1,0:T(8,128)(2,1)}), bf16[16,64,256]{2,1,0:T(8,128)(2,1)}, u32[]{:S(2)}, u32[]{:S(2)}) async-start(bf16[16,64,256]{2,1,0:T(8,128)(2,1)} %copy-done.4), calls=%async_computation.3 | async-start | bytes 1048576 | tf_op jit(solution)/shard_map/all_to_all | solution.py:193
  131.4 0.7 slice_bitcast_fusion.9
  132.2 3.9 %collective-permute-start.12 = (bf16[64,256]{1,0:T(8,128)(2,1)S(1)}, bf16[64,256]{1,0:T(8,128)(2,1)S(1)}, u32[]{:S(2)}, u32[]{:S(2)}) collective-permute-start(bf16[64,256]{1,0:T(8,128)(2,1)S(1)} %pad_maximum_fusion.10), channel_id=1, source_target_pairs={{0,1},{1,2},{2,3},{3,0},{4,5},{5,6},{6,7},{7,4},{8,9},{9,10},{10,1... | collective-permute-start | bytes 98312 | tf_op jit(solution)/shard_map/ppermute | solution.py:181
  136.1 5.3 %collective-permute-start.13 = (bf16[64,256]{1,0:T(8,128)(2,1)S(1)}, bf16[64,256]{1,0:T(8,128)(2,1)S(1)}, u32[]{:S(2)}, u32[]{:S(2)}) collective-permute-start(bf16[64,256]{1,0:T(8,128)(2,1)S(1)} %pad_maximum_fusion.10), channel_id=1, source_target_pairs={{0,2},{1,3},{2,0},{3,1},{4,6},{5,7},{6,4},{7,5},{8,10},{9,11},{10,... | collective-permute-start | bytes 98312 | tf_op jit(solution)/shard_map/ppermute | solution.py:181
  141.4 5.2 %collective-permute-start.14 = (bf16[64,256]{1,0:T(8,128)(2,1)S(1)}, bf16[64,256]{1,0:T(8,128)(2,1)S(1)}, u32[]{:S(2)}, u32[]{:S(2)}) collective-permute-start(bf16[64,256]{1,0:T(8,128)(2,1)S(1)} %pad_maximum_fusion.10), channel_id=1, source_target_pairs={{0,3},{1,0},{2,1},{3,2},{4,7},{5,4},{6,5},{7,6},{8,11},{9,8},{10,9... | collective-permute-start | bytes 98312 | tf_op jit(solution)/shard_map/ppermute | solution.py:181
  146.6 1.0 collective-permute-done.14
  147.6 0.7 pad_maximum_fusion.2
  148.3 1.9 collective-permute-start.15
  150.2 5.4 %collective-permute-start.16 = (bf16[4,64,256]{2,1,0:T(8,128)(2,1)}, bf16[4,64,256]{2,1,0:T(8,128)(2,1)}, u32[]{:S(2)}, u32[]{:S(2)}) collective-permute-start(bf16[4,64,256]{2,1,0:T(8,128)(2,1)} %pad_maximum_fusion.2), channel_id=1, source_target_pairs={{0,8},{4,12},{8,0},{12,4},{1,9},{5,13},{9,1},{13,5},{2,10},{6,14},... | collective-permute-start | bytes 393224 | tf_op jit(solution)/shard_map/ppermute | solution.py:181
  155.7 1.9 collective-permute-start.17
  157.6 1.3 copy-done.1
  158.9 0.9 copy-done.6
  159.8 2.1 %shard_map.115 = (bf16[16,64,256]{2,1,0:T(8,128)(2,1)S(1)}, f32[64,256]{1,0:T(8,128)S(1)}) custom-call(s32[36]{0:T(128)S(1)} %concatenate.51.pos, bf16[16,64,256]{2,1,0:T(8,128)(2,1)} %all-to-all-done.3.g, bf16[16,144,256]{2,1,0:T(8,128)(2,1)S(1)} %constant_dynamic-update-slice_fusion.3.mm, bf16[16,144,256]{2,1,0:T(8,128)(2,1)S(1)} %copy-done.1, ...), custom_call_target="tpu_custom_call" | custom-call | tf_op jit(solution)/shard_map/pallas_call | solution.py:42
  161.9 0.6 copy-done.12
  162.6 0.8 copy-done.9
  163.3 7.5 %all-to-all-start.4 = ((bf16[16,64,256]{2,1,0:T(8,128)(2,1)}), bf16[16,64,256]{2,1,0:T(8,128)(2,1)S(1)}, u32[]{:S(2)}, u32[]{:S(2)}) async-start(bf16[16,64,256]{2,1,0:T(8,128)(2,1)} %copy-done.9), calls=%async_computation.4 | async-start | bytes 1048576 | tf_op jit(solution)/shard_map/all_to_all | solution.py:193
  170.8 0.9 constant_dynamic-update-slice_fusion.10
  171.8 0.9 constant_dynamic-update-slice_fusion.9
  172.7 0.9 constant_dynamic-update-slice_fusion.8
  173.6 0.9 constant_dynamic-update-slice_fusion.7.um
  174.5 5.3 %collective-permute-start.18 = (bf16[16,64,256]{2,1,0:T(8,128)(2,1)S(1)}, bf16[16,64,256]{2,1,0:T(8,128)(2,1)S(1)}, u32[]{:S(2)}, u32[]{:S(2)}) collective-permute-start(bf16[16,64,256]{2,1,0:T(8,128)(2,1)S(1)} %constant_dynamic-update-slice_fusion.7.um), channel_id=1, source_target_pairs={{0,16},{16,0},{1,17},{17,1},{2,18},{18,2},{3,19},{19,3},{4,20},{20... | collective-permute-start | bytes 1572872 | tf_op jit(solution)/shard_map/ppermute | solution.py:185
  179.9 1.9 collective-permute-start.11
  181.8 0.7 copy-done.16
  182.6 1.0 shard_map.116.part
  183.6 0.8 copy-done.10
  184.4 1.0 copy-done.8
  185.5 1.0 copy-done.11
  186.5 1.0 shard_map.117
  187.5 3.9 %collective-permute-start.19 = (f32[2,64,64]{2,1,0:T(8,128)S(1)}, f32[2,64,64]{2,1,0:T(8,128)S(1)}, u32[]{:S(2)}, u32[]{:S(2)}) collective-permute-start(f32[2,64,64]{2,1,0:T(8,128)S(1)} %get-tuple-element.39), channel_id=1, source_target_pairs={{0,16},{16,0},{1,17},{17,1},{2,18},{18,2},{3,19},{19,3},{4,20},{20... | collective-permute-start | bytes 98312 | tf_op jit(solution)/shard_map/ppermute | solution.py:185
  191.4 0.7 copy.16
  192.3 0.7 pad_maximum_fusion.6
  (105 shorter events, 1.8 us)
Async XLA Ops:
  0.6 14.6 %copy-start.19 = (bf16[2,64,128]{2,1,0:T(8,128)(2,1)S(1)}, bf16[2,64,128]{2,1,0:T(8,128)(2,1)}, u32[]{:S(2)}) copy-start(bf16[2,64,128]{2,1,0:T(8,128)(2,1)} %param.13) | copy-start | bytes 98308
  0.6 14.6 %copy-start.20 = (bf16[2,64,128]{2,1,0:T(8,128)(2,1)S(1)}, bf16[2,64,128]{2,1,0:T(8,128)(2,1)}, u32[]{:S(2)}) copy-start(bf16[2,64,128]{2,1,0:T(8,128)(2,1)} %param.17) | copy-start | bytes 98308
  2.7 12.8 %collective-permute-start.4 = (bf16[192,128]{1,0:T(8,128)(2,1)S(1)}, bf16[192,128]{1,0:T(8,128)(2,1)S(1)}, u32[]{:S(2)}, u32[]{:S(2)}) collective-permute-start(bf16[192,128]{1,0:T(8,128)(2,1)S(1)} %pad_maximum_fusion.7), channel_id=1, source_target_pairs={{0,16},{16,0},{1,17},{17,1},{2,18},{18,2},{3,19},{19,3},{4,20},{20... | collective-permute-start | bytes 147464 | tf_op jit(solution)/shard_map/ppermute | solution.py:185
  13.2 12.1 %collective-permute-start = (bf16[384,128]{1,0:T(8,128)(2,1)S(1)}, bf16[384,128]{1,0:T(8,128)(2,1)S(1)}, u32[]{:S(2)}, u32[]{:S(2)}) collective-permute-start(bf16[384,128]{1,0:T(8,128)(2,1)S(1)} %pad_maximum_fusion.3), channel_id=1, source_target_pairs={{0,0},{16,32},{32,64},{48,96},{64,128},{80,160},{96,192},{112,224}... | collective-permute-start | bytes 294920 | tf_op jit(solution)/shard_map/ppermute | solution.py:226
  15.3 10.0 %copy-start.17 = (bf16[128,256]{1,0:T(8,128)(2,1)S(1)}, bf16[128,256]{1,0:T(8,128)(2,1)}, u32[]{:S(2)}) copy-start(bf16[128,256]{1,0:T(8,128)(2,1)} %param.15) | copy-start | bytes 196612
  15.3 10.0 %copy-start.18 = (bf16[128,256]{1,0:T(8,128)(2,1)S(1)}, bf16[128,256]{1,0:T(8,128)(2,1)}, u32[]{:S(2)}) copy-start(bf16[128,256]{1,0:T(8,128)(2,1)} %param.16) | copy-start | bytes 196612
  16.6 34.2 %all-to-all-start = ((bf16[16,64,256]{2,1,0:T(8,128)(2,1)}), bf16[16,64,256]{2,1,0:T(8,128)(2,1)S(1)}, u32[]{:S(2)}, u32[]{:S(2)}) async-start(bf16[16,64,256]{2,1,0:T(8,128)(2,1)} %broadcast_in_dim.49), calls=%async_computation | async-start | bytes 1048576 | tf_op jit(solution)/shard_map/all_to_all | solution.py:177
  25.5 17.2 %collective-permute-start.1 = (bf16[288,256]{1,0:T(8,128)(2,1)S(1)}, bf16[288,256]{1,0:T(8,128)(2,1)S(1)}, u32[]{:S(2)}, u32[]{:S(2)}) collective-permute-start(bf16[288,256]{1,0:T(8,128)(2,1)S(1)} %constant_dynamic-update-slice_fusion), channel_id=1, source_target_pairs={{0,1},{1,2},{2,3},{3,0},{4,5},{5,6},{6,7},{7,4},{8,9},{9,10},{10,1... | collective-permute-start | bytes 442376 | tf_op jit(solution)/shard_map/ppermute | solution.py:181
  29.7 21.0 %collective-permute-start.2 = (bf16[288,256]{1,0:T(8,128)(2,1)S(1)}, bf16[288,256]{1,0:T(8,128)(2,1)S(1)}, u32[]{:S(2)}, u32[]{:S(2)}) collective-permute-start(bf16[288,256]{1,0:T(8,128)(2,1)S(1)} %constant_dynamic-update-slice_fusion), channel_id=1, source_target_pairs={{0,2},{1,3},{2,0},{3,1},{4,6},{5,7},{6,4},{7,5},{8,10},{9,11},{10,... | collective-permute-start | bytes 442376 | tf_op jit(solution)/shard_map/ppermute | solution.py:181
  35.4 15.3 %collective-permute-start.3 = (bf16[288,256]{1,0:T(8,128)(2,1)S(1)}, bf16[288,256]{1,0:T(8,128)(2,1)S(1)}, u32[]{:S(2)}, u32[]{:S(2)}) collective-permute-start(bf16[288,256]{1,0:T(8,128)(2,1)S(1)} %constant_dynamic-update-slice_fusion), channel_id=1, source_target_pairs={{0,3},{1,0},{2,1},{3,2},{4,7},{5,4},{6,5},{7,6},{8,11},{9,8},{10,9... | collective-permute-start | bytes 442376 | tf_op jit(solution)/shard_map/ppermute | solution.py:181
  51.9 4.4 %copy-start.21 = (s32[4096]{0:T(1024)S(1)}, s32[4096]{0:T(1024)}, u32[]{:S(2)}) copy-start(s32[4096]{0:T(1024)} %param.19) | copy-start | bytes 49156
  51.9 20.0 %all-to-all-start.1 = ((bf16[4,4,144,256]{3,2,1,0:T(8,128)(2,1)}), bf16[4,4,144,256]{3,2,1,0:T(8,128)(2,1)S(1)}, u32[]{:S(2)}, u32[]{:S(2)}) async-start(bf16[4,4,144,256]{3,2,1,0:T(8,128)(2,1)} %broadcast_in_dim.50), calls=%async_computation.1 | async-start | bytes 2359296 | tf_op jit(solution)/shard_map/all_to_all | solution.py:177
  71.9 14.2 %collective-permute-start.5 = (bf16[16,144,256]{2,1,0:T(8,128)(2,1)S(1)}, bf16[16,144,256]{2,1,0:T(8,128)(2,1)S(1)}, u32[]{:S(2)}, u32[]{:S(2)}) collective-permute-start(bf16[16,144,256]{2,1,0:T(8,128)(2,1)S(1)} %bitcast.55), channel_id=1, source_target_pairs={{0,16},{16,0},{1,17},{17,1},{2,18},{18,2},{3,19},{19,3},{4,20},{20... | collective-permute-start | bytes 3538952 | tf_op jit(solution)/shard_map/ppermute | solution.py:185
  75.5 12.8 %copy-start.5 = (bf16[256,256]{1,0:T(8,128)(2,1)}, bf16[256,256]{1,0:T(8,128)(2,1)S(1)}, u32[]{:S(2)}) copy-start(bf16[256,256]{1,0:T(8,128)(2,1)S(1)} %compare_convert_fusion.e) | copy-start | bytes 393220
  75.6 10.4 %collective-permute-start.6 = (bf16[128,128]{1,0:T(8,128)(2,1)S(1)}, bf16[128,128]{1,0:T(8,128)(2,1)S(1)}, u32[]{:S(2)}, u32[]{:S(2)}) collective-permute-start(bf16[128,128]{1,0:T(8,128)(2,1)S(1)} %pad_maximum_fusion.9), channel_id=1, source_target_pairs={{0,16},{16,0},{1,17},{17,1},{2,18},{18,2},{3,19},{19,3},{4,20},{20... | collective-permute-start | bytes 98312 | tf_op jit(solution)/shard_map/ppermute | solution.py:185
  77.6 11.8 %collective-permute-start.7 = (bf16[4,144,256]{2,1,0:T(8,128)(2,1)S(1)}, bf16[4,144,256]{2,1,0:T(8,128)(2,1)S(1)}, u32[]{:S(2)}, u32[]{:S(2)}) collective-permute-start(bf16[4,144,256]{2,1,0:T(8,128)(2,1)S(1)} %pad_maximum_fusion.1), channel_id=1, source_target_pairs={{0,4},{4,8},{8,12},{12,0},{1,5},{5,9},{9,13},{13,1},{2,6},{6,10},{... | collective-permute-start | bytes 884744 | tf_op jit(solution)/shard_map/ppermute | solution.py:181
  79.8 14.7 %collective-permute-start.8 = (bf16[4,144,256]{2,1,0:T(8,128)(2,1)S(1)}, bf16[4,144,256]{2,1,0:T(8,128)(2,1)S(1)}, u32[]{:S(2)}, u32[]{:S(2)}) collective-permute-start(bf16[4,144,256]{2,1,0:T(8,128)(2,1)S(1)} %pad_maximum_fusion.1), channel_id=1, source_target_pairs={{0,8},{4,12},{8,0},{12,4},{1,9},{5,13},{9,1},{13,5},{2,10},{6,14},... | collective-permute-start | bytes 884744 | tf_op jit(solution)/shard_map/ppermute | solution.py:181
  83.5 13.9 %collective-permute-start.9 = (bf16[4,144,256]{2,1,0:T(8,128)(2,1)S(1)}, bf16[4,144,256]{2,1,0:T(8,128)(2,1)S(1)}, u32[]{:S(2)}, u32[]{:S(2)}) collective-permute-start(bf16[4,144,256]{2,1,0:T(8,128)(2,1)S(1)} %pad_maximum_fusion.1), channel_id=1, source_target_pairs={{0,12},{4,0},{8,4},{12,8},{1,13},{5,1},{9,5},{13,9},{2,14},{6,2},{... | collective-permute-start | bytes 884744 | tf_op jit(solution)/shard_map/ppermute | solution.py:181
  88.3 0.6 copy-start.15
  97.5 22.1 %collective-permute-start.10 = (bf16[16,144,256]{2,1,0:T(8,128)(2,1)S(1)}, bf16[16,144,256]{2,1,0:T(8,128)(2,1)S(1)}, u32[]{:S(2)}, u32[]{:S(2)}) collective-permute-start(bf16[16,144,256]{2,1,0:T(8,128)(2,1)S(1)} %constant_dynamic-update-slice_fusion.3.mm), channel_id=1, source_target_pairs={{0,16},{16,0},{1,17},{17,1},{2,18},{18,2},{3,19},{19,3},{4,20},{20... | collective-permute-start | bytes 3538952 | tf_op jit(solution)/shard_map/ppermute | solution.py:185
  121.1 1.1 copy-start
  122.2 0.8 copy-start.2
  123.0 0.8 copy-start.4
  123.8 33.8 %all-to-all-start.3 = ((bf16[16,64,256]{2,1,0:T(8,128)(2,1)}), bf16[16,64,256]{2,1,0:T(8,128)(2,1)}, u32[]{:S(2)}, u32[]{:S(2)}) async-start(bf16[16,64,256]{2,1,0:T(8,128)(2,1)} %copy-done.4), calls=%async_computation.3 | async-start | bytes 1048576 | tf_op jit(solution)/shard_map/all_to_all | solution.py:193
  132.2 14.4 %collective-permute-start.12 = (bf16[64,256]{1,0:T(8,128)(2,1)S(1)}, bf16[64,256]{1,0:T(8,128)(2,1)S(1)}, u32[]{:S(2)}, u32[]{:S(2)}) collective-permute-start(bf16[64,256]{1,0:T(8,128)(2,1)S(1)} %pad_maximum_fusion.10), channel_id=1, source_target_pairs={{0,1},{1,2},{2,3},{3,0},{4,5},{5,6},{6,7},{7,4},{8,9},{9,10},{10,1... | collective-permute-start | bytes 98312 | tf_op jit(solution)/shard_map/ppermute | solution.py:181
  136.1 10.6 %collective-permute-start.13 = (bf16[64,256]{1,0:T(8,128)(2,1)S(1)}, bf16[64,256]{1,0:T(8,128)(2,1)S(1)}, u32[]{:S(2)}, u32[]{:S(2)}) collective-permute-start(bf16[64,256]{1,0:T(8,128)(2,1)S(1)} %pad_maximum_fusion.10), channel_id=1, source_target_pairs={{0,2},{1,3},{2,0},{3,1},{4,6},{5,7},{6,4},{7,5},{8,10},{9,11},{10,... | collective-permute-start | bytes 98312 | tf_op jit(solution)/shard_map/ppermute | solution.py:181
  141.4 6.2 %collective-permute-start.14 = (bf16[64,256]{1,0:T(8,128)(2,1)S(1)}, bf16[64,256]{1,0:T(8,128)(2,1)S(1)}, u32[]{:S(2)}, u32[]{:S(2)}) collective-permute-start(bf16[64,256]{1,0:T(8,128)(2,1)S(1)} %pad_maximum_fusion.10), channel_id=1, source_target_pairs={{0,3},{1,0},{2,1},{3,2},{4,7},{5,4},{6,5},{7,6},{8,11},{9,8},{10,9... | collective-permute-start | bytes 98312 | tf_op jit(solution)/shard_map/ppermute | solution.py:181
  148.3 14.2 %collective-permute-start.15 = (bf16[4,64,256]{2,1,0:T(8,128)(2,1)}, bf16[4,64,256]{2,1,0:T(8,128)(2,1)}, u32[]{:S(2)}, u32[]{:S(2)}) collective-permute-start(bf16[4,64,256]{2,1,0:T(8,128)(2,1)} %pad_maximum_fusion.2), channel_id=1, source_target_pairs={{0,4},{4,8},{8,12},{12,0},{1,5},{5,9},{9,13},{13,1},{2,6},{6,10},{... | collective-permute-start | bytes 393224 | tf_op jit(solution)/shard_map/ppermute | solution.py:181
  150.2 12.3 %collective-permute-start.16 = (bf16[4,64,256]{2,1,0:T(8,128)(2,1)}, bf16[4,64,256]{2,1,0:T(8,128)(2,1)}, u32[]{:S(2)}, u32[]{:S(2)}) collective-permute-start(bf16[4,64,256]{2,1,0:T(8,128)(2,1)} %pad_maximum_fusion.2), channel_id=1, source_target_pairs={{0,8},{4,12},{8,0},{12,4},{1,9},{5,13},{9,1},{13,5},{2,10},{6,14},... | collective-permute-start | bytes 393224 | tf_op jit(solution)/shard_map/ppermute | solution.py:181
  155.7 6.9 %collective-permute-start.17 = (bf16[4,64,256]{2,1,0:T(8,128)(2,1)}, bf16[4,64,256]{2,1,0:T(8,128)(2,1)}, u32[]{:S(2)}, u32[]{:S(2)}) collective-permute-start(bf16[4,64,256]{2,1,0:T(8,128)(2,1)} %pad_maximum_fusion.2), channel_id=1, source_target_pairs={{0,12},{4,0},{8,4},{12,8},{1,13},{5,1},{9,5},{13,9},{2,14},{6,2},{... | collective-permute-start | bytes 393224 | tf_op jit(solution)/shard_map/ppermute | solution.py:181
  157.6 1.3 copy-start.1
  158.9 0.9 copy-start.6
  161.9 0.6 copy-start.12
  162.5 0.8 copy-start.9
  162.5 19.3 %copy-start.3 = (bf16[16,64,256]{2,1,0:T(8,128)(2,1)S(1)}, bf16[16,64,256]{2,1,0:T(8,128)(2,1)}, u32[]{:S(2)}) copy-start(bf16[16,64,256]{2,1,0:T(8,128)(2,1)} %copy-done.2) | copy-start | bytes 1572868
  162.5 17.3 %copy-start.13 = (f32[64,256]{1,0:T(8,128)S(1)}, f32[64,256]{1,0:T(8,128)}, u32[]{:S(2)}) copy-start(f32[64,256]{1,0:T(8,128)} %copy-done.12) | copy-start | bytes 196612
  163.3 21.1 %all-to-all-start.4 = ((bf16[16,64,256]{2,1,0:T(8,128)(2,1)}), bf16[16,64,256]{2,1,0:T(8,128)(2,1)S(1)}, u32[]{:S(2)}, u32[]{:S(2)}) async-start(bf16[16,64,256]{2,1,0:T(8,128)(2,1)} %copy-done.9), calls=%async_computation.4 | async-start | bytes 1048576 | tf_op jit(solution)/shard_map/all_to_all | solution.py:193
  174.5 9.0 %copy-start.7 = (bf16[16,64,256]{2,1,0:T(8,128)(2,1)}, bf16[16,64,256]{2,1,0:T(8,128)(2,1)S(1)}, u32[]{:S(2)}) copy-start(bf16[16,64,256]{2,1,0:T(8,128)(2,1)S(1)} %constant_dynamic-update-slice_fusion.7.um) | copy-start | bytes 1572868
  174.5 9.1 %collective-permute-start.18 = (bf16[16,64,256]{2,1,0:T(8,128)(2,1)S(1)}, bf16[16,64,256]{2,1,0:T(8,128)(2,1)S(1)}, u32[]{:S(2)}, u32[]{:S(2)}) collective-permute-start(bf16[16,64,256]{2,1,0:T(8,128)(2,1)S(1)} %constant_dynamic-update-slice_fusion.7.um), channel_id=1, source_target_pairs={{0,16},{16,0},{1,17},{17,1},{2,18},{18,2},{3,19},{19,3},{4,20},{20... | collective-permute-start | bytes 1572872 | tf_op jit(solution)/shard_map/ppermute | solution.py:185
  179.9 3.7 %collective-permute-start.11 = (f32[64,128]{1,0:T(8,128)S(1)}, f32[64,128]{1,0:T(8,128)S(1)}, u32[]{:S(2)}, u32[]{:S(2)}) collective-permute-start(f32[64,128]{1,0:T(8,128)S(1)} %slice_select_fusion), channel_id=1, source_target_pairs={{0,16},{16,0},{1,17},{17,1},{2,18},{18,2},{3,19},{19,3},{4,20},{20... | collective-permute-start | bytes 98312 | tf_op jit(solution)/shard_map/ppermute | solution.py:185
  181.8 0.8 copy-start.16
  182.6 1.0 copy-start.14
  183.6 0.8 copy-start.10
  184.4 1.0 copy-start.8
  185.4 1.0 copy-start.11
  187.5 4.8 %collective-permute-start.19 = (f32[2,64,64]{2,1,0:T(8,128)S(1)}, f32[2,64,64]{2,1,0:T(8,128)S(1)}, u32[]{:S(2)}, u32[]{:S(2)}) collective-permute-start(f32[2,64,64]{2,1,0:T(8,128)S(1)} %get-tuple-element.39), channel_id=1, source_target_pairs={{0,16},{16,0},{1,17},{17,1},{2,18},{18,2},{3,19},{19,3},{4,20},{20... | collective-permute-start | bytes 98312 | tf_op jit(solution)/shard_map/ppermute | solution.py:185

commit v3 on v2

--- a/solution.py
+++ b/solution.py
@@ -73,7 +73,33 @@
     return jnp.concatenate([f[at, 0:64, :HALF], f[at, 0:64, HALF:]], axis=0)
 
 
-def forward_children(pos, xg, fm, fo, ur, pr, e, send, ps_out, piv_out):
+def own_columns(core, rows):
+    turned = rows.T
+    return jnp.where(core == 0, turned[:W], turned[W:])
+
+
+def first_block(pos, mine, other, send):
+    core = pos[1]
+    a = mine[...].astype(F32)
+    b = other[...].astype(F32)
+    low, high = jnp.where(core == 0, a, b), jnp.where(core == 0, b, a)
+    rows = jnp.concatenate([low[:64], high[:64], low[64:], high[64:]], axis=0)
+    block = own_columns(core, rows).astype(BF)
+    for q in range(NP):
+        send[q] = block
+
+
+def join(pos, a, b, c, d, out):
+    for i, x in enumerate((a, b, c, d)):
+        out[4 * i : 4 * i + 4] = x[...]
+
+
+def joined(pos, pieces):
+    n, *rest = pieces[0].shape
+    return call(join, jax.ShapeDtypeStruct((4 * n, *rest), pieces[0].dtype), pos, *pieces)
+
+
+def forward_children(pos, xg, fm, fo, mine, other, e, send, piv_out, diag_out):
     chip, core, mid_at = pos[0], pos[1], pos[2]
     acc_m = jnp.zeros((W, HALF), F32)
     acc_o = jnp.zeros((W, HALF), F32)
@@ -88,10 +114,16 @@
         acc_o += nt(xo, update_rows(fo, r))
         for k in range(2):
             piv[k] += nt(keep(xs[k], src < chip), pivot_rows(fm, fo, r, k))
-    u0 = jnp.where(core == 0, acc_m, acc_o) + ur[0]
-    u1 = jnp.where(core == 0, acc_o, acc_m) + ur[1]
+    terms = [x[...].astype(F32) for x in (mine, other)]
+    acc_m += own_columns(core, terms[0][:HALF] + terms[0][HALF : 2 * HALF])
+    acc_o += own_columns(core, terms[1][:HALF] + terms[1][HALF : 2 * HALF])
+    u0 = jnp.where(core == 0, acc_m, acc_o)
+    u1 = jnp.where(core == 0, acc_o, acc_m)
+    pr_m, pr_o = (t[2 * HALF : 3 * HALF] + t[3 * HALF :] for t in terms)
+    pr_rows = jnp.concatenate([jnp.where(core == 0, pr_m, pr_o), jnp.where(core == 0, pr_o, pr_m)], axis=0)
+    pr = own_columns(core, pr_rows)
     u = jnp.concatenate([u0.astype(BF), u1.astype(BF)], axis=1)
-    ps = (pr[...] + nn(u, e[...])).astype(BF)
+    ps = (pr + nn(u, e[...])).astype(BF)
     rows = row_ids(core, HALF)
     cols = lax.broadcasted_iota(jnp.int32, (HALF, HALF), 1)
     own = xg[chip]
@@ -103,13 +135,14 @@
         total = ordered(piv[k] + nt(x, keep(pivot_rows(fm, fo, mid_at, k), cols < rows)), core)
         outs.append((total + x.astype(F32) * diag[:, cut]).astype(BF))
     pivot = jnp.concatenate(outs, axis=1)
-    ps_out[...] = ps
     piv_out[...] = pivot
+    diag_out[0] = fm[mid_at, 128:144, :]
+    diag_out[1] = fo[mid_at, 128:144, :]
     for q in range(NP):
         send[q] = jnp.where(chip <= q, ps, pivot)
 
 
-def parent_forward(pos, g, ps_ref, mm, mo, send):
+def parent_forward(pos, g, mm, mo, diags, send):
     chip, core, mid_at = pos[0], pos[1], pos[3]
     acc_m = jnp.zeros((W, HALF), F32)
     acc_o = jnp.zeros((W, HALF), F32)
@@ -121,9 +154,9 @@
     rows = row_ids(core, ROWS)
     cols = lax.broadcasted_iota(jnp.int32, (ROWS, ROWS), 1)
     block = jnp.concatenate([mm[mid_at, 0:HALF, :], mo[mid_at, 0:HALF, :]], axis=0)
-    ps = ps_ref[...]
+    ps = g[chip]
     total = ordered(jnp.concatenate([acc_m, acc_o], axis=1) + nt(ps, keep(block, cols < rows)), core)
-    diag = mm[mid_at, 128:144, :].astype(F32)[0:1] + mo[mid_at, 128:144, :].astype(F32)[0:1]
+    diag = diags[0].astype(F32)[1:2] + diags[1].astype(F32)[1:2]
     mid = (total + ps.astype(F32) * diag).astype(BF)
     for q in range(NP):
         send[q] = mid
@@ -167,7 +200,7 @@
         acc = part[k]
         for r in range(NP):
             cut = slice(k * HALF, (k + 1) * HALF)
-            block = jnp.concatenate([um[r, :, cut], uo[r, :, cut]], axis=0)
+            block = jnp.concatenate([um[r, 128:192, cut], uo[r, 128:192, cut]], axis=0)
             acc += nt(block, g[pos[20 + r], :, cut])
         mine[k] = acc[:64]
         other[k] = acc[64:]
@@ -178,7 +211,10 @@
 
 
 def shifts(x, axis):
-    return [x] + [lax.ppermute(x, axis, [(i, (i + k) % 4) for i in range(4)]) for k in (1, 2, 3)]
+    moved = [x]
+    for k in (1, 2, 3):
+        moved.append(lax.ppermute(x, axis, [(i, (i + k) % 4) for i in range(4)]))
+    return moved
 
 
 def partner(x):
@@ -222,26 +258,17 @@
     for p in range(32):
         k, j = divmod(p, 16)
         to_parent.append((p, 2 * j + k))
-    uh, ul = two_terms(update_rhs.T)
+    uh, ul = two_terms(update_rhs)
     moved = lax.ppermute(jnp.concatenate([lower_update, uh, ul], axis=0), PANEL, to_parent)
 
-    xt = pivot_rhs.astype(BF).transpose(2, 0, 1).reshape(128, 128)
-    ph, plo = two_terms(parent_rhs.T)
-    x_mine, x_give = halves(xt, core, 0)
-    ph_mine, ph_give = halves(ph, core, 0)
-    pl_mine, pl_give = halves(plo, core, 0)
-    got = partner(jnp.concatenate([x_give, ph_give, pl_give], axis=0))
+    x_rows = pivot_rhs.astype(BF).reshape(128, 128)
+    x_other = partner(x_rows)
+    sent = jax.ShapeDtypeStruct((NP, W, ROWS), BF)
+    send1 = call(first_block, sent, pos, x_rows, x_other)
+    xg = exchange(send1)
 
     def sides(mine, other):
         return jnp.where(core == 0, mine, other), jnp.where(core == 0, other, mine)
-
-    x0, x1 = sides(x_mine, got[:64])
-    x_block = jnp.concatenate([x0[:, :64], x1[:, :64], x0[:, 64:], x1[:, 64:]], axis=1)
-    pr_own = ph_mine.astype(F32) + pl_mine.astype(F32)
-    pr_got = got[64:128].astype(F32) + got[128:].astype(F32)
-    pr = jnp.concatenate(sides(pr_own, pr_got), axis=1)
-
-    xg = to_all(x_block, CHIPS, NP)
 
     full_l, on_block = group < chip, group == chip
     r_at = lax.broadcasted_iota(jnp.int32, (1, 64, 128), 1) + core * 64
@@ -254,55 +281,44 @@
     pick_low = jnp.logical_or(full_l, jnp.logical_and(on_block, c_at < r_at))
     parents = jnp.where(pick_low, parent_lower, parent_upper)
     pdiag = jnp.sum(jnp.where(jnp.logical_and(on_block, c_at == r_at), parent_lower, jnp.zeros_like(parent_lower)), axis=0)
-    diags = jnp.stack([jnp.concatenate([diag[0], diag[1]]), pdiag])
-    diags = jnp.broadcast_to(diags[:, None], (2, 16, 256))
+    diags = jnp.pad(jnp.stack([jnp.concatenate([diag[0], diag[1]]), pdiag]), ((0, 14), (0, 0)))
 
     def side_by_side(two):
         return jnp.concatenate([two[0], two[1]], axis=1)
 
-    own = jnp.concatenate(
-        [side_by_side((moved[0:64], moved[64:128])), side_by_side(pivots), diags[0], parents, diags[1]], axis=0
-    )
-    by_y = shifts(own, "yh")
-    first_y, xg = lax.optimization_barrier((jnp.stack([a[:144] for a in by_y]), xg))
+    first_own = jnp.concatenate([side_by_side((moved[0:64], moved[64:128])), side_by_side(pivots), diags], axis=0)
+    second_own = jnp.concatenate([parents, side_by_side(upper_update)], axis=0)
+    first_y = shifts(first_own, "yh")
+    first_y, xg = lax.optimization_barrier((jnp.stack(first_y), xg))
     first = to_all(first_y, "x", 4).reshape(16, 144, 256)
     first_other = partner(first)
-    second_y = jnp.stack([a[144:] for a in by_y])
+    second_y = jnp.stack(shifts(after(second_own, first_y), "yh"))
     second_x = shifts(second_y, "x")
 
-    uh_mine, uh_give = halves(moved[128:256], core, 0)
-    ul_mine, ul_give = halves(moved[256:384], core, 0)
-    got = partner(jnp.concatenate([uh_give, ul_give], axis=0))
-    ur_own = uh_mine.astype(F32) + ul_mine.astype(F32)
-    ur_got = got[:64].astype(F32) + got[64:].astype(F32)
-    ur = jnp.stack(sides(ur_own, ur_got), axis=0)
+    ph, plo = two_terms(parent_rhs)
+    others = jnp.concatenate([moved[128:], ph, plo], axis=0)
+    others_got = partner(others)
 
     own_maps = lax.dynamic_slice(maps.reshape(2, 2048), (0, chip * 128), (2, 128)).reshape(256, 1)
     spots = lax.broadcasted_iota(jnp.int32, (256, 256), 1) + chip * 256
     e = (own_maps == spots).astype(BF)
 
     block = jax.ShapeDtypeStruct((W, ROWS), BF)
-    sent = jax.ShapeDtypeStruct((NP, W, ROWS), BF)
-    send2, ps, piv = call(forward_children, [sent, block, block], pos, xg, first, first_other, ur, pr, e)
+    send2, piv, diags = call(forward_children, [sent, block, jax.ShapeDtypeStruct((2, 16, ROWS), BF)], pos, xg, first, first_other, others, others_got, e)
     g2 = exchange(send2)
-    second = jnp.concatenate(after(second_x, ps), axis=0)
+    second = joined(pos, after(second_x, piv))
     second_other = partner(second)
-    last_y = jnp.stack(shifts(after(side_by_side(upper_update), ps), "yh"))
-    send3 = call(parent_forward, sent, pos, g2, ps, second, second_other)
+    send3 = call(parent_forward, sent, pos, g2, second, second_other, diags)
     g3 = exchange(send3)
-    last_x = shifts(after(last_y, send3), "x")
     part = call(pivot_backward, jax.ShapeDtypeStruct((2, HALF, W), F32), pos, g2, piv, first, first_other)
     send4, sol_t = call(parent_backward, [sent, jax.ShapeDtypeStruct((W, ROWS), F32)], pos, g3, second, second_other, e)
     g4 = exchange(send4)
-    last = jnp.concatenate(after(last_x, sol_t), axis=0)
-    last_other = partner(last)
-
     s0, s1 = halves(sol_t, core, 1)
     s_got = partner(s1)
     parent_solution = jnp.concatenate(sides(s0, s_got), axis=0).T
 
     out_half = jax.ShapeDtypeStruct((2, 64, W), F32)
-    mine, other = call(children_backward, [out_half, out_half], pos, g4, last, last_other, part)
+    mine, other = call(children_backward, [out_half, out_half], pos, g4, second, second_other, part)
     got = partner(other)
     child_solution = jnp.concatenate(sides(mine, got), axis=2)
     return (parent_solution, child_solution)

time: 196 us -> 190 us (0.969)
  blocking collectives: 18.7 us -> 38.9 us
  starting transfers between devices: 106 us -> 88.1 us
  local copies, waits for them, and re-layouts: 20.2 us -> 6.55 us
  waiting for transfers between devices: 35.4 us -> 37.9 us
  Pallas kernels: 7.72 us -> 9.82 us
    all_to_all x1 -> x2, blocking collectives: 18.7 us -> 38.9 us  [exchange(): return lax.all_to_all(send, CHIPS, 0, 0, tiled=True)]
    ppermute x12 -> x9, starting transfers between devices: 46.9 us -> 35.3 us  [shifts(): moved.append(lax.ppermute(x, axis, [(i, (i + k) % 4) for i in range(4)]))]
    unnamed x54 -> x21, local copies, waits for them, and re-layouts: 15.9 us -> 5.12 us
    all_to_all x2 -> x1, starting transfers between devices: 12.8 us -> 4.14 us  [to_all(): lax.all_to_all(jnp.broadcast_to(block[None], (n, *block.shape)), axes, 0,...]
    all_to_all x2, waiting for transfers between devices: 0.01 us -> 4.8 us  [exchange(): return lax.all_to_all(send, CHIPS, 0, 0, tiled=True)]
    ppermute x1, starting transfers between devices: 1.91 us -> 5.37 us  [shards(): lax.ppermute(jnp.concatenate([lower_update, uh, ul], axis=0), PANEL, to_p...]
    ppermute x7 -> x6, starting transfers between devices: 28.7 us -> 25.3 us  [partner(): return lax.ppermute(x, 'c', [(0, 1), (1, 0)])]
    all_to_all x2, starting transfers between devices: 15.1 us -> 17.9 us  [exchange(): return lax.all_to_all(send, CHIPS, 0, 0, tiled=True)]
  transfers between devices with their start and end apart: 24 -> 19, of which waited for: 8 -> 10; matrix products, arithmetic and copies ran while one was open for 5% -> 2% of each run, Pallas kernels for 3% -> 2%
where the time goes in v3:
time: 190 us; the launch traced here: 188 us
  starting transfers between devices  88.1 us (46%)
  blocking collectives  38.9 us (20%)
  waiting for transfers between devices  37.9 us (20%)
  Pallas kernels  9.82 us (5%)
  local copies, waits for them, and re-layouts  6.55 us (3%)
  other arithmetic  5.5 us (3%)
    all_to_all x2, blocking collectives, exchange(): return lax.all_to_all(send, CHIPS, 0, 0, tiled=True)  38.9 us
    ppermute x9, starting transfers between devices, shifts(): moved.append(lax.ppermute(x, axis, [(i, (i + k) % 4) for i in range(4)]))  35.3 us
    ppermute x6, starting transfers between devices, partner(): return lax.ppermute(x, 'c', [(0, 1), (1, 0)])  25.3 us
    ppermute x9, waiting for transfers between devices, shifts(): moved.append(lax.ppermute(x, axis, [(i, (i + k) % 4) for i in range(4)]))  18.5 us
    all_to_all x2, starting transfers between devices, exchange(): return lax.all_to_all(send, CHIPS, 0, 0, tiled=True)  17.9 us
    all_to_all x1, waiting for transfers between devices, to_all(): lax.all_to_all(jnp.broadcast_to(block[None], (n, *block.shape)), axes, 0,...  13.5 us
    pallas_call x7, Pallas kernels, call(): pl.pallas_call(kernel, out_shape=outs, in_specs=[smem()] + [vmem()] * (le...  9.82 us
    ppermute x1, starting transfers between devices, shards(): lax.ppermute(jnp.concatenate([lower_update, uh, ul], axis=0), PANEL, to_p...  5.37 us
  transfers between devices with their start and end apart: 19, of which 10 were waited for; matrix products, arithmetic and copies ran while one was open for 2% of the time, Pallas kernels for 2%

profile of v3, /device:TPU:1, one launch (start us, length us, event | category | flops | bytes accessed | tf_op | source)
XLA Modules:
  0.0 188.0 jit_solution(15998900847270065391)
XLA Ops:
  0.6 0.9 reduce-precision_convert_fusion.1
  1.5 0.8 pad_maximum_fusion.3
  2.3 5.4 %collective-permute-start = (bf16[384,128]{1,0:T(8,128)(2,1)S(1)}, bf16[384,128]{1,0:T(8,128)(2,1)S(1)}, u32[]{:S(2)}, u32[]{:S(2)}) collective-permute-start(bf16[384,128]{1,0:T(8,128)(2,1)S(1)} %pad_maximum_fusion.3), channel_id=1, source_target_pairs={{0,0},{16,32},{32,64},{48,96},{64,128},{80,160},{96,192},{112,224}... | collective-permute-start | bytes 294920 | tf_op jit(solution)/shard_map/ppermute | solution.py:262
  7.6 0.8 convert_element_type.26
  8.5 4.0 %collective-permute-start.4 = (bf16[128,128]{1,0:T(8,128)(2,1)S(1)}, bf16[128,128]{1,0:T(8,128)(2,1)S(1)}, u32[]{:S(2)}, u32[]{:S(2)}) collective-permute-start(bf16[128,128]{1,0:T(8,128)(2,1)S(1)} %bitcast.34), channel_id=1, source_target_pairs={{0,16},{16,0},{1,17},{17,1},{2,18},{18,2},{3,19},{19,3},{4,20},{20... | collective-permute-start | bytes 98312 | tf_op jit(solution)/shard_map/ppermute | solution.py:221
  12.6 0.1 fusion.9
  12.7 1.0 fusion.4
  13.7 0.1 broadcast_add_fusion
  13.8 0.8 broadcast_select_fusion.2
  14.7 0.1 add.109
  14.7 0.1 add.113
  14.8 0.1 concatenate.33.pos
  14.9 0.0 collective-permute-done.4.other
  14.9 1.5 shard_map.113
  16.4 9.3 %all-to-all-start = ((bf16[16,64,256]{2,1,0:T(8,128)(2,1)}), bf16[16,64,256]{2,1,0:T(8,128)(2,1)S(1)}, u32[]{:S(2)}, u32[]{:S(2)}) async-start(bf16[16,64,256]{2,1,0:T(8,128)(2,1)} %shard_map.113), calls=%async_computation | async-start | bytes 1048576 | tf_op jit(solution)/shard_map/all_to_all | solution.py:229
  25.7 0.0 collective-permute-done
  25.7 7.5 %collective-permute-start.2 = (bf16[144,256]{1,0:T(8,128)(2,1)S(1)}, bf16[144,256]{1,0:T(8,128)(2,1)S(1)}, u32[]{:S(2)}, u32[]{:S(2)}) collective-permute-start(bf16[144,256]{1,0:T(8,128)(2,1)S(1)} %pad_maximum_fusion.4), channel_id=1, source_target_pairs={{0,2},{1,3},{2,0},{3,1},{4,6},{5,7},{6,4},{7,5},{8,10},{9,11},{10,... | collective-permute-start | bytes 221192 | tf_op jit(solution)/shard_map/ppermute | solution.py:216
  33.2 2.0 %collective-permute-start.3 = (bf16[144,256]{1,0:T(8,128)(2,1)S(1)}, bf16[144,256]{1,0:T(8,128)(2,1)S(1)}, u32[]{:S(2)}, u32[]{:S(2)}) collective-permute-start(bf16[144,256]{1,0:T(8,128)(2,1)S(1)} %pad_maximum_fusion.4), channel_id=1, source_target_pairs={{0,3},{1,0},{2,1},{3,2},{4,7},{5,4},{6,5},{7,6},{8,11},{9,8},{10,9... | collective-permute-start | bytes 221192 | tf_op jit(solution)/shard_map/ppermute | solution.py:216
  35.2 4.2 %collective-permute-start.1 = (bf16[144,256]{1,0:T(8,128)(2,1)S(1)}, bf16[144,256]{1,0:T(8,128)(2,1)S(1)}, u32[]{:S(2)}, u32[]{:S(2)}) collective-permute-start(bf16[144,256]{1,0:T(8,128)(2,1)S(1)} %pad_maximum_fusion.4), channel_id=1, source_target_pairs={{0,1},{1,2},{2,3},{3,0},{4,5},{5,6},{6,7},{7,4},{8,9},{9,10},{10,1... | collective-permute-start | bytes 221192 | tf_op jit(solution)/shard_map/ppermute | solution.py:216
  39.4 0.6 collective-permute-done.2
  40.0 2.4 %collective-permute-done.1 = bf16[144,256]{1,0:T(8,128)(2,1)S(1)} collective-permute-done((bf16[144,256]{1,0:T(8,128)(2,1)S(1)}, bf16[144,256]{1,0:T(8,128)(2,1)S(1)}, u32[]{:S(2)}, u32[]{:S(2)}) %collective-permute-start.1) | collective-permute-done | bytes 73760 | tf_op jit(solution)/shard_map/ppermute | solution.py:216
  42.5 0.0 all-to-all-done.xg
  42.5 1.1 broadcast_in_dim.33
  43.6 4.1 %all-to-all-start.1 = ((bf16[4,4,144,256]{3,2,1,0:T(8,128)(2,1)}), bf16[4,4,144,256]{3,2,1,0:T(8,128)(2,1)S(1)}, u32[]{:S(2)}, u32[]{:S(2)}) async-start(bf16[4,4,144,256]{3,2,1,0:T(8,128)(2,1)} %broadcast_in_dim.33), calls=%async_computation.1 | async-start | bytes 2359296 | tf_op jit(solution)/shard_map/all_to_all | solution.py:210
  47.8 13.5 %all-to-all-done.1 = bf16[4,4,144,256]{3,2,1,0:T(8,128)(2,1)S(1)} async-done(((bf16[4,4,144,256]{3,2,1,0:T(8,128)(2,1)}), bf16[4,4,144,256]{3,2,1,0:T(8,128)(2,1)S(1)}, u32[]{:S(2)}, u32[]{:S(2)}) %all-to-all-start.1) | async-done | bytes 1179680 | tf_op jit(solution)/shard_map/all_to_all | solution.py:210
  61.3 5.8 %collective-permute-start.5 = (bf16[16,144,256]{2,1,0:T(8,128)(2,1)S(1)}, bf16[16,144,256]{2,1,0:T(8,128)(2,1)S(1)}, u32[]{:S(2)}, u32[]{:S(2)}) collective-permute-start(bf16[16,144,256]{2,1,0:T(8,128)(2,1)S(1)} %bitcast.31), channel_id=1, source_target_pairs={{0,16},{16,0},{1,17},{17,1},{2,18},{18,2},{3,19},{19,3},{4,20},{20... | collective-permute-start | bytes 3538952 | tf_op jit(solution)/shard_map/ppermute | solution.py:221
  67.2 3.2 %collective-permute-start.7 = (bf16[192,256]{1,0:T(8,128)(2,1)S(1)}, bf16[192,256]{1,0:T(8,128)(2,1)S(1)}, u32[]{:S(2)}, u32[]{:S(2)}) collective-permute-start(bf16[192,256]{1,0:T(8,128)(2,1)S(1)} %maximum_maximum_fusion), channel_id=1, source_target_pairs={{0,1},{1,2},{2,3},{3,0},{4,5},{5,6},{6,7},{7,4},{8,9},{9,10},{10,1... | collective-permute-start | bytes 294920 | tf_op jit(solution)/shard_map/ppermute | solution.py:216
  70.5 4.8 %collective-permute-start.8 = (bf16[192,256]{1,0:T(8,128)(2,1)S(1)}, bf16[192,256]{1,0:T(8,128)(2,1)S(1)}, u32[]{:S(2)}, u32[]{:S(2)}) collective-permute-start(bf16[192,256]{1,0:T(8,128)(2,1)S(1)} %maximum_maximum_fusion), channel_id=1, source_target_pairs={{0,2},{1,3},{2,0},{3,1},{4,6},{5,7},{6,4},{7,5},{8,10},{9,11},{10,... | collective-permute-start | bytes 294920 | tf_op jit(solution)/shard_map/ppermute | solution.py:216
  75.2 5.3 %collective-permute-start.9 = (bf16[192,256]{1,0:T(8,128)(2,1)S(1)}, bf16[192,256]{1,0:T(8,128)(2,1)S(1)}, u32[]{:S(2)}, u32[]{:S(2)}) collective-permute-start(bf16[192,256]{1,0:T(8,128)(2,1)S(1)} %maximum_maximum_fusion), channel_id=1, source_target_pairs={{0,3},{1,0},{2,1},{3,2},{4,7},{5,4},{6,5},{7,6},{8,11},{9,8},{10,9... | collective-permute-start | bytes 294920 | tf_op jit(solution)/shard_map/ppermute | solution.py:216
  80.6 0.0 collective-permute-done.7
  80.6 3.4 %collective-permute-done.8 = bf16[192,256]{1,0:T(8,128)(2,1)S(1)} collective-permute-done((bf16[192,256]{1,0:T(8,128)(2,1)S(1)}, bf16[192,256]{1,0:T(8,128)(2,1)S(1)}, u32[]{:S(2)}, u32[]{:S(2)}) %collective-permute-start.8) | collective-permute-done | bytes 98336 | tf_op jit(solution)/shard_map/ppermute | solution.py:216
  84.0 3.4 %collective-permute-done.9 = bf16[192,256]{1,0:T(8,128)(2,1)S(1)} collective-permute-done((bf16[192,256]{1,0:T(8,128)(2,1)S(1)}, bf16[192,256]{1,0:T(8,128)(2,1)S(1)}, u32[]{:S(2)}, u32[]{:S(2)}) %collective-permute-start.9) | collective-permute-done | bytes 98336 | tf_op jit(solution)/shard_map/ppermute | solution.py:216
  87.5 0.1 pad_maximum_fusion.a
  87.5 2.2 %collective-permute-start.10 = (bf16[4,192,256]{2,1,0:T(8,128)(2,1)S(1)}, bf16[4,192,256]{2,1,0:T(8,128)(2,1)S(1)}, u32[]{:S(2)}, u32[]{:S(2)}) collective-permute-start(bf16[4,192,256]{2,1,0:T(8,128)(2,1)S(1)} %pad_maximum_fusion.a), channel_id=1, source_target_pairs={{0,4},{4,8},{8,12},{12,0},{1,5},{5,9},{9,13},{13,1},{2,6},{6,10},{... | collective-permute-start | bytes 1179656 | tf_op jit(solution)/shard_map/ppermute | solution.py:216
  89.7 3.7 %collective-permute-start.11 = (bf16[4,192,256]{2,1,0:T(8,128)(2,1)S(1)}, bf16[4,192,256]{2,1,0:T(8,128)(2,1)S(1)}, u32[]{:S(2)}, u32[]{:S(2)}) collective-permute-start(bf16[4,192,256]{2,1,0:T(8,128)(2,1)S(1)} %pad_maximum_fusion.a), channel_id=1, source_target_pairs={{0,8},{4,12},{8,0},{12,4},{1,9},{5,13},{9,1},{13,5},{2,10},{6,14},... | collective-permute-start | bytes 1179656 | tf_op jit(solution)/shard_map/ppermute | solution.py:216
  93.4 2.5 %collective-permute-start.12 = (bf16[4,192,256]{2,1,0:T(8,128)(2,1)S(1)}, bf16[4,192,256]{2,1,0:T(8,128)(2,1)S(1)}, u32[]{:S(2)}, u32[]{:S(2)}) collective-permute-start(bf16[4,192,256]{2,1,0:T(8,128)(2,1)S(1)} %pad_maximum_fusion.a), channel_id=1, source_target_pairs={{0,12},{4,0},{8,4},{12,8},{1,13},{5,1},{9,5},{13,9},{2,14},{6,2},{... | collective-permute-start | bytes 1179656 | tf_op jit(solution)/shard_map/ppermute | solution.py:216
  96.0 3.7 %collective-permute-start.6 = (bf16[512,128]{1,0:T(8,128)(2,1)S(1)}, bf16[512,128]{1,0:T(8,128)(2,1)S(1)}, u32[]{:S(2)}, u32[]{:S(2)}) collective-permute-start(bf16[512,128]{1,0:T(8,128)(2,1)S(1)} %pad_maximum_fusion.2.mine), channel_id=1, source_target_pairs={{0,16},{16,0},{1,17},{17,1},{2,18},{18,2},{3,19},{19,3},{4,20},{20... | collective-permute-start | bytes 393224 | tf_op jit(solution)/shard_map/ppermute | solution.py:221
  99.7 0.1 compare_convert_fusion.e
  99.8 0.9 collective-permute-done.6.other
  100.7 0.0 collective-permute-done.5.fo
  100.7 2.2 %shard_map.114 = (bf16[16,64,256]{2,1,0:T(8,128)(2,1)S(1)}, bf16[64,256]{1,0:T(8,128)(2,1)S(1)}, bf16[2,16,256]{2,1,0:T(8,128)(2,1)S(1)}) custom-call(s32[36]{0:T(128)S(1)} %concatenate.33.pos, bf16[16,64,256]{2,1,0:T(8,128)(2,1)S(1)} %all-to-all-done.xg, bf16[16,144,256]{2,1,0:T(8,128)(2,1)S(1)} %bitcast.32, ...), custom_call_target="tpu_custom_call" | custom-call | tf_op jit(solution)/shard_map/pallas_call | solution.py:42
  102.9 5.0 %collective-permute-done.11.c = bf16[4,192,256]{2,1,0:T(8,128)(2,1)S(1)} collective-permute-done((bf16[4,192,256]{2,1,0:T(8,128)(2,1)S(1)}, bf16[4,192,256]{2,1,0:T(8,128)(2,1)S(1)}, u32[]{:S(2)}, u32[]{:S(2)}) %collective-permute-start.11) | collective-permute-done | bytes 393248 | tf_op jit(solution)/shard_map/ppermute | solution.py:216
  107.9 3.6 %collective-permute-done.12.d = bf16[4,192,256]{2,1,0:T(8,128)(2,1)S(1)} collective-permute-done((bf16[4,192,256]{2,1,0:T(8,128)(2,1)S(1)}, bf16[4,192,256]{2,1,0:T(8,128)(2,1)S(1)}, u32[]{:S(2)}, u32[]{:S(2)}) %collective-permute-start.12) | collective-permute-done | bytes 393248 | tf_op jit(solution)/shard_map/ppermute | solution.py:216
  111.6 0.6 shard_map.115.mm.um
  112.2 3.5 %collective-permute-start.13 = (bf16[16,192,256]{2,1,0:T(8,128)(2,1)S(1)}, bf16[16,192,256]{2,1,0:T(8,128)(2,1)S(1)}, u32[]{:S(2)}, u32[]{:S(2)}) collective-permute-start(bf16[16,192,256]{2,1,0:T(8,128)(2,1)S(1)} %shard_map.115.mm.um), channel_id=1, source_target_pairs={{0,16},{16,0},{1,17},{17,1},{2,18},{18,2},{3,19},{19,3},{4,20},{20... | collective-permute-start | bytes 4718600 | tf_op jit(solution)/shard_map/ppermute | solution.py:221
  115.7 19.4 %all_to_all.25.g = bf16[16,64,256]{2,1,0:T(8,128)(2,1)S(1)} all-to-all(bf16[16,64,256]{2,1,0:T(8,128)(2,1)S(1)} %get-tuple-element.18), channel_id=1, replica_groups=mesh['yl'=2,'z'=8,'c'=2,'x'=4,'yh'=4] {'yl','z'}, dimensions={0} | all-to-all | bytes 1048576 | tf_op jit(solution)/shard_map/all_to_all | solution.py:229
  135.0 0.0 collective-permute-done.13.mo.uo
  135.1 1.4 shard_map.116
  136.5 19.5 %all_to_all.26.g = bf16[16,64,256]{2,1,0:T(8,128)(2,1)S(1)} all-to-all(bf16[16,64,256]{2,1,0:T(8,128)(2,1)S(1)} %shard_map.116), channel_id=1, replica_groups=mesh['yl'=2,'z'=8,'c'=2,'x'=4,'yh'=4] {'yl','z'}, dimensions={0} | all-to-all | bytes 1048576 | tf_op jit(solution)/shard_map/all_to_all | solution.py:229
  156.0 1.6 shard_map.117
  157.6 0.8 copy-done.6
  158.4 8.6 %all-to-all-start.4 = ((bf16[16,64,256]{2,1,0:T(8,128)(2,1)}), bf16[16,64,256]{2,1,0:T(8,128)(2,1)}, u32[]{:S(2)}, u32[]{:S(2)}) async-start(bf16[16,64,256]{2,1,0:T(8,128)(2,1)} %copy-done.6), calls=%async_computation.4 | async-start | bytes 1048576 | tf_op jit(solution)/shard_map/all_to_all | solution.py:229
  167.1 2.8 %collective-permute-start.14 = (f32[64,128]{1,0:T(8,128)S(1)}, f32[64,128]{1,0:T(8,128)S(1)}, u32[]{:S(2)}, u32[]{:S(2)}) collective-permute-start(f32[64,128]{1,0:T(8,128)S(1)} %slice_select_fusion), channel_id=1, source_target_pairs={{0,16},{16,0},{1,17},{17,1},{2,18},{18,2},{3,19},{19,3},{4,20},{20... | collective-permute-start | bytes 98312 | tf_op jit(solution)/shard_map/ppermute | solution.py:221
  169.9 1.3 copy-done.1
  171.1 1.0 copy-done.3
  172.2 1.3 copy-done.5
  173.4 1.0 shard_map.118.part
  174.4 0.0 collective-permute-done.14
  174.5 4.8 %all-to-all-done.4.g = bf16[16,64,256]{2,1,0:T(8,128)(2,1)} async-done(((bf16[16,64,256]{2,1,0:T(8,128)(2,1)}), bf16[16,64,256]{2,1,0:T(8,128)(2,1)}, u32[]{:S(2)}, u32[]{:S(2)}) %all-to-all-start.4) | async-done | bytes 524320 | tf_op jit(solution)/shard_map/all_to_all | solution.py:229
  179.3 1.5 shard_map.119
  180.7 5.6 %collective-permute-start.15 = (f32[2,64,64]{2,1,0:T(8,128)S(1)}, f32[2,64,64]{2,1,0:T(8,128)S(1)}, u32[]{:S(2)}, u32[]{:S(2)}) collective-permute-start(f32[2,64,64]{2,1,0:T(8,128)S(1)} %get-tuple-element.29), channel_id=1, source_target_pairs={{0,16},{16,0},{1,17},{17,1},{2,18},{18,2},{3,19},{19,3},{4,20},{20... | collective-permute-start | bytes 98312 | tf_op jit(solution)/shard_map/ppermute | solution.py:221
  186.4 0.7 copy.12
  187.1 0.1 collective-permute-done.15
  187.2 0.7 pad_maximum_fusion.5
  (44 shorter events, 0.3 us)
Async XLA Ops:
  2.3 23.5 %collective-permute-start = (bf16[384,128]{1,0:T(8,128)(2,1)S(1)}, bf16[384,128]{1,0:T(8,128)(2,1)S(1)}, u32[]{:S(2)}, u32[]{:S(2)}) collective-permute-start(bf16[384,128]{1,0:T(8,128)(2,1)S(1)} %pad_maximum_fusion.3), channel_id=1, source_target_pairs={{0,0},{16,32},{32,64},{48,96},{64,128},{80,160},{96,192},{112,224}... | collective-permute-start | bytes 294920 | tf_op jit(solution)/shard_map/ppermute | solution.py:262
  8.5 6.4 %collective-permute-start.4 = (bf16[128,128]{1,0:T(8,128)(2,1)S(1)}, bf16[128,128]{1,0:T(8,128)(2,1)S(1)}, u32[]{:S(2)}, u32[]{:S(2)}) collective-permute-start(bf16[128,128]{1,0:T(8,128)(2,1)S(1)} %bitcast.34), channel_id=1, source_target_pairs={{0,16},{16,0},{1,17},{17,1},{2,18},{18,2},{3,19},{19,3},{4,20},{20... | collective-permute-start | bytes 98312 | tf_op jit(solution)/shard_map/ppermute | solution.py:221
  16.4 26.1 %all-to-all-start = ((bf16[16,64,256]{2,1,0:T(8,128)(2,1)}), bf16[16,64,256]{2,1,0:T(8,128)(2,1)S(1)}, u32[]{:S(2)}, u32[]{:S(2)}) async-start(bf16[16,64,256]{2,1,0:T(8,128)(2,1)} %shard_map.113), calls=%async_computation | async-start | bytes 1048576 | tf_op jit(solution)/shard_map/all_to_all | solution.py:229
  25.7 14.3 %collective-permute-start.2 = (bf16[144,256]{1,0:T(8,128)(2,1)S(1)}, bf16[144,256]{1,0:T(8,128)(2,1)S(1)}, u32[]{:S(2)}, u32[]{:S(2)}) collective-permute-start(bf16[144,256]{1,0:T(8,128)(2,1)S(1)} %pad_maximum_fusion.4), channel_id=1, source_target_pairs={{0,2},{1,3},{2,0},{3,1},{4,6},{5,7},{6,4},{7,5},{8,10},{9,11},{10,... | collective-permute-start | bytes 221192 | tf_op jit(solution)/shard_map/ppermute | solution.py:216
  33.2 6.8 %collective-permute-start.3 = (bf16[144,256]{1,0:T(8,128)(2,1)S(1)}, bf16[144,256]{1,0:T(8,128)(2,1)S(1)}, u32[]{:S(2)}, u32[]{:S(2)}) collective-permute-start(bf16[144,256]{1,0:T(8,128)(2,1)S(1)} %pad_maximum_fusion.4), channel_id=1, source_target_pairs={{0,3},{1,0},{2,1},{3,2},{4,7},{5,4},{6,5},{7,6},{8,11},{9,8},{10,9... | collective-permute-start | bytes 221192 | tf_op jit(solution)/shard_map/ppermute | solution.py:216
  35.2 7.3 %collective-permute-start.1 = (bf16[144,256]{1,0:T(8,128)(2,1)S(1)}, bf16[144,256]{1,0:T(8,128)(2,1)S(1)}, u32[]{:S(2)}, u32[]{:S(2)}) collective-permute-start(bf16[144,256]{1,0:T(8,128)(2,1)S(1)} %pad_maximum_fusion.4), channel_id=1, source_target_pairs={{0,1},{1,2},{2,3},{3,0},{4,5},{5,6},{6,7},{7,4},{8,9},{9,10},{10,1... | collective-permute-start | bytes 221192 | tf_op jit(solution)/shard_map/ppermute | solution.py:216
  43.6 4.2 %copy-start.9 = (s32[4096]{0:T(1024)S(1)}, s32[4096]{0:T(1024)}, u32[]{:S(2)}) copy-start(s32[4096]{0:T(1024)} %param.19) | copy-start | bytes 49156
  43.6 23.5 %copy-start.8 = (bf16[2,64,128]{2,1,0:T(8,128)(2,1)S(1)}, bf16[2,64,128]{2,1,0:T(8,128)(2,1)}, u32[]{:S(2)}) copy-start(bf16[2,64,128]{2,1,0:T(8,128)(2,1)} %param.18) | copy-start | bytes 98308
  43.6 23.6 %copy-start.7 = (f32[128,128]{1,0:T(8,128)S(1)}, f32[128,128]{1,0:T(8,128)}, u32[]{:S(2)}) copy-start(f32[128,128]{1,0:T(8,128)} %param.12) | copy-start | bytes 196612
  43.6 17.7 %all-to-all-start.1 = ((bf16[4,4,144,256]{3,2,1,0:T(8,128)(2,1)}), bf16[4,4,144,256]{3,2,1,0:T(8,128)(2,1)S(1)}, u32[]{:S(2)}, u32[]{:S(2)}) async-start(bf16[4,4,144,256]{3,2,1,0:T(8,128)(2,1)} %broadcast_in_dim.33), calls=%async_computation.1 | async-start | bytes 2359296 | tf_op jit(solution)/shard_map/all_to_all | solution.py:210
  61.3 41.6 %copy-start = (bf16[4,4,144,256]{3,2,1,0:T(8,128)(2,1)}, bf16[4,4,144,256]{3,2,1,0:T(8,128)(2,1)S(1)}, u32[]{:S(2)}) copy-start(bf16[4,4,144,256]{3,2,1,0:T(8,128)(2,1)S(1)} %all-to-all-done.1) | copy-start | bytes 3538948
  61.3 39.3 %collective-permute-start.5 = (bf16[16,144,256]{2,1,0:T(8,128)(2,1)S(1)}, bf16[16,144,256]{2,1,0:T(8,128)(2,1)S(1)}, u32[]{:S(2)}, u32[]{:S(2)}) collective-permute-start(bf16[16,144,256]{2,1,0:T(8,128)(2,1)S(1)} %bitcast.31), channel_id=1, source_target_pairs={{0,16},{16,0},{1,17},{17,1},{2,18},{18,2},{3,19},{19,3},{4,20},{20... | collective-permute-start | bytes 3538952 | tf_op jit(solution)/shard_map/ppermute | solution.py:221
  67.2 13.3 %collective-permute-start.7 = (bf16[192,256]{1,0:T(8,128)(2,1)S(1)}, bf16[192,256]{1,0:T(8,128)(2,1)S(1)}, u32[]{:S(2)}, u32[]{:S(2)}) collective-permute-start(bf16[192,256]{1,0:T(8,128)(2,1)S(1)} %maximum_maximum_fusion), channel_id=1, source_target_pairs={{0,1},{1,2},{2,3},{3,0},{4,5},{5,6},{6,7},{7,4},{8,9},{9,10},{10,1... | collective-permute-start | bytes 294920 | tf_op jit(solution)/shard_map/ppermute | solution.py:216
  70.5 13.6 %collective-permute-start.8 = (bf16[192,256]{1,0:T(8,128)(2,1)S(1)}, bf16[192,256]{1,0:T(8,128)(2,1)S(1)}, u32[]{:S(2)}, u32[]{:S(2)}) collective-permute-start(bf16[192,256]{1,0:T(8,128)(2,1)S(1)} %maximum_maximum_fusion), channel_id=1, source_target_pairs={{0,2},{1,3},{2,0},{3,1},{4,6},{5,7},{6,4},{7,5},{8,10},{9,11},{10,... | collective-permute-start | bytes 294920 | tf_op jit(solution)/shard_map/ppermute | solution.py:216
  75.2 12.2 %collective-permute-start.9 = (bf16[192,256]{1,0:T(8,128)(2,1)S(1)}, bf16[192,256]{1,0:T(8,128)(2,1)S(1)}, u32[]{:S(2)}, u32[]{:S(2)}) collective-permute-start(bf16[192,256]{1,0:T(8,128)(2,1)S(1)} %maximum_maximum_fusion), channel_id=1, source_target_pairs={{0,3},{1,0},{2,1},{3,2},{4,7},{5,4},{6,5},{7,6},{8,11},{9,8},{10,9... | collective-permute-start | bytes 294920 | tf_op jit(solution)/shard_map/ppermute | solution.py:216
  87.5 15.4 %collective-permute-start.10 = (bf16[4,192,256]{2,1,0:T(8,128)(2,1)S(1)}, bf16[4,192,256]{2,1,0:T(8,128)(2,1)S(1)}, u32[]{:S(2)}, u32[]{:S(2)}) collective-permute-start(bf16[4,192,256]{2,1,0:T(8,128)(2,1)S(1)} %pad_maximum_fusion.a), channel_id=1, source_target_pairs={{0,4},{4,8},{8,12},{12,0},{1,5},{5,9},{9,13},{13,1},{2,6},{6,10},{... | collective-permute-start | bytes 1179656 | tf_op jit(solution)/shard_map/ppermute | solution.py:216
  89.7 18.2 %collective-permute-start.11 = (bf16[4,192,256]{2,1,0:T(8,128)(2,1)S(1)}, bf16[4,192,256]{2,1,0:T(8,128)(2,1)S(1)}, u32[]{:S(2)}, u32[]{:S(2)}) collective-permute-start(bf16[4,192,256]{2,1,0:T(8,128)(2,1)S(1)} %pad_maximum_fusion.a), channel_id=1, source_target_pairs={{0,8},{4,12},{8,0},{12,4},{1,9},{5,13},{9,1},{13,5},{2,10},{6,14},... | collective-permute-start | bytes 1179656 | tf_op jit(solution)/shard_map/ppermute | solution.py:216
  93.4 18.1 %collective-permute-start.12 = (bf16[4,192,256]{2,1,0:T(8,128)(2,1)S(1)}, bf16[4,192,256]{2,1,0:T(8,128)(2,1)S(1)}, u32[]{:S(2)}, u32[]{:S(2)}) collective-permute-start(bf16[4,192,256]{2,1,0:T(8,128)(2,1)S(1)} %pad_maximum_fusion.a), channel_id=1, source_target_pairs={{0,12},{4,0},{8,4},{12,8},{1,13},{5,1},{9,5},{13,9},{2,14},{6,2},{... | collective-permute-start | bytes 1179656 | tf_op jit(solution)/shard_map/ppermute | solution.py:216
  96.0 4.7 %collective-permute-start.6 = (bf16[512,128]{1,0:T(8,128)(2,1)S(1)}, bf16[512,128]{1,0:T(8,128)(2,1)S(1)}, u32[]{:S(2)}, u32[]{:S(2)}) collective-permute-start(bf16[512,128]{1,0:T(8,128)(2,1)S(1)} %pad_maximum_fusion.2.mine), channel_id=1, source_target_pairs={{0,16},{16,0},{1,17},{17,1},{2,18},{18,2},{3,19},{19,3},{4,20},{20... | collective-permute-start | bytes 393224 | tf_op jit(solution)/shard_map/ppermute | solution.py:221
  100.7 2.3 %copy-start.4 = (bf16[16,144,256]{2,1,0:T(8,128)(2,1)}, bf16[16,144,256]{2,1,0:T(8,128)(2,1)S(1)}, u32[]{:S(2)}) copy-start(bf16[16,144,256]{2,1,0:T(8,128)(2,1)S(1)} %collective-permute-done.5.fo) | copy-start | bytes 3538948
  112.2 22.8 %collective-permute-start.13 = (bf16[16,192,256]{2,1,0:T(8,128)(2,1)S(1)}, bf16[16,192,256]{2,1,0:T(8,128)(2,1)S(1)}, u32[]{:S(2)}, u32[]{:S(2)}) collective-permute-start(bf16[16,192,256]{2,1,0:T(8,128)(2,1)S(1)} %shard_map.115.mm.um), channel_id=1, source_target_pairs={{0,16},{16,0},{1,17},{17,1},{2,18},{18,2},{3,19},{19,3},{4,20},{20... | collective-permute-start | bytes 4718600 | tf_op jit(solution)/shard_map/ppermute | solution.py:221
  135.0 1.4 copy-start.2
  157.6 0.8 copy-start.6
  158.4 20.8 %all-to-all-start.4 = ((bf16[16,64,256]{2,1,0:T(8,128)(2,1)}), bf16[16,64,256]{2,1,0:T(8,128)(2,1)}, u32[]{:S(2)}, u32[]{:S(2)}) async-start(bf16[16,64,256]{2,1,0:T(8,128)(2,1)} %copy-done.6), calls=%async_computation.4 | async-start | bytes 1048576 | tf_op jit(solution)/shard_map/all_to_all | solution.py:229
  167.1 7.4 %collective-permute-start.14 = (f32[64,128]{1,0:T(8,128)S(1)}, f32[64,128]{1,0:T(8,128)S(1)}, u32[]{:S(2)}, u32[]{:S(2)}) collective-permute-start(f32[64,128]{1,0:T(8,128)S(1)} %slice_select_fusion), channel_id=1, source_target_pairs={{0,16},{16,0},{1,17},{17,1},{2,18},{18,2},{3,19},{19,3},{4,20},{20... | collective-permute-start | bytes 98312 | tf_op jit(solution)/shard_map/ppermute | solution.py:221
  169.9 1.3 copy-start.1
  171.1 1.0 copy-start.3
  172.2 1.3 copy-start.5
  180.7 6.5 %collective-permute-start.15 = (f32[2,64,64]{2,1,0:T(8,128)S(1)}, f32[2,64,64]{2,1,0:T(8,128)S(1)}, u32[]{:S(2)}, u32[]{:S(2)}) collective-permute-start(f32[2,64,64]{2,1,0:T(8,128)S(1)} %get-tuple-element.29), channel_id=1, source_target_pairs={{0,16},{16,0},{1,17},{17,1},{2,18},{18,2},{3,19},{19,3},{4,20},{20... | collective-permute-start | bytes 98312 | tf_op jit(solution)/shard_map/ppermute | solution.py:221

commit v4 on v3

--- a/solution.py
+++ b/solution.py
@@ -37,8 +37,15 @@
     return pltpu.with_memory_space_constraint(x, pltpu.VMEM)
 
 
+def from_hbm(kernel, outs, pos, *args):
+    return plain(kernel, outs, pos, *[pltpu.with_memory_space_constraint(a, pltpu.HBM) for a in args])
+
+
 def call(kernel, outs, pos, *args):
-    args = [pos] + [near(a) if a.ndim > 2 else a for a in args]
+    return plain(kernel, outs, pos, *[near(a) if a.ndim > 2 else a for a in args])
+
+
+def plain(kernel, outs, *args):
     return pl.pallas_call(
         kernel,
         out_shape=outs,
@@ -76,6 +83,52 @@
 def own_columns(core, rows):
     turned = rows.T
     return jnp.where(core == 0, turned[:W], turned[W:])
+
+
+def write_terms(x, out, at):
+    high = x.astype(BF)
+    n = x.shape[0]
+    out[at : at + n] = high
+    out[at + n : at + 2 * n] = (x - high.astype(F32)).astype(BF)
+
+
+def ready(pos, pivot_rhs, update_rhs, parent_rhs, lower_update, x_out, moved_out, parent_out):
+    x_out[...] = jnp.concatenate([pivot_rhs[0], pivot_rhs[1]], axis=0).astype(BF)
+    moved_out[0:HALF] = lower_update[...]
+    write_terms(update_rhs[...], moved_out, HALF)
+    write_terms(parent_rhs[...], parent_out, 0)
+
+
+def packed(pos, lower_pivot, upper_pivot, parent_lower, parent_upper, upper_update, first_out, second_out):
+    chip, core, group = pos[0], pos[1], pos[36]
+    sides = []
+    for k in range(2):
+        at = lax.broadcasted_iota(jnp.int32, (64, HALF), 0) + core * 64
+        to = lax.broadcasted_iota(jnp.int32, (64, HALF), 1)
+        lower = lower_pivot[k].astype(F32)
+        low = jnp.logical_or(group < chip, jnp.logical_and(group == chip, to < at))
+        sides.append(jnp.where(low, lower, upper_pivot[k].astype(F32)))
+        on = jnp.logical_and(group == chip, to == at)
+        sides.append(jnp.sum(keep(lower, on), axis=0, keepdims=True))
+    first_out[0:64] = jnp.concatenate([sides[0], sides[2]], axis=1).astype(BF)
+    at = lax.broadcasted_iota(jnp.int32, (HALF, ROWS), 0) + core * HALF
+    to = lax.broadcasted_iota(jnp.int32, (HALF, ROWS), 1)
+    lower = parent_lower[...].astype(F32)
+    low = jnp.logical_or(group < chip, jnp.logical_and(group == chip, to < at))
+    second_out[0:HALF] = jnp.where(low, lower, parent_upper[...].astype(F32)).astype(BF)
+    on = jnp.logical_and(group == chip, to == at)
+    parent_diag = jnp.sum(keep(lower, on), axis=0, keepdims=True)
+    pivot_diag = jnp.concatenate([sides[1], sides[3]], axis=1)
+    row = lax.broadcasted_iota(jnp.int32, (16, ROWS), 0)
+    first_out[64:80] = jnp.where(row == 0, pivot_diag, jnp.where(row == 1, parent_diag, 0.0)).astype(BF)
+    second_out[HALF:] = jnp.concatenate([upper_update[0], upper_update[1]], axis=1)
+
+
+def columns_joined(pos, mine, got, out):
+    core = pos[1]
+    for k in range(2):
+        a, b = mine[k], got[k]
+        out[k] = jnp.where(core == 0, jnp.concatenate([a, b], axis=1), jnp.concatenate([b, a], axis=1))
 
 
 def first_block(pos, mine, other, send):
@@ -99,7 +152,7 @@
     return call(join, jax.ShapeDtypeStruct((4 * n, *rest), pieces[0].dtype), pos, *pieces)
 
 
-def forward_children(pos, xg, fm, fo, mine, other, e, send, piv_out, diag_out):
+def forward_children(pos, xg, fm, fo, mine, other, e, send, piv_out):
     chip, core, mid_at = pos[0], pos[1], pos[2]
     acc_m = jnp.zeros((W, HALF), F32)
     acc_o = jnp.zeros((W, HALF), F32)
@@ -127,7 +180,8 @@
     rows = row_ids(core, HALF)
     cols = lax.broadcasted_iota(jnp.int32, (HALF, HALF), 1)
     own = xg[chip]
-    diag = fm[mid_at, 128:144, :].astype(F32)[0:1] + fo[mid_at, 128:144, :].astype(F32)[0:1]
+    diags = fm[mid_at, 128:144, :].astype(F32) + fo[mid_at, 128:144, :].astype(F32)
+    diag = diags[0:1]
     outs = []
     for k in range(2):
         cut = slice(k * HALF, (k + 1) * HALF)
@@ -135,9 +189,8 @@
         total = ordered(piv[k] + nt(x, keep(pivot_rows(fm, fo, mid_at, k), cols < rows)), core)
         outs.append((total + x.astype(F32) * diag[:, cut]).astype(BF))
     pivot = jnp.concatenate(outs, axis=1)
-    piv_out[...] = pivot
-    diag_out[0] = fm[mid_at, 128:144, :]
-    diag_out[1] = fo[mid_at, 128:144, :]
+    piv_out[0:W] = pivot
+    piv_out[W:] = diags.astype(BF)
     for q in range(NP):
         send[q] = jnp.where(chip <= q, ps, pivot)
 
@@ -156,7 +209,7 @@
     block = jnp.concatenate([mm[mid_at, 0:HALF, :], mo[mid_at, 0:HALF, :]], axis=0)
     ps = g[chip]
     total = ordered(jnp.concatenate([acc_m, acc_o], axis=1) + nt(ps, keep(block, cols < rows)), core)
-    diag = diags[0].astype(F32)[1:2] + diags[1].astype(F32)[1:2]
+    diag = diags[W : W + 16].astype(F32)[1:2]
     mid = (total + ps.astype(F32) * diag).astype(BF)
     for q in range(NP):
         send[q] = mid
@@ -191,7 +244,7 @@
         for r in range(NP):
             src = pos[4 + r]
             acc += nt(pivot_rows(fm, fo, r, k), keep(g[src, :, cut], src > chip))
-        acc += nt(keep(pivot_rows(fm, fo, mid_at, k), cols >= rows), piv_ref[:, cut])
+        acc += nt(keep(pivot_rows(fm, fo, mid_at, k), cols >= rows), piv_ref[0:W, cut])
         out[k] = acc
 
 
@@ -232,11 +285,6 @@
 def halves(x, core, axis):
     a, b = jnp.split(x, 2, axis=axis)
     return jnp.where(core == 0, a, b), jnp.where(core == 0, b, a)
-
-
-def two_terms(x):
-    high = lax.reduce_precision(x, 8, 7)
-    return high.astype(BF), (x - high).astype(BF)
 
 
 def shards(pivot_rhs, update_rhs, parent_rhs, lower_pivot, lower_update, parent_lower, parent_upper, upper_pivot, upper_update, maps):
@@ -252,16 +300,16 @@
     sources_rx = (x_from[:, None] * 4 + y_from[None, :]).reshape(16)
     mid_ax = chip // 4 * 4 + y_at
     mid_rx = (gx - chip // 4) % 4 * 4 + y_at
-    pos = jnp.concatenate([jnp.stack([chip, core, mid_ax, mid_rx]), sources_ax, sources_rx]).astype(jnp.int32)
+    pos = jnp.concatenate([jnp.stack([chip, core, mid_ax, mid_rx]), sources_ax, sources_rx, group[None]]).astype(jnp.int32)
 
     to_parent = []
     for p in range(32):
         k, j = divmod(p, 16)
         to_parent.append((p, 2 * j + k))
-    uh, ul = two_terms(update_rhs)
-    moved = lax.ppermute(jnp.concatenate([lower_update, uh, ul], axis=0), PANEL, to_parent)
-
-    x_rows = pivot_rhs.astype(BF).reshape(128, 128)
+    shapes = [jax.ShapeDtypeStruct((n, 128), BF) for n in (128, 384, 256)]
+    x_rows, to_move, parent_terms = from_hbm(ready, shapes, pos, pivot_rhs, update_rhs, parent_rhs, lower_update)
+    moved = lax.ppermute(to_move, PANEL, to_parent)
+
     x_other = partner(x_rows)
     sent = jax.ShapeDtypeStruct((NP, W, ROWS), BF)
     send1 = call(first_block, sent, pos, x_rows, x_other)
@@ -270,45 +318,29 @@
     def sides(mine, other):
         return jnp.where(core == 0, mine, other), jnp.where(core == 0, other, mine)
 
-    full_l, on_block = group < chip, group == chip
-    r_at = lax.broadcasted_iota(jnp.int32, (1, 64, 128), 1) + core * 64
-    c_at = lax.broadcasted_iota(jnp.int32, (1, 64, 128), 2)
-    pick_low = jnp.logical_or(full_l, jnp.logical_and(on_block, c_at < r_at))
-    pivots = jnp.where(pick_low, lower_pivot, upper_pivot)
-    diag = jnp.sum(jnp.where(jnp.logical_and(on_block, c_at == r_at), lower_pivot, jnp.zeros_like(lower_pivot)), axis=1)
-    r_at = lax.broadcasted_iota(jnp.int32, (128, 256), 0) + core * 128
-    c_at = lax.broadcasted_iota(jnp.int32, (128, 256), 1)
-    pick_low = jnp.logical_or(full_l, jnp.logical_and(on_block, c_at < r_at))
-    parents = jnp.where(pick_low, parent_lower, parent_upper)
-    pdiag = jnp.sum(jnp.where(jnp.logical_and(on_block, c_at == r_at), parent_lower, jnp.zeros_like(parent_lower)), axis=0)
-    diags = jnp.pad(jnp.stack([jnp.concatenate([diag[0], diag[1]]), pdiag]), ((0, 14), (0, 0)))
-
-    def side_by_side(two):
-        return jnp.concatenate([two[0], two[1]], axis=1)
-
-    first_own = jnp.concatenate([side_by_side((moved[0:64], moved[64:128])), side_by_side(pivots), diags], axis=0)
-    second_own = jnp.concatenate([parents, side_by_side(upper_update)], axis=0)
+    shapes = [jax.ShapeDtypeStruct((n, 256), BF) for n in (80, 192)]
+    pivots, second_own = from_hbm(packed, shapes, pos, lower_pivot, upper_pivot, parent_lower, parent_upper, upper_update)
+    first_own = jnp.concatenate([jnp.concatenate([moved[0:64], moved[64:128]], axis=1), pivots], axis=0)
     first_y = shifts(first_own, "yh")
     first_y, xg = lax.optimization_barrier((jnp.stack(first_y), xg))
     first = to_all(first_y, "x", 4).reshape(16, 144, 256)
     first_other = partner(first)
-    second_y = jnp.stack(shifts(after(second_own, first_y), "yh"))
+    second_y = jnp.stack(shifts(second_own, "yh"))
     second_x = shifts(second_y, "x")
 
-    ph, plo = two_terms(parent_rhs)
-    others = jnp.concatenate([moved[128:], ph, plo], axis=0)
+    others = jnp.concatenate([moved[128:], parent_terms], axis=0)
     others_got = partner(others)
 
     own_maps = lax.dynamic_slice(maps.reshape(2, 2048), (0, chip * 128), (2, 128)).reshape(256, 1)
     spots = lax.broadcasted_iota(jnp.int32, (256, 256), 1) + chip * 256
     e = (own_maps == spots).astype(BF)
 
-    block = jax.ShapeDtypeStruct((W, ROWS), BF)
-    send2, piv, diags = call(forward_children, [sent, block, jax.ShapeDtypeStruct((2, 16, ROWS), BF)], pos, xg, first, first_other, others, others_got, e)
+    kept = pltpu.HBM((W + 16, ROWS), BF)
+    send2, piv = call(forward_children, [sent, kept], pos, xg, first, first_other, others, others_got, e)
     g2 = exchange(send2)
     second = joined(pos, after(second_x, piv))
     second_other = partner(second)
-    send3 = call(parent_forward, sent, pos, g2, second, second_other, diags)
+    send3 = call(parent_forward, sent, pos, g2, second, second_other, piv)
     g3 = exchange(send3)
     part = call(pivot_backward, jax.ShapeDtypeStruct((2, HALF, W), F32), pos, g2, piv, first, first_other)
     send4, sol_t = call(parent_backward, [sent, jax.ShapeDtypeStruct((W, ROWS), F32)], pos, g3, second, second_other, e)
@@ -320,7 +352,7 @@
     out_half = jax.ShapeDtypeStruct((2, 64, W), F32)
     mine, other = call(children_backward, [out_half, out_half], pos, g4, second, second_other, part)
     got = partner(other)
-    child_solution = jnp.concatenate(sides(mine, got), axis=2)
+    child_solution = plain(columns_joined, jax.ShapeDtypeStruct((2, 64, 128), F32), pos, mine, got)
     return (parent_solution, child_solution)
 
 

time: 190 us -> 197 us (1.037)
  blocking collectives: 38.9 us -> 67 us
  waiting for transfers between devices: 37.9 us -> 28.6 us
  starting transfers between devices: 88.1 us -> 80.2 us
  other arithmetic: 5.5 us -> 0.33 us
  Pallas kernels: 9.82 us -> 13.6 us
    all_to_all x0 -> x1, blocking collectives: none -> 14.3 us  [to_all(): lax.all_to_all(jnp.broadcast_to(block[None], (n, *block.shape)), axes, 0,...]
    all_to_all x2, blocking collectives: 38.9 us -> 52.8 us  [exchange(): return lax.all_to_all(send, CHIPS, 0, 0, tiled=True)]
    all_to_all x1 -> x0, waiting for transfers between devices: 13.5 us -> none  [to_all(): lax.all_to_all(jnp.broadcast_to(block[None], (n, *block.shape)), axes, 0,...]
    ppermute x1, waiting for transfers between devices: 0.01 us -> 8.25 us  [shards(): moved = lax.ppermute(to_move, PANEL, to_parent)]
    ppermute x9, waiting for transfers between devices: 18.5 us -> 13.7 us  [shifts(): moved.append(lax.ppermute(x, axis, [(i, (i + k) % 4) for i in range(4)]))]
    all_to_all x1 -> x0, starting transfers between devices: 4.14 us -> none  [to_all(): lax.all_to_all(jnp.broadcast_to(block[None], (n, *block.shape)), axes, 0,...]
    pallas_call x7 -> x10, Pallas kernels: 9.82 us -> 13.6 us  [plain(): pl.pallas_call(kernel, out_shape=outs, in_specs=[smem()] + [vmem()] * (le...]
    all_to_all x2, starting transfers between devices: 17.9 us -> 14.4 us  [exchange(): return lax.all_to_all(send, CHIPS, 0, 0, tiled=True)]
  transfers between devices with their start and end apart: 19 -> 18, of which waited for: 10 -> 10; matrix products, arithmetic and copies ran while one was open for 2% -> 1% of each run, Pallas kernels for 2% -> 2%
where the time goes in v4:
time: 197 us; the launch traced here: 196 us
  starting transfers between devices  80.2 us (41%)
  blocking collectives  67 us (34%)
  waiting for transfers between devices  28.6 us (15%)
  Pallas kernels  13.6 us (7%)
  local copies, waits for them, and re-layouts  5.47 us (3%)
    all_to_all x2, blocking collectives, exchange(): return lax.all_to_all(send, CHIPS, 0, 0, tiled=True)  52.8 us
    ppermute x9, starting transfers between devices, shifts(): moved.append(lax.ppermute(x, axis, [(i, (i + k) % 4) for i in range(4)]))  34.3 us
    ppermute x6, starting transfers between devices, partner(): return lax.ppermute(x, 'c', [(0, 1), (1, 0)])  27.4 us
    all_to_all x2, starting transfers between devices, exchange(): return lax.all_to_all(send, CHIPS, 0, 0, tiled=True)  14.4 us
    all_to_all x1, blocking collectives, to_all(): lax.all_to_all(jnp.broadcast_to(block[None], (n, *block.shape)), axes, 0,...  14.3 us
    ppermute x9, waiting for transfers between devices, shifts(): moved.append(lax.ppermute(x, axis, [(i, (i + k) % 4) for i in range(4)]))  13.7 us
    pallas_call x10, Pallas kernels, plain(): pl.pallas_call(kernel, out_shape=outs, in_specs=[smem()] + [vmem()] * (le...  13.6 us
    ppermute x1, waiting for transfers between devices, shards(): moved = lax.ppermute(to_move, PANEL, to_parent)  8.25 us
  transfers between devices with their start and end apart: 18, of which 10 were waited for; matrix products, arithmetic and copies ran while one was open for 1% of the time, Pallas kernels for 2%

profile of v4, /device:TPU:1, one launch (start us, length us, event | category | flops | bytes accessed | tf_op | source)
XLA Modules:
  0.0 196.3 jit_solution(961254942866606613)
XLA Ops:
  0.7 0.1 broadcast_add_fusion
  0.8 0.1 add.93
  0.9 0.1 add.97
  1.0 0.1 concatenate.15.pos
  1.1 0.9 shard_map.113
  2.0 8.7 %collective-permute-start.4 = (bf16[128,128]{1,0:T(8,128)(2,1)S(1)}, bf16[128,128]{1,0:T(8,128)(2,1)S(1)}, u32[]{:S(2)}, u32[]{:S(2)}) collective-permute-start(bf16[128,128]{1,0:T(8,128)(2,1)S(1)} %get-tuple-element.21.mine), channel_id=1, source_target_pairs={{0,16},{16,0},{1,17},{17,1},{2,18},{18,2},{3,19},{19,3},{4,20},{20... | collective-permute-start | bytes 98312 | tf_op jit(solution)/shard_map/ppermute | solution.py:274
  10.8 0.8 collective-permute-done.4.other
  11.6 1.5 shard_map.115
  13.1 5.8 %all-to-all-start = ((bf16[16,64,256]{2,1,0:T(8,128)(2,1)}), bf16[16,64,256]{2,1,0:T(8,128)(2,1)S(1)}, u32[]{:S(2)}, u32[]{:S(2)}) async-start(bf16[16,64,256]{2,1,0:T(8,128)(2,1)} %shard_map.115), calls=%async_computation | async-start | bytes 1048576 | tf_op jit(solution)/shard_map/all_to_all | solution.py:282
  18.9 4.1 %collective-permute-start = (bf16[384,128]{1,0:T(8,128)(2,1)S(1)}, bf16[384,128]{1,0:T(8,128)(2,1)S(1)}, u32[]{:S(2)}, u32[]{:S(2)}) collective-permute-start(bf16[384,128]{1,0:T(8,128)(2,1)S(1)} %get-tuple-element.19), channel_id=1, source_target_pairs={{0,0},{16,32},{32,64},{48,96},{64,128},{80,160},{96,192},{112,224}... | collective-permute-start | bytes 294920 | tf_op jit(solution)/shard_map/ppermute | solution.py:311
  23.0 1.0 shard_map.114
  24.0 8.3 %collective-permute-done = bf16[384,128]{1,0:T(8,128)(2,1)S(1)} collective-permute-done((bf16[384,128]{1,0:T(8,128)(2,1)S(1)}, bf16[384,128]{1,0:T(8,128)(2,1)S(1)}, u32[]{:S(2)}, u32[]{:S(2)}) %collective-permute-start) | collective-permute-done | bytes 98336 | tf_op jit(solution)/shard_map/ppermute | solution.py:311
  32.2 4.2 %collective-permute-start.1 = (bf16[144,256]{1,0:T(8,128)(2,1)S(1)}, bf16[144,256]{1,0:T(8,128)(2,1)S(1)}, u32[]{:S(2)}, u32[]{:S(2)}) collective-permute-start(bf16[144,256]{1,0:T(8,128)(2,1)S(1)} %get-tuple-element.43), channel_id=1, source_target_pairs={{0,1},{1,2},{2,3},{3,0},{4,5},{5,6},{6,7},{7,4},{8,9},{9,10},{10,1... | collective-permute-start | bytes 221192 | tf_op jit(solution)/shard_map/ppermute | solution.py:269
  36.5 4.8 %collective-permute-start.2 = (bf16[144,256]{1,0:T(8,128)(2,1)S(1)}, bf16[144,256]{1,0:T(8,128)(2,1)S(1)}, u32[]{:S(2)}, u32[]{:S(2)}) collective-permute-start(bf16[144,256]{1,0:T(8,128)(2,1)S(1)} %get-tuple-element.43), channel_id=1, source_target_pairs={{0,2},{1,3},{2,0},{3,1},{4,6},{5,7},{6,4},{7,5},{8,10},{9,11},{10,... | collective-permute-start | bytes 221192 | tf_op jit(solution)/shard_map/ppermute | solution.py:269
  41.2 5.0 %collective-permute-start.3 = (bf16[144,256]{1,0:T(8,128)(2,1)S(1)}, bf16[144,256]{1,0:T(8,128)(2,1)S(1)}, u32[]{:S(2)}, u32[]{:S(2)}) collective-permute-start(bf16[144,256]{1,0:T(8,128)(2,1)S(1)} %get-tuple-element.43), channel_id=1, source_target_pairs={{0,3},{1,0},{2,1},{3,2},{4,7},{5,4},{6,5},{7,6},{8,11},{9,8},{10,9... | collective-permute-start | bytes 221192 | tf_op jit(solution)/shard_map/ppermute | solution.py:269
  46.2 0.0 collective-permute-done.1
  46.2 0.0 collective-permute-done.2
  46.2 2.6 %collective-permute-done.3 = bf16[144,256]{1,0:T(8,128)(2,1)S(1)} collective-permute-done((bf16[144,256]{1,0:T(8,128)(2,1)S(1)}, bf16[144,256]{1,0:T(8,128)(2,1)S(1)}, u32[]{:S(2)}, u32[]{:S(2)}) %collective-permute-start.3) | collective-permute-done | bytes 73760 | tf_op jit(solution)/shard_map/ppermute | solution.py:269
  48.8 0.0 all-to-all-done.xg
  48.8 0.1 broadcast_in_dim.5
  48.9 0.0 copy-start.8
  48.9 14.3 %all_to_all.25 = bf16[4,4,144,256]{3,2,1,0:T(8,128)(2,1)S(1)} all-to-all(bf16[4,4,144,256]{3,2,1,0:T(8,128)(2,1)S(1)} %broadcast_in_dim.5), channel_id=1, replica_groups=mesh['yl'=2,'z'=8,'c'=2,'x'=4,'yh'=4] {'x'}, dimensions={0} | all-to-all | bytes 2359296 | tf_op jit(solution)/shard_map/all_to_all | solution.py:263
  63.2 1.9 collective-permute-start.5
  65.1 2.1 %collective-permute-start.7 = (bf16[192,256]{1,0:T(8,128)(2,1)S(1)}, bf16[192,256]{1,0:T(8,128)(2,1)S(1)}, u32[]{:S(2)}, u32[]{:S(2)}) collective-permute-start(bf16[192,256]{1,0:T(8,128)(2,1)S(1)} %get-tuple-element.26), channel_id=1, source_target_pairs={{0,1},{1,2},{2,3},{3,0},{4,5},{5,6},{6,7},{7,4},{8,9},{9,10},{10,1... | collective-permute-start | bytes 294920 | tf_op jit(solution)/shard_map/ppermute | solution.py:269
  67.2 7.9 %collective-permute-start.8 = (bf16[192,256]{1,0:T(8,128)(2,1)S(1)}, bf16[192,256]{1,0:T(8,128)(2,1)S(1)}, u32[]{:S(2)}, u32[]{:S(2)}) collective-permute-start(bf16[192,256]{1,0:T(8,128)(2,1)S(1)} %get-tuple-element.26), channel_id=1, source_target_pairs={{0,2},{1,3},{2,0},{3,1},{4,6},{5,7},{6,4},{7,5},{8,10},{9,11},{10,... | collective-permute-start | bytes 294920 | tf_op jit(solution)/shard_map/ppermute | solution.py:269
  75.1 1.9 collective-permute-start.9
  77.1 0.0 copy-done.8
  77.1 0.0 collective-permute-done.7
  77.1 0.8 collective-permute-done.8
  77.9 3.5 %collective-permute-done.9 = bf16[192,256]{1,0:T(8,128)(2,1)S(1)} collective-permute-done((bf16[192,256]{1,0:T(8,128)(2,1)S(1)}, bf16[192,256]{1,0:T(8,128)(2,1)S(1)}, u32[]{:S(2)}, u32[]{:S(2)}) %collective-permute-start.9) | collective-permute-done | bytes 98336 | tf_op jit(solution)/shard_map/ppermute | solution.py:269
  81.4 0.1 pad_maximum_fusion.a
  81.5 2.2 %collective-permute-start.10 = (bf16[4,192,256]{2,1,0:T(8,128)(2,1)S(1)}, bf16[4,192,256]{2,1,0:T(8,128)(2,1)S(1)}, u32[]{:S(2)}, u32[]{:S(2)}) collective-permute-start(bf16[4,192,256]{2,1,0:T(8,128)(2,1)S(1)} %pad_maximum_fusion.a), channel_id=1, source_target_pairs={{0,4},{4,8},{8,12},{12,0},{1,5},{5,9},{9,13},{13,1},{2,6},{6,10},{... | collective-permute-start | bytes 1179656 | tf_op jit(solution)/shard_map/ppermute | solution.py:269
  83.7 3.7 %collective-permute-start.11 = (bf16[4,192,256]{2,1,0:T(8,128)(2,1)S(1)}, bf16[4,192,256]{2,1,0:T(8,128)(2,1)S(1)}, u32[]{:S(2)}, u32[]{:S(2)}) collective-permute-start(bf16[4,192,256]{2,1,0:T(8,128)(2,1)S(1)} %pad_maximum_fusion.a), channel_id=1, source_target_pairs={{0,8},{4,12},{8,0},{12,4},{1,9},{5,13},{9,1},{13,5},{2,10},{6,14},... | collective-permute-start | bytes 1179656 | tf_op jit(solution)/shard_map/ppermute | solution.py:269
  87.4 2.5 %collective-permute-start.12 = (bf16[4,192,256]{2,1,0:T(8,128)(2,1)S(1)}, bf16[4,192,256]{2,1,0:T(8,128)(2,1)S(1)}, u32[]{:S(2)}, u32[]{:S(2)}) collective-permute-start(bf16[4,192,256]{2,1,0:T(8,128)(2,1)S(1)} %pad_maximum_fusion.a), channel_id=1, source_target_pairs={{0,12},{4,0},{8,4},{12,8},{1,13},{5,1},{9,5},{13,9},{2,14},{6,2},{... | collective-permute-start | bytes 1179656 | tf_op jit(solution)/shard_map/ppermute | solution.py:269
  89.9 4.9 %collective-permute-start.6 = (bf16[512,128]{1,0:T(8,128)(2,1)S(1)}, bf16[512,128]{1,0:T(8,128)(2,1)S(1)}, u32[]{:S(2)}, u32[]{:S(2)}) collective-permute-start(bf16[512,128]{1,0:T(8,128)(2,1)S(1)} %pad_maximum_fusion.2.mine), channel_id=1, source_target_pairs={{0,16},{16,0},{1,17},{17,1},{2,18},{18,2},{3,19},{19,3},{4,20},{20... | collective-permute-start | bytes 393224 | tf_op jit(solution)/shard_map/ppermute | solution.py:274
  94.8 0.1 compare_convert_fusion.e
  94.9 0.9 collective-permute-done.6.other
  95.8 0.0 collective-permute-done.5.fo
  95.8 2.8 %shard_map.116 = (bf16[16,64,256]{2,1,0:T(8,128)(2,1)S(1)}, bf16[80,256]{1,0:T(8,128)(2,1)}) custom-call(s32[37]{0:T(128)S(1)} %concatenate.15.pos, bf16[16,64,256]{2,1,0:T(8,128)(2,1)S(1)} %all-to-all-done.xg, bf16[16,144,256]{2,1,0:T(8,128)(2,1)S(1)} %bitcast.20, bf16[16,144,256]{2,1,0:T(8,128)(2,1)S(1)} %collective-permute-done.5.fo, ...), custom_call_target="tpu_custom_call" | custom-call | tf_op jit(solution)/shard_map/pallas_call | solution.py:49
  98.7 0.0 collective-permute-done.10.b
  98.7 2.2 %collective-permute-done.11.c = bf16[4,192,256]{2,1,0:T(8,128)(2,1)S(1)} collective-permute-done((bf16[4,192,256]{2,1,0:T(8,128)(2,1)S(1)}, bf16[4,192,256]{2,1,0:T(8,128)(2,1)S(1)}, u32[]{:S(2)}, u32[]{:S(2)}) %collective-permute-start.11) | collective-permute-done | bytes 393248 | tf_op jit(solution)/shard_map/ppermute | solution.py:269
  100.9 4.6 %collective-permute-done.12.d = bf16[4,192,256]{2,1,0:T(8,128)(2,1)S(1)} collective-permute-done((bf16[4,192,256]{2,1,0:T(8,128)(2,1)S(1)}, bf16[4,192,256]{2,1,0:T(8,128)(2,1)S(1)}, u32[]{:S(2)}, u32[]{:S(2)}) %collective-permute-start.12) | collective-permute-done | bytes 393248 | tf_op jit(solution)/shard_map/ppermute | solution.py:269
  105.5 0.6 shard_map.117.mm.um
  106.2 3.5 %collective-permute-start.13 = (bf16[16,192,256]{2,1,0:T(8,128)(2,1)S(1)}, bf16[16,192,256]{2,1,0:T(8,128)(2,1)S(1)}, u32[]{:S(2)}, u32[]{:S(2)}) collective-permute-start(bf16[16,192,256]{2,1,0:T(8,128)(2,1)S(1)} %shard_map.117.mm.um), channel_id=1, source_target_pairs={{0,16},{16,0},{1,17},{17,1},{2,18},{18,2},{3,19},{19,3},{4,20},{20... | collective-permute-start | bytes 4718600 | tf_op jit(solution)/shard_map/ppermute | solution.py:274
  109.6 33.2 %all_to_all.26.g = bf16[16,64,256]{2,1,0:T(8,128)(2,1)S(1)} all-to-all(bf16[16,64,256]{2,1,0:T(8,128)(2,1)S(1)} %get-tuple-element.25), channel_id=1, replica_groups=mesh['yl'=2,'z'=8,'c'=2,'x'=4,'yh'=4] {'yl','z'}, dimensions={0} | all-to-all | bytes 1048576 | tf_op jit(solution)/shard_map/all_to_all | solution.py:282
  142.9 0.0 collective-permute-done.13.mo.uo
  142.9 1.4 shard_map.118
  144.3 19.5 %all_to_all.27.g = bf16[16,64,256]{2,1,0:T(8,128)(2,1)S(1)} all-to-all(bf16[16,64,256]{2,1,0:T(8,128)(2,1)S(1)} %shard_map.118), channel_id=1, replica_groups=mesh['yl'=2,'z'=8,'c'=2,'x'=4,'yh'=4] {'yl','z'}, dimensions={0} | all-to-all | bytes 1048576 | tf_op jit(solution)/shard_map/all_to_all | solution.py:282
  163.8 1.6 shard_map.119
  165.4 0.0 copy-start.6
  165.5 0.8 copy-done.6
  166.2 8.6 %all-to-all-start.4 = ((bf16[16,64,256]{2,1,0:T(8,128)(2,1)}), bf16[16,64,256]{2,1,0:T(8,128)(2,1)}, u32[]{:S(2)}, u32[]{:S(2)}) async-start(bf16[16,64,256]{2,1,0:T(8,128)(2,1)} %copy-done.6), calls=%async_computation.4 | async-start | bytes 1048576 | tf_op jit(solution)/shard_map/all_to_all | solution.py:282
  174.9 2.8 %collective-permute-start.14 = (f32[64,128]{1,0:T(8,128)S(1)}, f32[64,128]{1,0:T(8,128)S(1)}, u32[]{:S(2)}, u32[]{:S(2)}) collective-permute-start(f32[64,128]{1,0:T(8,128)S(1)} %slice_select_fusion), channel_id=1, source_target_pairs={{0,16},{16,0},{1,17},{17,1},{2,18},{18,2},{3,19},{19,3},{4,20},{20... | collective-permute-start | bytes 98312 | tf_op jit(solution)/shard_map/ppermute | solution.py:274
  177.7 1.3 copy-done.1
  178.9 1.0 copy-done.3
  180.0 1.3 copy-done.5
  181.3 1.0 shard_map.120.part
  182.2 0.0 collective-permute-done.14
  182.3 4.8 %all-to-all-done.4.g = bf16[16,64,256]{2,1,0:T(8,128)(2,1)} async-done(((bf16[16,64,256]{2,1,0:T(8,128)(2,1)}), bf16[16,64,256]{2,1,0:T(8,128)(2,1)}, u32[]{:S(2)}, u32[]{:S(2)}) %all-to-all-start.4) | async-done | bytes 524320 | tf_op jit(solution)/shard_map/all_to_all | solution.py:282
  187.1 1.5 shard_map.121
  188.5 5.6 %collective-permute-start.15 = (f32[2,64,64]{2,1,0:T(8,128)S(1)}, f32[2,64,64]{2,1,0:T(8,128)S(1)}, u32[]{:S(2)}, u32[]{:S(2)}) collective-permute-start(f32[2,64,64]{2,1,0:T(8,128)S(1)} %get-tuple-element.35), channel_id=1, source_target_pairs={{0,16},{16,0},{1,17},{17,1},{2,18},{18,2},{3,19},{19,3},{4,20},{20... | collective-permute-start | bytes 98312 | tf_op jit(solution)/shard_map/ppermute | solution.py:274
  194.2 0.7 copy.12
  194.9 0.1 collective-permute-done.15.got
  195.1 1.3 shard_map.122
  (24 shorter events, 0.2 us)
Async XLA Ops:
  2.0 9.6 %collective-permute-start.4 = (bf16[128,128]{1,0:T(8,128)(2,1)S(1)}, bf16[128,128]{1,0:T(8,128)(2,1)S(1)}, u32[]{:S(2)}, u32[]{:S(2)}) collective-permute-start(bf16[128,128]{1,0:T(8,128)(2,1)S(1)} %get-tuple-element.21.mine), channel_id=1, source_target_pairs={{0,16},{16,0},{1,17},{17,1},{2,18},{18,2},{3,19},{19,3},{4,20},{20... | collective-permute-start | bytes 98312 | tf_op jit(solution)/shard_map/ppermute | solution.py:274
  13.1 35.7 %all-to-all-start = ((bf16[16,64,256]{2,1,0:T(8,128)(2,1)}), bf16[16,64,256]{2,1,0:T(8,128)(2,1)S(1)}, u32[]{:S(2)}, u32[]{:S(2)}) async-start(bf16[16,64,256]{2,1,0:T(8,128)(2,1)} %shard_map.115), calls=%async_computation | async-start | bytes 1048576 | tf_op jit(solution)/shard_map/all_to_all | solution.py:282
  18.9 13.3 %collective-permute-start = (bf16[384,128]{1,0:T(8,128)(2,1)S(1)}, bf16[384,128]{1,0:T(8,128)(2,1)S(1)}, u32[]{:S(2)}, u32[]{:S(2)}) collective-permute-start(bf16[384,128]{1,0:T(8,128)(2,1)S(1)} %get-tuple-element.19), channel_id=1, source_target_pairs={{0,0},{16,32},{32,64},{48,96},{64,128},{80,160},{96,192},{112,224}... | collective-permute-start | bytes 294920 | tf_op jit(solution)/shard_map/ppermute | solution.py:311
  32.2 14.0 %collective-permute-start.1 = (bf16[144,256]{1,0:T(8,128)(2,1)S(1)}, bf16[144,256]{1,0:T(8,128)(2,1)S(1)}, u32[]{:S(2)}, u32[]{:S(2)}) collective-permute-start(bf16[144,256]{1,0:T(8,128)(2,1)S(1)} %get-tuple-element.43), channel_id=1, source_target_pairs={{0,1},{1,2},{2,3},{3,0},{4,5},{5,6},{6,7},{7,4},{8,9},{9,10},{10,1... | collective-permute-start | bytes 221192 | tf_op jit(solution)/shard_map/ppermute | solution.py:269
  36.5 9.8 %collective-permute-start.2 = (bf16[144,256]{1,0:T(8,128)(2,1)S(1)}, bf16[144,256]{1,0:T(8,128)(2,1)S(1)}, u32[]{:S(2)}, u32[]{:S(2)}) collective-permute-start(bf16[144,256]{1,0:T(8,128)(2,1)S(1)} %get-tuple-element.43), channel_id=1, source_target_pairs={{0,2},{1,3},{2,0},{3,1},{4,6},{5,7},{6,4},{7,5},{8,10},{9,11},{10,... | collective-permute-start | bytes 221192 | tf_op jit(solution)/shard_map/ppermute | solution.py:269
  41.2 7.6 %collective-permute-start.3 = (bf16[144,256]{1,0:T(8,128)(2,1)S(1)}, bf16[144,256]{1,0:T(8,128)(2,1)S(1)}, u32[]{:S(2)}, u32[]{:S(2)}) collective-permute-start(bf16[144,256]{1,0:T(8,128)(2,1)S(1)} %get-tuple-element.43), channel_id=1, source_target_pairs={{0,3},{1,0},{2,1},{3,2},{4,7},{5,4},{6,5},{7,6},{8,11},{9,8},{10,9... | collective-permute-start | bytes 221192 | tf_op jit(solution)/shard_map/ppermute | solution.py:269
  48.9 28.1 %copy-start.8 = (s32[4096]{0:T(1024)S(1)}, s32[4096]{0:T(1024)}, u32[]{:S(2)}) copy-start(s32[4096]{0:T(1024)} %param.19) | copy-start | bytes 49156
  63.2 35.5 %copy-start = (bf16[4,4,144,256]{3,2,1,0:T(8,128)(2,1)}, bf16[4,4,144,256]{3,2,1,0:T(8,128)(2,1)S(1)}, u32[]{:S(2)}) copy-start(bf16[4,4,144,256]{3,2,1,0:T(8,128)(2,1)S(1)} %all_to_all.25) | copy-start | bytes 3538948
  63.2 32.6 %collective-permute-start.5 = (bf16[16,144,256]{2,1,0:T(8,128)(2,1)S(1)}, bf16[16,144,256]{2,1,0:T(8,128)(2,1)S(1)}, u32[]{:S(2)}, u32[]{:S(2)}) collective-permute-start(bf16[16,144,256]{2,1,0:T(8,128)(2,1)S(1)} %bitcast.19), channel_id=1, source_target_pairs={{0,16},{16,0},{1,17},{17,1},{2,18},{18,2},{3,19},{19,3},{4,20},{20... | collective-permute-start | bytes 3538952 | tf_op jit(solution)/shard_map/ppermute | solution.py:274
  65.1 12.0 %collective-permute-start.7 = (bf16[192,256]{1,0:T(8,128)(2,1)S(1)}, bf16[192,256]{1,0:T(8,128)(2,1)S(1)}, u32[]{:S(2)}, u32[]{:S(2)}) collective-permute-start(bf16[192,256]{1,0:T(8,128)(2,1)S(1)} %get-tuple-element.26), channel_id=1, source_target_pairs={{0,1},{1,2},{2,3},{3,0},{4,5},{5,6},{6,7},{7,4},{8,9},{9,10},{10,1... | collective-permute-start | bytes 294920 | tf_op jit(solution)/shard_map/ppermute | solution.py:269
  67.2 10.7 %collective-permute-start.8 = (bf16[192,256]{1,0:T(8,128)(2,1)S(1)}, bf16[192,256]{1,0:T(8,128)(2,1)S(1)}, u32[]{:S(2)}, u32[]{:S(2)}) collective-permute-start(bf16[192,256]{1,0:T(8,128)(2,1)S(1)} %get-tuple-element.26), channel_id=1, source_target_pairs={{0,2},{1,3},{2,0},{3,1},{4,6},{5,7},{6,4},{7,5},{8,10},{9,11},{10,... | collective-permute-start | bytes 294920 | tf_op jit(solution)/shard_map/ppermute | solution.py:269
  75.1 6.3 %collective-permute-start.9 = (bf16[192,256]{1,0:T(8,128)(2,1)S(1)}, bf16[192,256]{1,0:T(8,128)(2,1)S(1)}, u32[]{:S(2)}, u32[]{:S(2)}) collective-permute-start(bf16[192,256]{1,0:T(8,128)(2,1)S(1)} %get-tuple-element.26), channel_id=1, source_target_pairs={{0,3},{1,0},{2,1},{3,2},{4,7},{5,4},{6,5},{7,6},{8,11},{9,8},{10,9... | collective-permute-start | bytes 294920 | tf_op jit(solution)/shard_map/ppermute | solution.py:269
  81.5 17.2 %collective-permute-start.10 = (bf16[4,192,256]{2,1,0:T(8,128)(2,1)S(1)}, bf16[4,192,256]{2,1,0:T(8,128)(2,1)S(1)}, u32[]{:S(2)}, u32[]{:S(2)}) collective-permute-start(bf16[4,192,256]{2,1,0:T(8,128)(2,1)S(1)} %pad_maximum_fusion.a), channel_id=1, source_target_pairs={{0,4},{4,8},{8,12},{12,0},{1,5},{5,9},{9,13},{13,1},{2,6},{6,10},{... | collective-permute-start | bytes 1179656 | tf_op jit(solution)/shard_map/ppermute | solution.py:269
  83.7 17.2 %collective-permute-start.11 = (bf16[4,192,256]{2,1,0:T(8,128)(2,1)S(1)}, bf16[4,192,256]{2,1,0:T(8,128)(2,1)S(1)}, u32[]{:S(2)}, u32[]{:S(2)}) collective-permute-start(bf16[4,192,256]{2,1,0:T(8,128)(2,1)S(1)} %pad_maximum_fusion.a), channel_id=1, source_target_pairs={{0,8},{4,12},{8,0},{12,4},{1,9},{5,13},{9,1},{13,5},{2,10},{6,14},... | collective-permute-start | bytes 1179656 | tf_op jit(solution)/shard_map/ppermute | solution.py:269
  87.4 18.1 %collective-permute-start.12 = (bf16[4,192,256]{2,1,0:T(8,128)(2,1)S(1)}, bf16[4,192,256]{2,1,0:T(8,128)(2,1)S(1)}, u32[]{:S(2)}, u32[]{:S(2)}) collective-permute-start(bf16[4,192,256]{2,1,0:T(8,128)(2,1)S(1)} %pad_maximum_fusion.a), channel_id=1, source_target_pairs={{0,12},{4,0},{8,4},{12,8},{1,13},{5,1},{9,5},{13,9},{2,14},{6,2},{... | collective-permute-start | bytes 1179656 | tf_op jit(solution)/shard_map/ppermute | solution.py:269
  89.9 5.8 %collective-permute-start.6 = (bf16[512,128]{1,0:T(8,128)(2,1)S(1)}, bf16[512,128]{1,0:T(8,128)(2,1)S(1)}, u32[]{:S(2)}, u32[]{:S(2)}) collective-permute-start(bf16[512,128]{1,0:T(8,128)(2,1)S(1)} %pad_maximum_fusion.2.mine), channel_id=1, source_target_pairs={{0,16},{16,0},{1,17},{17,1},{2,18},{18,2},{3,19},{19,3},{4,20},{20... | collective-permute-start | bytes 393224 | tf_op jit(solution)/shard_map/ppermute | solution.py:274
  95.8 2.9 %copy-start.4 = (bf16[16,144,256]{2,1,0:T(8,128)(2,1)}, bf16[16,144,256]{2,1,0:T(8,128)(2,1)S(1)}, u32[]{:S(2)}) copy-start(bf16[16,144,256]{2,1,0:T(8,128)(2,1)S(1)} %collective-permute-done.5.fo) | copy-start | bytes 3538948
  105.5 37.4 %copy-start.7 = (bf16[80,256]{1,0:T(8,128)(2,1)S(1)}, bf16[80,256]{1,0:T(8,128)(2,1)}, u32[]{:S(2)}) copy-start(bf16[80,256]{1,0:T(8,128)(2,1)} %get-tuple-element.27.diags.piv_ref) | copy-start | bytes 122884
  106.2 36.7 %collective-permute-start.13 = (bf16[16,192,256]{2,1,0:T(8,128)(2,1)S(1)}, bf16[16,192,256]{2,1,0:T(8,128)(2,1)S(1)}, u32[]{:S(2)}, u32[]{:S(2)}) collective-permute-start(bf16[16,192,256]{2,1,0:T(8,128)(2,1)S(1)} %shard_map.117.mm.um), channel_id=1, source_target_pairs={{0,16},{16,0},{1,17},{17,1},{2,18},{18,2},{3,19},{19,3},{4,20},{20... | collective-permute-start | bytes 4718600 | tf_op jit(solution)/shard_map/ppermute | solution.py:274
  142.9 1.5 copy-start.2
  165.4 0.8 copy-start.6
  166.2 20.8 %all-to-all-start.4 = ((bf16[16,64,256]{2,1,0:T(8,128)(2,1)}), bf16[16,64,256]{2,1,0:T(8,128)(2,1)}, u32[]{:S(2)}, u32[]{:S(2)}) async-start(bf16[16,64,256]{2,1,0:T(8,128)(2,1)} %copy-done.6), calls=%async_computation.4 | async-start | bytes 1048576 | tf_op jit(solution)/shard_map/all_to_all | solution.py:282
  174.9 7.3 %collective-permute-start.14 = (f32[64,128]{1,0:T(8,128)S(1)}, f32[64,128]{1,0:T(8,128)S(1)}, u32[]{:S(2)}, u32[]{:S(2)}) collective-permute-start(f32[64,128]{1,0:T(8,128)S(1)} %slice_select_fusion), channel_id=1, source_target_pairs={{0,16},{16,0},{1,17},{17,1},{2,18},{18,2},{3,19},{19,3},{4,20},{20... | collective-permute-start | bytes 98312 | tf_op jit(solution)/shard_map/ppermute | solution.py:274
  177.7 1.3 copy-start.1
  178.9 1.0 copy-start.3
  180.0 1.3 copy-start.5
  188.5 6.5 %collective-permute-start.15 = (f32[2,64,64]{2,1,0:T(8,128)S(1)}, f32[2,64,64]{2,1,0:T(8,128)S(1)}, u32[]{:S(2)}, u32[]{:S(2)}) collective-permute-start(f32[2,64,64]{2,1,0:T(8,128)S(1)} %get-tuple-element.35), channel_id=1, source_target_pairs={{0,16},{16,0},{1,17},{17,1},{2,18},{18,2},{3,19},{19,3},{4,20},{20... | collective-permute-start | bytes 98312 | tf_op jit(solution)/shard_map/ppermute | solution.py:274
